TPU v7x, 128 devices: a whole 4x4x4 slice. The times are simulated.
128 devices in a mesh: seq: 64 (over y, x_hi, z, core), dp: 2 (over x_lo).
Axes of the slice: x: 4 (x_hi: 2, x_lo: 2; x = x_hi * 2 + x_lo), y: 4, z: 4, core: 2. Of those that a mesh axis runs over, the one named last changes fastest.
Arguments:
- acceptors: bfloat16 [2, 8192, 2560], P('dp', 'seq'), may hold values from -2 to 2
- lookups: bfloat16 [2, 8192, 2560], P('dp', 'seq'), may hold values from -0.3125 to 0.3125
- payloads: bfloat16 [2, 8192, 2560], P('dp', 'seq'), may hold values from -6 to 6
- lagged_fading_source: bfloat16 [2, 8192, 2560], P('dp', 'seq'), may hold values from -6 to 6
- response_cotangent: bfloat16 [2, 8192, 2560], P('dp', 'seq'), may hold values from -2.5 to 2.5
- fading_lowering_array: bfloat16 [2560, 128], replicated, may hold values from -0.125 to 0.125
- fading_raising_array: bfloat16 [2560, 128], replicated, may hold values from -1.25 to 1.25
- feature_fading_speed: float32 [2560], replicated, may hold values from 5.812872e-06 to 0.125
- present_reward: float32 [2560], replicated, may hold values from 2.828427 to 22.627417
Outputs:
- mixed: bfloat16 [2, 8192, 2560], P('dp', 'seq')
- grad_receptance: bfloat16 [2, 8192, 2560], P('dp', 'seq')
- lookup_deriv: bfloat16 [2, 8192, 2560], P('dp', 'seq')
- payload_deriv: bfloat16 [2, 8192, 2560], P('dp', 'seq')
- grad_decay_input: bfloat16 [2, 8192, 2560], P('dp', 'seq')
- grad_lora_a: float32 [2560, 128], P('dp')
- grad_lora_b: float32 [2560, 128], P('dp')
- grad_time_decay: float32 [2560], P('dp')
- present_reward_deriv: float32 [2560], P('dp')
All inputs are finite; a program needn't handle non-finite values.
Results may differ from a plain program's by a relative error of at most 0.006.
Values sent between devices are 32-bit elements.
No kernel may reach another device: no remote copies, remote signals or barrier semaphores. Data moves between devices by JAX's collectives and lax.ppermute only.
A program may use at most 320 MiB of HBM per device.

v0:
```python
import jax
import jax.numpy as jnp
from jax import lax
from jax.sharding import Mesh
from jax.sharding import PartitionSpec as P

ATTENDER_TOTAL = 40
LANE_TOTAL = 64
BLOCK = 64
SEQ = ("seq_0", "seq_1", "seq_2", "seq_3")
SEQ_DP = ("seq_0", "seq_1", "seq_2", "seq_3", "dp")


HIGH = lax.Precision.HIGHEST


def filled_with(x, identity):
    return jax.tree.map(
        lambda part, zero: jnp.zeros_like(part) + jnp.asarray(zero, part.dtype), x, identity
    )


def entering_2(x, axes, combine, identity, reverse):
    before = start = filled_with(x, identity)
    subtotal = x
    for axis in reversed(axes):
        devices, mine = (lax.axis_size(axis), lax.axis_index(axis))
        pieces = jax.tree.map(lambda part: lax.all_gather(part, axis), subtotal)
        inside, subtotal = (start, start)
        for k in reversed(range(devices)) if reverse else range(devices):
            passed = k > mine if reverse else k < mine
            subtotal = combine(subtotal, jax.tree.map(lambda part: part[k], pieces))
            inside = jax.tree.map(lambda new, old: jnp.where(passed, new, old), subtotal, inside)
        before = combine(inside, before)
    return before


def contract(pattern, left, right):
    return jnp.einsum(pattern, left, right, precision=HIGH, preferred_element_type=jnp.float32)


def decay_log_values(input_rows, fading_lowering_array, fading_raising_array, feature_fading_speed):
    apply_projection = jnp.dot(
        input_rows, fading_lowering_array, preferred_element_type=jnp.float32
    )
    smoothed_values = jnp.tanh(apply_projection)
    gate_portion = smoothed_values.astype(jnp.bfloat16)
    rank_projection = lax.dot_general(
        gate_portion,
        fading_raising_array,
        (((1,), (1,)), ((), ())),
        preferred_element_type=jnp.float32,
    )
    return (
        smoothed_values,
        gate_portion,
        -feature_fading_speed[None, :] * jnp.exp(rank_projection),
    )


def compose(decays, own_states, backward):

    def advance(carry, member):
        run_decay, run_state = carry
        decay, own_state = member
        return ((run_decay * decay, decay[..., None] * run_state + own_state), carry)

    initial = (
        jnp.ones(decays.shape[1:], jnp.float32),
        jnp.zeros(own_states.shape[1:], jnp.float32),
    )
    return lax.scan(advance, initial, (decays, own_states), reverse=backward)


def follow(earlier, later):
    return (earlier[0] * later[0], later[0][..., None] * earlier[1] + later[1])


def temporal_blend_sublevel(
    acceptor_lines,
    lookups,
    payloads,
    incoming_cotangent,
    fading_exponent,
    reward_by_attender,
    adjacent_shardlink,
):
    inclusive = jnp.cumsum(fading_exponent, axis=1)
    exclusive = inclusive - fading_exponent
    middle = inclusive[:, BLOCK // 2 - 1 : BLOCK // 2]
    overall = inclusive[:, -1]
    entering = jnp.exp(exclusive)
    leaving = jnp.exp(overall[:, None] - inclusive)
    upward = jnp.exp(exclusive - middle)
    downward = jnp.exp(middle - inclusive)
    decays = jnp.exp(overall)
    reached = acceptor_lines * entering
    faded_keys = lookups * leaving
    own_states = contract("nchk,nchv->nhkv", faded_keys, payloads)
    pull_states = contract("nchk,nchv->nhkv", reached, incoming_cotangent)
    starts, block_ends = adjacent_shardlink(decays, own_states, pull_states)
    position = jnp.arange(BLOCK)
    beneath = position[:, None] > position[None, :]
    early_recept = acceptor_lines * upward
    late_keys = lookups * downward
    scores = jnp.where(beneath, contract("nthk,nshk->nhts", early_recept, late_keys), 0.0)
    present_contribution = jnp.sum(acceptor_lines * reward_by_attender * lookups, axis=-1)[
        ..., None
    ]
    blended_response = (
        contract("nhts,nshv->nthv", scores, payloads)
        + present_contribution * payloads
        + contract("nthk,nhkv->nthv", reached, starts)
    )
    grad_start = decays[..., None] * block_ends + pull_states
    products = jnp.where(beneath, contract("nthv,nshv->nhts", incoming_cotangent, payloads), 0.0)
    agreement_verify = jnp.sum(payloads * incoming_cotangent, axis=-1)[..., None]
    memory_acceptors = entering * contract(
        "nhkv,nthv->nthk", starts, incoming_cotangent
    ) + upward * contract("nhts,nshk->nthk", products, late_keys)
    memory_lookup_lines = leaving * contract(
        "nhkv,nthv->nthk", block_ends, payloads
    ) + downward * contract("nhst,nshk->nthk", products, early_recept)
    payload_deriv = (
        contract("nthk,nhkv->nthv", faded_keys, block_ends)
        + contract("nhst,nshv->nthv", scores, incoming_cotangent)
        + present_contribution * incoming_cotangent
    )
    acceptor_deriv = memory_acceptors + reward_by_attender * lookups * agreement_verify
    lookup_deriv = memory_lookup_lines + reward_by_attender * acceptor_lines * agreement_verify
    present_reward_deriv = jnp.sum(acceptor_lines * lookups * agreement_verify, axis=(0, 1))
    coupling = jnp.sum(grad_start * starts, axis=-1)
    change = lookups * memory_lookup_lines - acceptor_lines * memory_acceptors
    fading_deriv = (
        coupling[:, None] + jnp.cumsum(change, axis=1) - change - acceptor_lines * memory_acceptors
    )
    return (
        blended_response,
        acceptor_deriv,
        lookup_deriv,
        payload_deriv,
        fading_deriv,
        present_reward_deriv,
    )


def sublevel_evaluation(
    reshaped_acceptors,
    reshaped_lookups,
    reshaped_payloads,
    reshaped_source,
    incoming_cotangent_reshaped,
    fading_lowering_array,
    fading_raising_array,
    feature_fading_speed,
    present_reward,
    adjacent_shardlink,
):
    smoothed_values, gate_portion, fading_exponent = decay_log_values(
        reshaped_source, fading_lowering_array, fading_raising_array, feature_fading_speed
    )
    tokens, feature_span = reshaped_acceptors.shape
    tiling_arrangement = (tokens // BLOCK, BLOCK, ATTENDER_TOTAL, LANE_TOTAL)
    collected_outcomes = temporal_blend_sublevel(
        reshaped_acceptors.astype(jnp.float32).reshape(tiling_arrangement),
        reshaped_lookups.astype(jnp.float32).reshape(tiling_arrangement),
        reshaped_payloads.astype(jnp.float32).reshape(tiling_arrangement),
        incoming_cotangent_reshaped.astype(jnp.float32).reshape(tiling_arrangement),
        fading_exponent.reshape(tiling_arrangement),
        present_reward.reshape(ATTENDER_TOTAL, LANE_TOTAL),
        adjacent_shardlink,
    )
    (
        blended_response,
        acceptor_deriv,
        lookup_deriv,
        payload_deriv,
        fading_deriv,
        present_reward_deriv,
    ) = collected_outcomes
    slope = fading_deriv.reshape(tokens, feature_span) * fading_exponent
    slope_portion = slope.astype(jnp.bfloat16)
    gate_gradient = jnp.dot(slope_portion, fading_raising_array, preferred_element_type=jnp.float32)
    projection_gradient = (gate_gradient * (1.0 - smoothed_values * smoothed_values)).astype(
        jnp.bfloat16
    )
    input_gradient = lax.dot_general(
        projection_gradient,
        fading_lowering_array,
        (((1,), (1,)), ((), ())),
        preferred_element_type=jnp.float32,
    ).astype(jnp.bfloat16)
    lowering_array_deriv = lax.dot_general(
        reshaped_source,
        projection_gradient,
        (((0,), (0,)), ((), ())),
        preferred_element_type=jnp.float32,
    )
    raising_array_deriv = lax.dot_general(
        slope_portion, gate_portion, (((0,), (0,)), ((), ())), preferred_element_type=jnp.float32
    )
    speed_deriv = jnp.sum(slope, axis=0)

    def flatten(member):
        return member.reshape(tokens, feature_span).astype(jnp.bfloat16)

    return (
        flatten(blended_response),
        flatten(acceptor_deriv),
        flatten(lookup_deriv),
        flatten(payload_deriv),
        input_gradient,
        (
            lowering_array_deriv,
            raising_array_deriv,
            speed_deriv,
            present_reward_deriv.reshape(feature_span),
        ),
    )


def shard_link(decays, own_states, pull_states):
    ahead_total, ahead = compose(decays, own_states, False)
    behind_total, behind = compose(decays, pull_states, True)
    identity = (jnp.ones_like(ahead_total[0]), jnp.zeros_like(ahead_total[1]))
    prior, state_in = entering_2(ahead_total, SEQ, follow, identity, False)
    latter, grad_after = entering_2(behind_total, SEQ, follow, identity, True)
    starts = ahead[0][..., None] * state_in[None] + ahead[1]
    block_ends = behind[0][..., None] * grad_after[None] + behind[1]
    return (starts, block_ends)


def per_device(
    acceptors,
    lookups,
    payloads,
    lagged_fading_source,
    response_cotangent,
    fading_lowering_array,
    fading_raising_array,
    feature_fading_speed,
    present_reward,
):
    collected_outcomes = sublevel_evaluation(
        acceptors[0],
        lookups[0],
        payloads[0],
        lagged_fading_source[0],
        response_cotangent[0],
        fading_lowering_array,
        fading_raising_array,
        feature_fading_speed,
        present_reward,
        shard_link,
    )
    sums = collected_outcomes[5]
    dp_count = lax.axis_size("dp")
    share_rows = fading_lowering_array.shape[0] // dp_count
    whole = lax.psum((sums[0], sums[1], sums[2], sums[3]), SEQ_DP)
    offset = lax.axis_index("dp") * share_rows
    reduced = tuple((lax.dynamic_slice_in_dim(member, offset, share_rows, 0) for member in whole))
    return (
        collected_outcomes[0][None],
        collected_outcomes[1][None],
        collected_outcomes[2][None],
        collected_outcomes[3][None],
        collected_outcomes[4][None],
        reduced[0],
        reduced[1],
        reduced[2],
        reduced[3],
    )


def solution(mesh):
    split = Mesh(
        mesh.devices.reshape(4, 2, 4, 2, mesh.shape["dp"]),
        ("seq_0", "seq_1", "seq_2", "seq_3", "dp"),
    )
    placed = (
        P("dp", SEQ, None),
        P("dp", SEQ, None),
        P("dp", SEQ, None),
        P("dp", SEQ, None),
        P("dp", SEQ, None),
        P(),
        P(),
        P(),
        P(),
    )
    return jax.shard_map(
        per_device,
        mesh=split,
        in_specs=placed,
        out_specs=(
            P("dp", SEQ, None),
            P("dp", SEQ, None),
            P("dp", SEQ, None),
            P("dp", SEQ, None),
            P("dp", SEQ, None),
            P("dp", None),
            P("dp", None),
            P("dp"),
            P("dp"),
        ),
        check_vma=False,
    )
```

profile of v0, /device:TPU:1, one launch (start us, length us, event | category | flops | bytes accessed | tf_op | source)
XLA Modules:
  0.0 685.3 jit_solution(13759978778250514535)
XLA Ops:
  28.3 7.0 %fusion.62 = f32[2,40,64,64]{2,3,1,0:T(8,128)} fusion(f32[2,64,40,64]{1,3,2,0:T(8,128)} %copy.91, bf16[2,64,40,64]{3,2,1,0:T(8,128)(2,1)} %reshape.319, f32[2,64,40,64]{1,3,2,0:T(8,128)S(1)} %copy.89, f32[2,64,40,64]{1,3,2,0:T(8,128)} %copy.90), kind=kOutput, calls=%fused_computation.117 | convolution fusion | flops 252313600 | bytes 5898240 | tf_op jit(solution)/shard_map/nchk,nchv->nhkv/dot_general | solution.py:39
  37.2 28.0 %while.39 = (s32[]{:T(128)}, f32[40,64]{1,0:T(8,128)S(1)}, f32[40,64,64]{2,1,0:T(8,128)}, f32[2,40,64]{2,1,0:T(8,128)S(1)}, f32[2,40,64,64]{2,3,1,0:T(8,128)}, /...) while((s32[]{:T(128)}, f32[40,64]{1,0:T(8,128)S(1)}, ...), condition=%wide.region_6.7_spmd.clone, body=%wide.region_5.6_spmd.clone.sunk | while | flops 499204 | bytes 9267333 | solution.py:72
  83.0 17.7 %while.38 = (s32[]{:T(128)}, f32[40,64]{1,0:T(8,128)S(1)}, f32[40,64,64]{2,1,0:T(8,128)}, f32[2,40,64]{2,1,0:T(8,128)S(1)}, f32[2,40,64,64]{2,3,1,0:T(8,128)}, /...) while((s32[]{:T(128)}, f32[40,64]{1,0:T(8,128)S(1)}, ...), condition=%wide.region_3.4_spmd.clone, body=%wide.region_2.3_spmd.clone.sunk | while | flops 499203 | bytes 6646389 | solution.py:72
  111.3 7.6 %all-gather.27.cloned.1.call-done = f32[80,64,64]{2,1,0:T(8,128)} async-done(((f32[40,64,64]{2,1,0:T(8,128)}), f32[80,64,64]{2,1,0:T(8,128)}) %all-gather.27.cloned.1.call-update) | async-done | bytes 1310736 | tf_op jit(solution)/shard_map/all_gather | solution.py:28
  122.1 9.9 %all-gather.5 = f32[160,64]{1,0:T(8,128)S(1)} all-gather(f32[40,64]{1,0:T(8,128)S(1)} %get-tuple-element.372), channel_id=7, replica_groups=mesh['seq_0'=4,'seq_1'=2,'seq_2'=4,'seq_3'=2,'dp'=2] {'seq_2'}, dimensions={0}, use_global_device_ids=true | all-gather | bytes 51200 | tf_op jit(solution)/shard_map/all_gather | solution.py:28
  138.8 39.7 %all-gather.21.cloned.1.call-done = f32[4,40,64,64]{3,2,1,0:T(8,128)} async-done(((f32[1,40,64,64]{3,2,1,0:T(8,128)}), f32[4,40,64,64]{3,2,1,0:T(8,128)}) %all-gather.21.cloned.1.call-update) | async-done | bytes 2621456 | tf_op jit(solution)/shard_map/all_gather | solution.py:28
  183.5 9.2 %all-gather.4 = f32[160,64]{1,0:T(8,128)S(1)} all-gather(f32[40,64]{1,0:T(8,128)} %get-tuple-element.377), channel_id=6, replica_groups=mesh['seq_0'=4,'seq_1'=2,'seq_2'=4,'seq_3'=2,'dp'=2] {'seq_2'}, dimensions={0}, use_global_device_ids=true | all-gather | bytes 51200 | tf_op jit(solution)/shard_map/all_gather | solution.py:28
  200.2 37.4 %all-gather.15.cloned.1.call-done = f32[4,40,64,64]{3,2,1,0:T(8,128)} async-done(((f32[1,40,64,64]{3,2,1,0:T(8,128)}), f32[4,40,64,64]{3,2,1,0:T(8,128)}) %all-gather.15.cloned.1.call-update) | async-done | bytes 2621456 | tf_op jit(solution)/shard_map/all_gather | solution.py:28
  243.8 38.6 %all-gather.23.cloned.1.call-done = f32[2,40,64,64]{3,2,1,0:T(8,128)} async-done(((f32[1,40,64,64]{3,2,1,0:T(8,128)}), f32[2,40,64,64]{3,2,1,0:T(8,128)}) %all-gather.23.cloned.1.call-update) | async-done | bytes 1310736 | tf_op jit(solution)/shard_map/all_gather | solution.py:28
  287.4 39.0 %all-gather.17.cloned.1.call-done = f32[2,40,64,64]{3,2,1,0:T(8,128)} async-done(((f32[1,40,64,64]{3,2,1,0:T(8,128)}), f32[2,40,64,64]{3,2,1,0:T(8,128)}) %all-gather.17.cloned.1.call-update) | async-done | bytes 1310736 | tf_op jit(solution)/shard_map/all_gather | solution.py:28
  339.8 11.4 %all_gather.86 = f32[4,40,64]{2,1,0:T(8,128)S(1)} all-gather(f32[1,40,64]{2,1,0:T(8,128)} %get-tuple-element.370), channel_id=1, replica_groups=mesh['seq_0'=4,'seq_1'=2,'seq_2'=4,'seq_3'=2,'dp'=2] {'seq_0'}, dimensions={0}, use_global_device_ids=true | all-gather | bytes 51200 | tf_op jit(solution)/shard_map/all_gather | solution.py:28
  351.2 11.1 %all_gather.76 = f32[4,40,64]{2,1,0:T(8,128)S(1)} all-gather(f32[1,40,64]{2,1,0:T(8,128)} %get-tuple-element.375), channel_id=1, replica_groups=mesh['seq_0'=4,'seq_1'=2,'seq_2'=4,'seq_3'=2,'dp'=2] {'seq_0'}, dimensions={0}, use_global_device_ids=true | all-gather | bytes 51200 | tf_op jit(solution)/shard_map/all_gather | solution.py:28
  370.5 8.1 %fusion.64 = f32[2,40,64,64]{3,2,1,0:T(8,128)} fusion(f32[2,64,40,64]{1,3,2,0:T(8,128)S(1)} %copy-done.3, f32[2,64,40,64]{1,3,2,0:T(8,128)S(1)} %copy.89, f32[2,40,64]{2,1,0:T(8,128)S(1)} %get-tuple-element.350, f32[2,64,40,64]{1,3,2,0:T(8,128)S(1)} %copy-done.6, f32[2,64,40,64]{1,3,2,0:T(8,128)S(1)} %copy-done.1), kind=kOutput, calls=%fused_computation.118 | convolution fusion | flops 253296640 | bytes 6574080 | tf_op jit(solution)/shard_map/nthk,nshk->nhts/dot_general | solution.py:39
  378.6 7.2 %all-gather.25.cloned.1.call-done = f32[4,40,64,64]{3,2,1,0:T(8,128)} async-done(((f32[1,40,64,64]{3,2,1,0:T(8,128)}), f32[4,40,64,64]{3,2,1,0:T(8,128)}) %all-gather.25.cloned.1.call-update) | async-done | bytes 2621456 | tf_op jit(solution)/shard_map/all_gather | solution.py:28
  385.8 9.0 %fusion.36 = f32[40,64,64]{2,1,0:T(8,128)} fusion(f32[4,40,64,64]{3,2,1,0:T(8,128)} %all-gather.25.cloned.1.call-done, f32[4,40,64,64]{3,2,1,0:T(8,128)} %all-gather.21.cloned.1.call-done, f32[2,40,64,64]{3,2,1,0:T(8,128)} %all-gather.23.cloned.1.call-done, f32[80,64,64]{2,1,0:T(8,128)} %all-gather.29.cloned.1.call-done, f32[40,64]{1,0:T(8,128)} %get-tuple-element.337, ...), kind=kLoop, calls=%fused_computation.65 | loop fusion | flops 6225920 | bytes 8673292 | tf_op jit(solution)/shard_map/mul | solution.py:229
  397.7 47.1 %all-gather.19.cloned.1.call-done = f32[4,40,64,64]{3,2,1,0:T(8,128)} async-done(((f32[1,40,64,64]{3,2,1,0:T(8,128)}), f32[4,40,64,64]{3,2,1,0:T(8,128)}) %all-gather.19.cloned.1.call-update) | async-done | bytes 2621456 | tf_op jit(solution)/shard_map/all_gather | solution.py:28
  444.8 9.0 %fusion.42 = f32[40,64,64]{2,1,0:T(8,128)} fusion(f32[4,40,64,64]{3,2,1,0:T(8,128)} %all-gather.19.cloned.1.call-done, f32[4,40,64,64]{3,2,1,0:T(8,128)} %all-gather.15.cloned.1.call-done, f32[2,40,64,64]{3,2,1,0:T(8,128)} %all-gather.17.cloned.1.call-done, f32[80,64,64]{2,1,0:T(8,128)} %all-gather.27.cloned.1.call-done, f32[40,64]{1,0:T(8,128)} %get-tuple-element.340, ...), kind=kLoop, calls=%fused_computation.83 | loop fusion | flops 6225920 | bytes 8673292 | tf_op jit(solution)/shard_map/mul | solution.py:228
  470.4 6.5 fusion.9
  476.9 11.0 %multiply_subtract_fusion = (f32[2,64,40,64]{1,3,2,0:T(8,128)}, f32[2,64,40,64]{1,3,2,0:T(8,128)}, bf16[2,64,40,64]{1,3,2,0:T(8,128)(2,1)}, bf16[2,64,40,64]{1,3,2,0:T(8,128)(2,1)}, f32[2,64,40]{1,2,0:T(8,128)}) fusion(f32[2,64,40,64]{1,3,2,0:T(8,128)S(1)} %copy-done.4, f32[2,64,40,64]{1,3,2,0:T(8,128)S(1)} %copy-done.7, f32[2,64,40,64]{1,3,2,0:T(8,128)} %fusion.9, ...), kind=kOutput, calls=%fused_computation.35 | convolution fusion | flops 258862080 | bytes 13203456 | tf_op jit(solution)/shard_map/nhst,nshk->nthk/dot_general | solution.py:39
  513.6 6.7 fusion.23
  522.5 7.2 %fusion.7 = bf16[2,64,40,64]{3,1,2,0:T(8,128)(2,1)} fusion(f32[2,40,64,64]{2,3,1,0:T(8,128)} %fusion.23, f32[2,40,64,64]{3,2,1,0:T(8,128)} %fusion.64, f32[2,64,40]{1,2,0:T(8,128)S(1)} %copy-done.28, pred[64,64]{1,0:T(8,128)(4,1)S(1)} %iota_compare_fusion, bf16[2,64,40,64]{3,2,1,0:T(8,128)(2,1)} %reshape.319), kind=kOutput, calls=%fused_computation.26 | convolution fusion | flops 253624320 | bytes 3956736 | tf_op jit(solution)/shard_map/nhst,nshv->nthv/dot_general | solution.py:39
  529.7 66.3 %all-reduce = (f32[2560]{0:T(1024)S(1)}, f32[2560]{0:T(1024)S(1)}) all-reduce(f32[2560]{0:T(1024)S(1)} %get-tuple-element.348, f32[2560]{0:T(1024)S(1)} %copy-done.40), channel_id=1, replica_groups=mesh['seq_0'=4,'seq_1'=2,'seq_2'=4,'seq_3'=2,'dp'=2] {'seq_0','seq_1','s..., use_global_device_ids=true, to_apply=%region_12.13 | all-reduce | flops 5120 | bytes 40960 | tf_op jit(solution)/shard_map/psum | solution.py:259
  603.4 8.8 %fusion.22 = f32[2,40,64,64]{2,3,1,0:T(8,128)S(1)} fusion(f32[2,40,64,64]{2,3,1,0:T(8,128)} %get-tuple-element.196, f32[40,64,64]{1,2,0:T(8,128)} %copy.103, f32[2,40,64]{2,1,0:T(8,128)S(1)} %get-tuple-element.193, f32[2,64,40,64]{1,3,2,0:T(8,128)} %copy.91, f32[2,64,40,64]{1,3,2,0:T(8,128)S(1)} %copy.89, f32[2,64,40,64]{1,3,2,0:T(8,128)} %copy.90), kind=kOutput, calls=%fused_computation.58 | convolution fusion | flops 252968960 | bytes 7229440 | tf_op jit(solution)/shard_map/nthk,nhkv->nthv/dot_general | solution.py:39
  623.5 51.8 %all-reduce.4.cloned.1.call-done = (f32[2560,128]{0,1:T(8,128)}, f32[2560,128]{1,0:T(8,128)}) async-done(((f32[2560,128]{0,1:T(8,128)}, f32[2560,128]{1,0:T(8,128)}), (f32[2560,128]{0,1:T(8,128)}, f32[2560,128]{1,0:T(8,128)})) %all-reduce.4.cloned.1.call-update) | async-done | bytes 2621456 | tf_op jit(solution)/shard_map/psum | solution.py:259
  (211 shorter events, 221.2 us)
Async XLA Ops:
  7.2 98.0 %all-gather.29.cloned.1.call-start = ((), (), s32[]{:S(2)}) async-start(), calls=%async_computation.7 | async-start | bytes 3932160 | tf_op jit(solution)/shard_map/all_gather | solution.py:28
  65.8 53.1 %all-gather.27.cloned.1.call-start = ((), (), s32[]{:S(2)}) async-start(), calls=%async_computation.6 | async-start | bytes 3932160 | tf_op jit(solution)/shard_map/all_gather | solution.py:28
  100.7 77.8 %all-gather.21.cloned.1.call-start = ((), (), s32[]{:S(2)}) async-start(), calls=%async_computation.3 | async-start | bytes 6553600 | tf_op jit(solution)/shard_map/all_gather | solution.py:28
  105.1 16.9 %copy-start.37 = (f32[40,64]{1,0:T(8,128)}, f32[40,64]{1,0:T(8,128)S(1)}, u32[]{:S(2)}) copy-start(f32[40,64]{1,0:T(8,128)S(1)} %get-tuple-element.372) | copy-start | bytes 30724
  108.2 129.4 %all-gather.15.cloned.1.call-start = ((), (), s32[]{:S(2)}) async-start(), calls=%async_computation | async-start | bytes 6553600 | tf_op jit(solution)/shard_map/all_gather | solution.py:28
  111.3 10.6 %copy-start.38 = (f32[40,64]{1,0:T(8,128)}, f32[40,64]{1,0:T(8,128)S(1)}, u32[]{:S(2)}) copy-start(f32[40,64]{1,0:T(8,128)S(1)} %get-tuple-element.378) | copy-start | bytes 30724
  122.0 160.4 %all-gather.23.cloned.1.call-start = ((), (), s32[]{:S(2)}) async-start(), calls=%async_computation.4 | async-start | bytes 3932160 | tf_op jit(solution)/shard_map/all_gather | solution.py:28
  183.4 143.0 %all-gather.17.cloned.1.call-start = ((), (), s32[]{:S(2)}) async-start(), calls=%async_computation.1 | async-start | bytes 3932160 | tf_op jit(solution)/shard_map/all_gather | solution.py:28
  242.6 143.2 %all-gather.25.cloned.1.call-start = ((), (), s32[]{:S(2)}) async-start(), calls=%async_computation.5 | async-start | bytes 6553600 | tf_op jit(solution)/shard_map/all_gather | solution.py:28
  285.4 159.3 %all-gather.19.cloned.1.call-start = ((), (), s32[]{:S(2)}) async-start(), calls=%async_computation.2 | async-start | bytes 6553600 | tf_op jit(solution)/shard_map/all_gather | solution.py:28
  329.5 345.8 %all-reduce.4.cloned.1.call-start = ((), (), s32[]{:S(2)}) async-start(), calls=%async_computation.8 | async-start | bytes 5242880 | tf_op jit(solution)/shard_map/psum | solution.py:259
  362.3 8.2 %copy-start.6 = (f32[2,64,40,64]{1,3,2,0:T(8,128)S(1)}, f32[2,64,40,64]{1,3,2,0:T(8,128)}, u32[]{:S(2)}) copy-start(f32[2,64,40,64]{1,3,2,0:T(8,128)} %copy.91) | copy-start | bytes 3932164
  370.5 15.3 %copy-start.32 = (f32[40,64]{1,0:T(8,128)S(1)}, f32[40,64]{1,0:T(8,128)}, u32[]{:S(2)}) copy-start(f32[40,64]{1,0:T(8,128)} %get-tuple-element.356) | copy-start | bytes 30724
  370.5 15.3 %copy-start.33 = (f32[40,64]{1,0:T(8,128)S(1)}, f32[40,64]{1,0:T(8,128)}, u32[]{:S(2)}) copy-start(f32[40,64]{1,0:T(8,128)} %get-tuple-element.357) | copy-start | bytes 30724
  394.8 50.0 %copy-start.34 = (f32[40,64]{1,0:T(8,128)S(1)}, f32[40,64]{1,0:T(8,128)}, u32[]{:S(2)}) copy-start(f32[40,64]{1,0:T(8,128)} %get-tuple-element.365) | copy-start | bytes 30724
  394.8 50.0 %copy-start.35 = (f32[40,64]{1,0:T(8,128)S(1)}, f32[40,64]{1,0:T(8,128)}, u32[]{:S(2)}) copy-start(f32[40,64]{1,0:T(8,128)} %get-tuple-element.366) | copy-start | bytes 30724
  456.6 6.4 copy-start.12
  470.4 6.5 copy-start.7
  470.4 6.5 copy-start.27
  470.4 6.5 copy-start.36
  513.6 6.7 copy-start.20
  522.5 7.2 %copy-start.40 = (f32[2560]{0:T(1024)S(1)}, f32[2560]{0:T(1024)}, u32[]{:S(2)}) copy-start(f32[2560]{0:T(1024)} %multiply_reduce_fusion.2) | copy-start | bytes 30724
  603.4 8.8 %copy-start.10 = (bf16[2,64,40,64]{3,2,1,0:T(8,128)(2,1)S(1)}, bf16[2,64,40,64]{3,2,1,0:T(8,128)(2,1)}, u32[]{:S(2)}) copy-start(bf16[2,64,40,64]{3,2,1,0:T(8,128)(2,1)} %reshape.318) | copy-start | bytes 1966084
  603.4 8.8 %copy-start.14 = (f32[2,40,64,64]{3,2,1,0:T(8,128)S(1)}, f32[2,40,64,64]{3,2,1,0:T(8,128)}, u32[]{:S(2)}) copy-start(f32[2,40,64,64]{3,2,1,0:T(8,128)} %fusion.64) | copy-start | bytes 3932164
  (27 other events, 71.6 us)
Sparse Core Ops, SparseCore 0:
  65.4 17.6 all-gather.28
  100.8 18.0 all-gather.26
  120.6 57.8 all-gather.20
  180.0 57.5 all-gather.14
  239.1 43.2 all-gather.22
  283.9 42.4 all-gather.16
  328.1 57.6 all-gather.24
  387.5 57.2 all-gather.18
  521.9 153.3 all-reduce.3
where the time goes:
time: 694 us; the launch traced here: 685 us
  waiting for transfers between devices  268 us (39%)
  blocking collectives  123 us (18%)
  local copies, waits for them, and re-layouts  111 us (16%)
  other arithmetic  84.8 us (12%)
  matrix products  83.6 us (12%)
  between operations  14.6 us (2%)
    all_gather x8, waiting for transfers between devices, entering_2(): pieces = jax.tree.map(lambda part: lax.all_gather(part, axis), subtotal)  216 us
    dot_general x12, matrix products, contract(): jnp.einsum(pattern, left, right, precision=HIGH, preferred_element_type=j...  76.2 us
    psum x1, blocking collectives, per_device(): whole = lax.psum((sums[0], sums[1], sums[2], sums[3]), SEQ_DP)  66.3 us
    all_gather x8, blocking collectives, entering_2(): pieces = jax.tree.map(lambda part: lax.all_gather(part, axis), subtotal)  56.3 us
    psum x1, waiting for transfers between devices, per_device(): whole = lax.psum((sums[0], sums[1], sums[2], sums[3]), SEQ_DP)  51.8 us
    add x6, other arithmetic, follow(): return (earlier[0] * later[0], later[0][..., None] * earlier[1] + later[1])  22 us
    dynamic_update_slice x8, local copies, waits for them, and re-layouts, compose(): return lax.scan(advance, initial, (decays, own_states), reverse=backward)  21.3 us
  transfers between devices with their start and end apart: 9, of which 8 were waited for; matrix products, arithmetic and copies ran while one was open for 20% of the time, Pallas kernels for 0%

commit v1 on v0

v1 whole, which is shorter than its diff:
```python
import functools
import jax
import jax.numpy as jnp
from jax import lax
from jax.experimental import pallas as pl
from jax.experimental.pallas import tpu as pltpu
from jax.sharding import Mesh
from jax.sharding import PartitionSpec as P

LANE_TOTAL = 64
BLOCK = 64
TOKENS = 128
PAIRS = 20
SPAN = 2560
SEQ = ("seq_0", "seq_1", "seq_2", "seq_3")
F32 = jnp.float32
BF16 = jnp.bfloat16
NN = (((1,), (0,)), ((), ()))
NT = (((1,), (1,)), ((), ()))
TN = (((0,), (0,)), ((), ()))


def mm(left, right, dims):
    return lax.dot_general(left, right, dims, preferred_element_type=F32)


def iotas():
    rows = lax.broadcasted_iota(jnp.int32, (TOKENS, 128), 0)
    cols = lax.broadcasted_iota(jnp.int32, (TOKENS, 128), 1)
    return rows, cols


def parts3(x):
    hi = x.astype(BF16)
    rest = x - hi.astype(F32)
    mid = rest.astype(BF16)
    low = (rest - mid.astype(F32)).astype(BF16)
    return hi, mid, low


def sum_rows(matrix, x):
    hi, mid, low = parts3(x)
    return mm(matrix, hi, NN) + mm(matrix, mid, NN) + mm(matrix, low, NN)


def per_block(row_of, first):
    top = jnp.broadcast_to(row_of[first : first + 1], (BLOCK, 128))
    bottom = jnp.broadcast_to(row_of[BLOCK + first : BLOCK + first + 1], (BLOCK, 128))
    return jnp.concatenate([top, bottom], axis=0)


def pack(full, low_lanes):
    return jnp.where(low_lanes, full[:LANE_TOTAL], full[LANE_TOTAL:])


def early_kernel(x_ref, r_ref, k_ref, v_ref, g_ref, down_ref, up_ref, speed_ref,
                 send_ref, smooth_ref, log_ref, inc_ref, own_ref, pull_ref):
    project = mm(x_ref[...], down_ref[...], NN)
    smooth = jnp.tanh(project)
    smooth_ref[...] = smooth
    gate = smooth.astype(BF16)
    rows, cols = iotas()
    lower = ((rows >= cols) & (rows // BLOCK == cols // BLOCK)).astype(F32).astype(BF16)
    low_lanes = cols[:LANE_TOTAL] < LANE_TOTAL

    def pair(p, carry):
        lanes = pl.ds(pl.multiple_of(p * 128, 128), 128)
        rank = mm(gate, up_ref[lanes, :], NT)
        log_decay = -speed_ref[:, lanes] * jnp.exp(rank)
        inc = sum_rows(lower, log_decay)
        log_ref[:, lanes] = log_decay
        inc_ref[:, lanes] = inc
        exc = inc - log_decay
        total = per_block(inc, BLOCK - 1)
        reached = (r_ref[:, lanes].astype(F32) * jnp.exp(exc)).astype(BF16)
        faded = (k_ref[:, lanes].astype(F32) * jnp.exp(total - inc)).astype(BF16)
        v = v_ref[:, lanes]
        g = g_ref[:, lanes]
        own = [pack(mm(v[b : b + BLOCK], faded[b : b + BLOCK], TN), low_lanes) for b in (0, BLOCK)]
        pull = [pack(mm(g[b : b + BLOCK], reached[b : b + BLOCK], TN), low_lanes) for b in (0, BLOCK)]
        total_0 = inc[BLOCK - 1 : BLOCK]
        total_1 = inc[TOKENS - 1 : TOKENS]
        ahead = jnp.exp(total_1) * own[0] + own[1]
        behind = jnp.exp(total_0) * pull[1] + pull[0]
        whole = jnp.exp(total_0 + total_1)
        here = pl.ds(pl.multiple_of(p * LANE_TOTAL, LANE_TOTAL), LANE_TOTAL)
        own_ref[here, :] = own[0]
        pull_ref[0, here, :] = pull[0]
        pull_ref[1, here, :] = pull[1]
        for way, state in enumerate((ahead, behind)):
            for q in range(8):
                group = way * 160 + p * 8 + q
                slot = group // 5
                place = group % 5
                send_ref[slot, pl.ds(pl.multiple_of(place * 8, 8), 8), :] = state[q * 8 : q * 8 + 8]
                send_ref[slot, pl.ds(40 + place, 1), :] = whole
        return carry

    lax.fori_loop(0, PAIRS, pair, 0)


def scan_kernel(flip_ref, in_ref, out_ref):
    count = in_ref.shape[0]
    flip = flip_ref[0]

    def step(e, run):
        at = jnp.where(flip > 0, count - 1 - e, e)
        result = []
        for q in range(5):
            out_ref[at, q * 8 : q * 8 + 8, :] = run[q]
            decay = in_ref[at, 40 + q : 41 + q, :]
            result.append(decay * run[q] + in_ref[at, q * 8 : q * 8 + 8, :])
        return tuple(result)

    lax.fori_loop(0, count, step, tuple(jnp.zeros((8, 128), F32) for _ in range(5)))


def late_kernel(x_ref, r_ref, k_ref, v_ref, g_ref, down_ref, up_ref, bonus_ref,
                smooth_ref, log_ref, inc_ref, own_ref, pull_ref, state_ref,
                mixed_ref, gr_ref, gk_ref, gv_ref, gx_ref, send_ref):
    smooth = smooth_ref[...]
    gate = smooth.astype(BF16)
    rows, cols = iotas()
    same = rows // BLOCK == cols // BLOCK
    strict = (rows > cols) & same
    strict_2 = jnp.concatenate([strict, strict], axis=0)
    before = strict.astype(F32).astype(BF16)
    heads = ((rows // LANE_TOTAL) == (cols // LANE_TOTAL)).astype(F32).astype(BF16)
    heads_2 = jnp.concatenate([heads, heads], axis=0)
    low = cols < LANE_TOTAL
    low_lanes = low[:LANE_TOTAL]
    nothing = jnp.zeros((TOKENS, 128), BF16)
    nothing_f = jnp.zeros((LANE_TOTAL, 128), F32)

    def two(x):
        x = x.astype(F32)
        zero = jnp.zeros_like(x)
        return jnp.concatenate([jnp.where(low, x, zero), jnp.where(low, zero, x)], axis=0).astype(BF16)

    def corners(state):
        return jnp.concatenate([jnp.where(low_lanes, state, nothing_f), jnp.where(low_lanes, nothing_f, state)], axis=0).astype(BF16)

    def beside(x):
        return jnp.concatenate([x[:TOKENS], x[TOKENS:]], axis=1)

    def head_sums(x):
        hi = x.astype(BF16)
        rest = (x - hi.astype(F32)).astype(BF16)
        return mm(jnp.concatenate([hi, rest], axis=1), heads_2, NN)

    def put(base, p, tile):
        for q in range(16):
            group = base + p * 16 + q
            slot = group // 5
            place = group % 5
            send_ref[slot, pl.ds(pl.multiple_of(place * 8, 8), 8), :] = tile[q * 8 : q * 8 + 8]

    def base_of(p, second):
        half = p // (PAIRS // 2)
        return half * 320 + second * 160 - half * 160

    def pair(p, gate_grad):
        lanes = pl.ds(pl.multiple_of(p * 128, 128), 128)
        here = pl.ds(pl.multiple_of(p * LANE_TOTAL, LANE_TOTAL), LANE_TOTAL)
        there = pl.ds(pl.multiple_of(PAIRS * LANE_TOTAL + p * LANE_TOTAL, LANE_TOTAL), LANE_TOTAL)
        v = v_ref[:, lanes]
        g = g_ref[:, lanes]
        rf = r_ref[:, lanes].astype(F32)
        kf = k_ref[:, lanes].astype(F32)
        vf = v.astype(F32)
        gf = g.astype(F32)
        bonus = bonus_ref[:, lanes]
        log_decay = log_ref[:, lanes]
        inc = inc_ref[:, lanes]
        exc = inc - log_decay
        total = per_block(inc, BLOCK - 1)
        middle = per_block(inc, BLOCK // 2 - 1)
        entering = jnp.exp(exc)
        leaving = jnp.exp(total - inc)
        upward = jnp.exp(exc - middle)
        downward = jnp.exp(middle - inc)
        reached = (rf * entering).astype(BF16)
        faded = (kf * leaving).astype(BF16)
        early = (rf * upward).astype(BF16)
        late = (kf * downward).astype(BF16)
        early_2 = two(early)
        late_2 = two(late)
        v_2 = two(v)
        g_2 = two(g)
        scores = jnp.where(strict_2, mm(early_2, late, NT), 0.0).astype(BF16)
        products = jnp.where(strict_2, mm(g_2, v, NT), 0.0).astype(BF16)
        present = head_sums(rf * bonus * kf)
        agree = head_sums(vf * gf)
        decay_0 = jnp.exp(inc[BLOCK - 1 : BLOCK])
        decay_1 = jnp.exp(inc[TOKENS - 1 : TOKENS])
        start_0 = state_ref[here, :]
        end_1 = state_ref[there, :]
        start_1 = decay_0 * start_0 + own_ref[here, :]
        end_0 = decay_1 * end_1 + pull_ref[1, here, :]
        s_0, s_1, e_0, e_1 = (corners(z) for z in (start_0, start_1, end_0, end_1))

        def blocks(left, right_0, right_1, dims):
            return jnp.concatenate([mm(left[:BLOCK], right_0, dims), mm(left[BLOCK:], right_1, dims)], axis=0)

        mixed = mm(beside(scores), v_2, NN) + blocks(reached, s_0, s_1, NT) + present * vf
        mixed_ref[:, lanes] = mixed.astype(BF16)
        gv = mm(scores, g_2, TN) + blocks(faded, e_0, e_1, NT) + present * gf
        gv_ref[:, lanes] = gv.astype(BF16)
        r_start = blocks(g, s_0, s_1, NN)
        r_near = mm(beside(products), late_2, NN)
        k_end = blocks(v, e_0, e_1, NN)
        k_near = mm(products, early_2, TN)
        gr_ref[:, lanes] = (entering * r_start + upward * r_near + bonus * kf * agree).astype(BF16)
        gk_ref[:, lanes] = (leaving * k_end + downward * k_near + bonus * rf * agree).astype(BF16)
        bonus_row = jnp.sum(rf * kf * agree, axis=0, keepdims=True)
        r_part = reached.astype(F32) * r_start + early.astype(F32) * r_near
        k_part = faded.astype(F32) * k_end + late.astype(F32) * k_near

        def rounded(z):
            return z.astype(BF16).astype(F32)

        couple_0 = jnp.sum((decay_0 * rounded(end_0) + pull_ref[0, here, :]) * rounded(start_0), axis=0, keepdims=True)
        couple_1 = jnp.sum((decay_1 * rounded(end_1) + pull_ref[1, here, :]) * rounded(start_1), axis=0, keepdims=True)
        coupling = jnp.concatenate([jnp.broadcast_to(couple_0, (BLOCK, 128)), jnp.broadcast_to(couple_1, (BLOCK, 128))], axis=0)
        fading = coupling + sum_rows(before, k_part - r_part) - r_part
        slope = fading * log_decay
        slope_half = slope.astype(BF16)
        slope_row = jnp.sum(slope, axis=0, keepdims=True)
        put(base_of(p, 1), p, mm(slope_half, gate, TN))
        half = p // (PAIRS // 2)
        row_slot = half * 64 + p - half * (PAIRS // 2)
        send_ref[row_slot, 40:41, :] = slope_row
        send_ref[row_slot + PAIRS // 2, 40:41, :] = bonus_row
        return gate_grad + mm(slope_half, up_ref[lanes, :], NN)

    gate_grad = lax.fori_loop(0, PAIRS, pair, jnp.zeros((TOKENS, 128), F32))
    project_grad = (gate_grad * (1.0 - smooth * smooth)).astype(BF16)

    def tail(p, carry):
        lanes = pl.ds(pl.multiple_of(p * 128, 128), 128)
        gx_ref[:, lanes] = mm(project_grad, down_ref[lanes, :], NT).astype(BF16)
        put(base_of(p, 0), p, mm(x_ref[:, lanes], project_grad, TN))
        return carry

    lax.fori_loop(0, PAIRS, tail, 0)


def call(kernel, outs, name, flops=0):
    return pl.pallas_call(
        kernel,
        out_shape=[jax.ShapeDtypeStruct(s, d) for s, d in outs],
        compiler_params=pltpu.CompilerParams(vmem_limit_bytes=56 * 1024 * 1024),
        name=name,
    )


def per_device(r, k, v, x, g, down, up, speed, bonus):
    r, k, v, x, g = (z[0] for z in (r, k, v, x, g))
    speed = speed[None]
    bonus = bonus[None]
    wide = (TOKENS, SPAN)
    state_rows = PAIRS * LANE_TOTAL
    send, smooth, log_decay, inc, own, pull = call(
        early_kernel,
        [((64, 48, 128), F32), ((TOKENS, 128), F32), (wide, F32), (wide, F32), ((state_rows, 128), F32), ((2, state_rows, 128), F32)],
        "early",
    )(x, r, k, v, g, down, up, speed)
    got = lax.all_to_all(send, SEQ, 0, 0, tiled=True)
    flip = (lax.axis_index(SEQ) >= 32).astype(jnp.int32)[None]
    back = pl.pallas_call(
        scan_kernel,
        out_shape=jax.ShapeDtypeStruct((64, 40, 128), F32),
        in_specs=[pl.BlockSpec(memory_space=pltpu.SMEM), pl.BlockSpec(memory_space=pltpu.VMEM)],
        name="scan",
    )(flip, got)
    state = lax.all_to_all(back, SEQ, 0, 0, tiled=True).reshape(2 * state_rows, 128)
    mixed, gr, gk, gv, gx, grads = call(
        late_kernel,
        [(wide, BF16)] * 5 + [((128, 48, 128), F32)],
        "late",
    )(x, r, k, v, g, down, up, bonus, smooth, log_decay, inc, own, pull, state)
    pieces = lax.all_to_all(grads, ("dp",) + SEQ, 0, 0, tiled=True)
    mine = jnp.sum(pieces, axis=0)
    whole = lax.all_to_all(jnp.broadcast_to(mine[None], (64, 48, 128)), SEQ, 0, 0, tiled=True)
    lora_a = whole[:32, :40].reshape(SPAN // 2, 128)
    lora_b = whole[32:, :40].reshape(SPAN // 2, 128)
    rows = whole[:20, 40]
    return (mixed[None], gr[None], gk[None], gv[None], gx[None], lora_a, lora_b,
            rows[:10].reshape(SPAN // 2), rows[10:].reshape(SPAN // 2))


def solution(mesh):
    split = Mesh(mesh.devices.reshape(4, 2, 4, 2, mesh.shape["dp"]), SEQ + ("dp",))
    tokens = P("dp", SEQ, None)
    return jax.shard_map(
        per_device,
        mesh=split,
        in_specs=(tokens,) * 5 + (P(),) * 4,
        out_specs=(tokens,) * 5 + (P("dp", None), P("dp", None), P("dp"), P("dp")),
        check_vma=False,
    )
```

time: 694 us -> 195 us (0.28); the launches traced: 685 us -> 195 us
  waiting for transfers between devices: 268 us -> 46.5 us
  local copies, waits for them, and re-layouts: 111 us -> 6.04 us
  other arithmetic: 84.8 us -> 0.23 us
  matrix products: 83.6 us -> 0 us
  Pallas kernels: 0 us -> 47.7 us
  blocking collectives: 123 us -> 76.3 us
  starting transfers between devices: 0.5 us -> 17.3 us
  between operations: 14.6 us -> 0.69 us
    all_gather x8 -> x0, waiting for transfers between devices: 216 us -> none  [entering_2(): pieces = jax.tree.map(lambda part: lax.all_gather(part, axis), subtotal)]
    dot_general x18 -> x0, matrix products: 83.6 us -> none  [the longest x12 76.2 us: contract(): jnp.einsum(pattern, left, right, precision=HIGH, preferred_element_type=j...]
    all_to_all x0 -> x2, blocking collectives: none -> 76.3 us  [the longest x1 45.3 us: per_device(): pieces = lax.all_to_all(grads, ('dp',) + SEQ, 0, 0, tiled=True)]
    psum x1 -> x0, blocking collectives: 66.3 us -> none  [per_device(): whole = lax.psum((sums[0], sums[1], sums[2], sums[3]), SEQ_DP)]
    all_gather x8 -> x0, blocking collectives: 56.3 us -> none  [entering_2(): pieces = jax.tree.map(lambda part: lax.all_gather(part, axis), subtotal)]
    psum x1 -> x0, waiting for transfers between devices: 51.8 us -> none  [per_device(): whole = lax.psum((sums[0], sums[1], sums[2], sums[3]), SEQ_DP)]
    pallas_call x0 -> x3, Pallas kernels: none -> 47.7 us  [the longest x1 28.2 us: per_device(): call(late_kernel, [(wide, BF16)] * 5 + [((128, 48, 128), F32)], 'late')]
    all_to_all x0 -> x2, waiting for transfers between devices: none -> 46.5 us  [the longest x1 24.9 us: per_device(): got = lax.all_to_all(send, SEQ, 0, 0, tiled=True)]
  transfers between devices with their start and end apart: 9 -> 2, of which waited for: 8 -> 2; matrix products, arithmetic and copies ran while one was open for 20% -> 0% of each run, Pallas kernels for 0% -> 0%
where the time goes in v1:
time: 195 us
  blocking collectives  76.3 us (39%)
  Pallas kernels  47.7 us (24%)
  waiting for transfers between devices  46.5 us (24%)
  starting transfers between devices  17.3 us (9%)
  local copies, waits for them, and re-layouts  6.04 us (3%)
    all_to_all x1, blocking collectives, per_device(): pieces = lax.all_to_all(grads, ('dp',) + SEQ, 0, 0, tiled=True)  45.3 us
    all_to_all x1, blocking collectives, per_device(): lax.all_to_all(jnp.broadcast_to(mine[None], (64, 48, 128)), SEQ, 0, 0, ti...  31.1 us
    pallas_call x1, Pallas kernels, per_device(): call(late_kernel, [(wide, BF16)] * 5 + [((128, 48, 128), F32)], 'late')  28.2 us
    all_to_all x1, waiting for transfers between devices, per_device(): got = lax.all_to_all(send, SEQ, 0, 0, tiled=True)  24.9 us
    all_to_all x1, waiting for transfers between devices, per_device(): lax.all_to_all(back, SEQ, 0, 0, tiled=True).reshape(2 * state_rows, 128)  21.6 us
    pallas_call x1, Pallas kernels, per_device(): call(early_kernel, [((64, 48, 128), F32), ((TOKENS, 128), F32), (wide, F3...  16.6 us
    all_to_all x1, starting transfers between devices, per_device(): got = lax.all_to_all(send, SEQ, 0, 0, tiled=True)  12.5 us
    all_to_all x1, starting transfers between devices, per_device(): lax.all_to_all(back, SEQ, 0, 0, tiled=True).reshape(2 * state_rows, 128)  4.8 us
  transfers between devices with their start and end apart: 2, of which 2 were waited for; matrix products, arithmetic and copies ran while one was open for 0% of the time, Pallas kernels for 0%

profile of v1, /device:TPU:1, one launch (start us, length us, event | category | flops | bytes accessed | tf_op | source)
XLA Modules:
  0.0 194.8 jit_solution(8309910110146338923)
XLA Ops:
  0.6 1.3 broadcast_in_dim.33.speed_ref
  2.0 16.6 %early.1 = (f32[64,48,128]{2,1,0:T(8,128)}, f32[128,128]{1,0:T(8,128)}, f32[128,2560]{1,0:T(8,128)}, f32[128,2560]{1,0:T(8,128)}, f32[1280,128]{1,0:T(8,128)}, /*index=5*/f32[2,1280,128]{2,1,0:T(8,128)}) custom-call(bf16[128,2560]{1,0:T(8,128)(2,1)} %bitcast.17, bf16[128,2560]{1,0:T(8,128)(2,1)} %bitcast.19, bf16[128,2560]{1,0:T(8,128)(2,1)} %bitcast.21, ...), custom_call_target="tpu_custom_call" | custom-call | tf_op jit(solution)/shard_map/early/pallas_call | solution.py:263
  18.5 12.5 %all-to-all-start = ((f32[64,48,128]{2,1,0:T(8,128)}), f32[64,48,128]{2,1,0:T(8,128)S(1)}, u32[]{:S(2)}, u32[]{:S(2)}) async-start(f32[64,48,128]{2,1,0:T(8,128)} %get-tuple-element.26), calls=%async_computation | async-start | bytes 3145728 | tf_op jit(solution)/shard_map/all_to_all | solution.py:268
  31.0 24.9 %all-to-all-done.in_ref = f32[64,48,128]{2,1,0:T(8,128)S(1)} async-done(((f32[64,48,128]{2,1,0:T(8,128)}), f32[64,48,128]{2,1,0:T(8,128)S(1)}, u32[]{:S(2)}, u32[]{:S(2)}) %all-to-all-start) | async-done | bytes 1572896 | tf_op jit(solution)/shard_map/all_to_all | solution.py:268
  55.9 0.0 copy-start
  55.9 1.2 copy-done
  57.1 3.0 %scan.1 = f32[64,40,128]{2,1,0:T(8,128)} custom-call(s32[1]{0:T(128)} %bitcast.5.flip_ref, f32[64,48,128]{2,1,0:T(8,128)} %copy-done), custom_call_target="tpu_custom_call" | custom-call | tf_op jit(solution)/shard_map/scan/pallas_call | solution.py:270
  60.1 0.0 copy-start.2
  60.1 4.8 %all-to-all-start.1 = ((f32[64,40,128]{2,1,0:T(8,128)}), f32[64,40,128]{2,1,0:T(8,128)S(1)}, u32[]{:S(2)}, u32[]{:S(2)}) async-start(f32[64,40,128]{2,1,0:T(8,128)} %scan.1), calls=%async_computation.1 | async-start | bytes 2621440 | tf_op jit(solution)/shard_map/all_to_all | solution.py:276
  64.9 0.0 copy-done.2
  64.9 0.6 broadcast_in_dim.32.bonus_ref
  65.5 21.6 %all-to-all-done.1 = f32[64,40,128]{2,1,0:T(8,128)S(1)} async-done(((f32[64,40,128]{2,1,0:T(8,128)}), f32[64,40,128]{2,1,0:T(8,128)S(1)}, u32[]{:S(2)}, u32[]{:S(2)}) %all-to-all-start.1) | async-done | bytes 1310752 | tf_op jit(solution)/shard_map/all_to_all | solution.py:276
  87.1 0.0 copy-start.1
  87.1 1.1 copy-done.1
  88.1 28.2 %late.1 = (bf16[128,2560]{1,0:T(8,128)(2,1)}, bf16[128,2560]{1,0:T(8,128)(2,1)}, bf16[128,2560]{1,0:T(8,128)(2,1)}, bf16[128,2560]{1,0:T(8,128)(2,1)}, bf16[128,...) custom-call(bf16[128,2560]{1,0:T(8,128)(2,1)} %bitcast.18, bf16[128,2560]{1,0:T(8,128)(2,1)} %bitcast.20, ...), custom_call_target="tpu_custom_call" | custom-call | tf_op jit(solution)/shard_map/late/pallas_call | solution.py:277
  116.3 45.3 %all_to_all.20 = f32[128,48,128]{2,1,0:T(8,128)S(1)} all-to-all(f32[128,48,128]{2,1,0:T(8,128)} %get-tuple-element.32), channel_id=1, replica_groups=mesh['seq_0'=4,'seq_1'=2,'seq_2'=4,'seq_3'=2,'dp'=2] {'dp','seq_0','seq_..., dimensions={0} | all-to-all | bytes 6291456 | tf_op jit(solution)/shard_map/all_to_all | solution.py:282
  161.6 0.2 reduce_sum.9
  161.8 0.1 broadcast_in_dim.41
  161.9 31.1 %all_to_all.21 = f32[64,48,128]{2,1,0:T(8,128)S(1)} all-to-all(f32[64,48,128]{2,1,0:T(8,128)S(1)} %broadcast_in_dim.41), channel_id=1, replica_groups=mesh['seq_0'=4,'seq_1'=2,'seq_2'=4,'seq_3'=2,'dp'=2] {'seq_0','seq_1','s..., dimensions={0} | all-to-all | bytes 3145728 | tf_op jit(solution)/shard_map/all_to_all | solution.py:284
  193.0 0.6 slice_reduce_fusion
  193.6 1.1 fusion
Async XLA Ops:
  18.5 37.4 %all-to-all-start = ((f32[64,48,128]{2,1,0:T(8,128)}), f32[64,48,128]{2,1,0:T(8,128)S(1)}, u32[]{:S(2)}, u32[]{:S(2)}) async-start(f32[64,48,128]{2,1,0:T(8,128)} %get-tuple-element.26), calls=%async_computation | async-start | bytes 3145728 | tf_op jit(solution)/shard_map/all_to_all | solution.py:268
  55.9 1.2 copy-start
  60.1 4.8 %copy-start.2 = (f32[2560]{0:T(1024)S(1)}, f32[2560]{0:T(1024)}, u32[]{:S(2)}) copy-start(f32[2560]{0:T(1024)} %param.17) | copy-start | bytes 30724
  60.1 27.0 %all-to-all-start.1 = ((f32[64,40,128]{2,1,0:T(8,128)}), f32[64,40,128]{2,1,0:T(8,128)S(1)}, u32[]{:S(2)}, u32[]{:S(2)}) async-start(f32[64,40,128]{2,1,0:T(8,128)} %scan.1), calls=%async_computation.1 | async-start | bytes 2621440 | tf_op jit(solution)/shard_map/all_to_all | solution.py:276
  87.1 1.1 copy-start.1

commit v2 on v1

v2 whole, which is shorter than its diff:
```python
import jax
import jax.numpy as jnp
from jax import lax
from jax.experimental import pallas as pl
from jax.experimental.pallas import tpu as pltpu
from jax.sharding import Mesh
from jax.sharding import PartitionSpec as P


LANE_TOTAL = 64
BLOCK = 64
TOKENS = 128
PAIRS = 20
SPAN = 2560
SEQ = ("seq_0", "seq_1", "seq_2", "seq_3")
CHIPS = SEQ[:3]
CORE = SEQ[3]
HALF = 10
HALF_ROWS = 640
CHUNK = 5
STEPS = 4
TAIL = 5
VMEM_LIMIT = 56
F32 = jnp.float32
BF16 = jnp.bfloat16
NN = (((1,), (0,)), ((), ()))
NT = (((1,), (1,)), ((), ()))
TN = (((0,), (0,)), ((), ()))


def mm(left, right, dims):
    return lax.dot_general(left, right, dims, preferred_element_type=F32)


def iotas():
    rows = lax.broadcasted_iota(jnp.int32, (TOKENS, 128), 0)
    cols = lax.broadcasted_iota(jnp.int32, (TOKENS, 128), 1)
    return rows, cols


def parts3(x):
    hi = x.astype(BF16)
    rest = x - hi.astype(F32)
    mid = rest.astype(BF16)
    low = (rest - mid.astype(F32)).astype(BF16)
    return hi, mid, low


def sum_rows(matrix, x):
    hi, mid, low = parts3(x)
    return mm(matrix, hi, NN) + mm(matrix, mid, NN) + mm(matrix, low, NN)


def per_block(row_of, first):
    top = jnp.broadcast_to(row_of[first : first + 1], (BLOCK, 128))
    bottom = jnp.broadcast_to(row_of[BLOCK + first : BLOCK + first + 1], (BLOCK, 128))
    return jnp.concatenate([top, bottom], axis=0)


def pack(full, low_lanes):
    return jnp.where(low_lanes, full[:LANE_TOTAL], full[LANE_TOTAL:])


def early_kernel(core_ref, x_ref, r_ref, k_ref, v_ref, g_ref, down_ref, up_ref, speed_ref,
                 theirs_ref, mine_ref, smooth_ref, log_ref, inc_ref, reached_ref, faded_ref, own_ref, pull_ref,
                 stage_ref, sems):
    step = pl.program_id(0)
    half = jnp.where(step < 2, 1 - core_ref[0], core_ref[0])

    @pl.when(step == 0)
    def _():
        smooth_ref[...] = jnp.tanh(mm(x_ref[...], down_ref[...], NN))

    gate = smooth_ref[...].astype(BF16)
    rows, cols = iotas()
    lower = ((rows >= cols) & (rows // BLOCK == cols // BLOCK)).astype(F32).astype(BF16)
    low_lanes = cols[:LANE_TOTAL] < LANE_TOTAL
    base = (step % 2) * CHUNK
    for i in range(CHUNK):
        lanes = slice(i * 128, i * 128 + 128)
        rank = mm(gate, up_ref[lanes, :], NT)
        log_decay = -speed_ref[pl.ds(half * HALF + base + i, 1), :] * jnp.exp(rank)
        inc = sum_rows(lower, log_decay)
        log_ref[:, lanes] = log_decay
        inc_ref[:, lanes] = inc
        exc = inc - log_decay
        total = per_block(inc, BLOCK - 1)
        reached = (r_ref[:, lanes].astype(F32) * jnp.exp(exc)).astype(BF16)
        faded = (k_ref[:, lanes].astype(F32) * jnp.exp(total - inc)).astype(BF16)
        reached_ref[:, lanes] = reached
        faded_ref[:, lanes] = faded
        v = v_ref[:, lanes]
        g = g_ref[:, lanes]
        own = [pack(mm(v[b : b + BLOCK], faded[b : b + BLOCK], TN), low_lanes) for b in (0, BLOCK)]
        pull = [pack(mm(g[b : b + BLOCK], reached[b : b + BLOCK], TN), low_lanes) for b in (0, BLOCK)]
        total_0 = inc[BLOCK - 1 : BLOCK]
        total_1 = inc[TOKENS - 1 : TOKENS]
        here = slice(i * LANE_TOTAL, i * LANE_TOTAL + LANE_TOTAL)
        own_ref[here, :] = own[0]
        pull_ref[0, here, :] = pull[0]
        pull_ref[1, here, :] = pull[1]
        row = pl.multiple_of((base + i) * LANE_TOTAL, LANE_TOTAL)
        stage_ref[step // 2, pl.ds(row, LANE_TOTAL), :] = jnp.exp(total_1) * own[0] + own[1]
        stage_ref[step // 2, pl.ds(HALF_ROWS + row, LANE_TOTAL), :] = jnp.exp(total_0) * pull[1] + pull[0]
        stage_ref[step // 2, pl.ds(2 * HALF_ROWS + base + i, 1), :] = jnp.exp(total_0 + total_1)

    @pl.when(step == STEPS - 1)
    def _():
        copies = [pltpu.make_async_copy(stage_ref.at[j], ref, sems.at[j]) for j, ref in enumerate((theirs_ref, mine_ref))]
        for copy in copies:
            copy.start()
        for copy in copies:
            copy.wait()


def join_kernel(place_ref, mine_ref, other_ref, send_ref):
    first = place_ref[0] == 0

    def both(rows):
        mine = mine_ref[rows, :]
        other = other_ref[rows, :]
        return jnp.where(first, mine, other), jnp.where(first, other, mine)

    for i in range(HALF):
        decay_a, decay_b = both(slice(2 * HALF_ROWS + i, 2 * HALF_ROWS + i + 1))
        decay = decay_a * decay_b
        for q in range(8):
            at = i * LANE_TOTAL + q * 8
            own_a, own_b = both(slice(at, at + 8))
            pull_a, pull_b = both(slice(HALF_ROWS + at, HALF_ROWS + at + 8))
            for way, state in enumerate((decay_b * own_a + own_b, pull_a + decay_a * pull_b)):
                group = way * 80 + i * 8 + q
                slot, place = divmod(group, 5)
                send_ref[slot, place * 8 : place * 8 + 8, :] = state
                send_ref[slot, 40 + place : 41 + place, :] = decay


def scan_kernel(place_ref, in_ref, out_ref):
    count = in_ref.shape[0]
    flip = place_ref[0]

    def step(e, run):
        at = jnp.where(flip > 0, count - 1 - e, e)
        result = []
        for q in range(5):
            out_ref[at, q * 8 : q * 8 + 8, :] = run[q]
            decay = in_ref[at, 40 + q : 41 + q, :]
            result.append(decay * run[q] + in_ref[at, q * 8 : q * 8 + 8, :])
        return tuple(result)

    lax.fori_loop(0, count, step, tuple(jnp.zeros((8, 128), F32) for _ in range(5)))


def part_kernel(place_ref, chip_ref, mine_ref, other_ref, keep_ref, give_ref):
    first = place_ref[0] == 0

    def both(rows):
        mine = mine_ref[rows, :]
        other = other_ref[rows, :]
        return jnp.where(first, mine, other), jnp.where(first, other, mine)

    for i in range(HALF):
        decay_a, decay_b = both(slice(2 * HALF_ROWS + i, 2 * HALF_ROWS + i + 1))
        ahead = slice(i * LANE_TOTAL, i * LANE_TOTAL + LANE_TOTAL)
        behind = slice(HALF_ROWS + i * LANE_TOTAL, HALF_ROWS + i * LANE_TOTAL + LANE_TOTAL)
        start_a = chip_ref[ahead, :]
        end_b = chip_ref[behind, :]
        start_b = decay_a * start_a + jnp.where(first, mine_ref[ahead, :], other_ref[ahead, :])
        end_a = decay_b * end_b + jnp.where(first, other_ref[behind, :], mine_ref[behind, :])
        keep_ref[ahead, :] = jnp.where(first, start_a, start_b)
        give_ref[ahead, :] = jnp.where(first, start_b, start_a)
        keep_ref[behind, :] = jnp.where(first, end_a, end_b)
        give_ref[behind, :] = jnp.where(first, end_b, end_a)


def two(x, low):
    x = x.astype(F32)
    zero = jnp.zeros_like(x)
    return jnp.concatenate([jnp.where(low, x, zero), jnp.where(low, zero, x)], axis=0).astype(BF16)


def corners(state, low_lanes):
    zero = jnp.zeros_like(state)
    return jnp.concatenate([jnp.where(low_lanes, state, zero), jnp.where(low_lanes, zero, state)], axis=0).astype(BF16)


def beside(x):
    return jnp.concatenate([x[:TOKENS], x[TOKENS:]], axis=1)


def blocks(left, right_0, right_1, dims):
    return jnp.concatenate([mm(left[:BLOCK], right_0, dims), mm(left[BLOCK:], right_1, dims)], axis=0)


def near_kernel(core_ref, r_ref, k_ref, v_ref, g_ref, bonus_ref, log_ref, inc_ref,
                fade_ref, mixed_ref, gr_ref, gk_ref, gv_ref, row_ref):
    rows, cols = iotas()
    same = rows // BLOCK == cols // BLOCK
    strict = (rows > cols) & same
    strict_2 = jnp.concatenate([strict, strict], axis=0)
    before = strict.astype(F32).astype(BF16)
    heads = ((rows // LANE_TOTAL) == (cols // LANE_TOTAL)).astype(F32).astype(BF16)
    heads_2 = jnp.concatenate([heads, heads], axis=0)
    low = cols < LANE_TOTAL

    def head_sums(x):
        hi = x.astype(BF16)
        rest = (x - hi.astype(F32)).astype(BF16)
        return mm(jnp.concatenate([hi, rest], axis=1), heads_2, NN)

    step = pl.program_id(0)
    for i in range(CHUNK):
        p = step * CHUNK + i
        lanes = slice(i * 128, i * 128 + 128)
        v = v_ref[:, lanes]
        g = g_ref[:, lanes]
        rf = r_ref[:, lanes].astype(F32)
        kf = k_ref[:, lanes].astype(F32)
        vf = v.astype(F32)
        gf = g.astype(F32)
        bonus = bonus_ref[pl.ds(p, 1), :]
        inc = inc_ref[:, lanes]
        exc = inc - log_ref[:, lanes]
        middle = per_block(inc, BLOCK // 2 - 1)
        upward = jnp.exp(exc - middle)
        downward = jnp.exp(middle - inc)
        early = (rf * upward).astype(BF16)
        late = (kf * downward).astype(BF16)
        early_2 = two(early, low)
        late_2 = two(late, low)
        v_2 = two(v, low)
        g_2 = two(g, low)
        scores = jnp.where(strict_2, mm(early_2, late, NT), 0.0).astype(BF16)
        products = jnp.where(strict_2, mm(g_2, v, NT), 0.0).astype(BF16)
        present = head_sums(rf * bonus * kf)
        agree = head_sums(vf * gf)
        mixed_ref[:, lanes] = mm(beside(scores), v_2, NN) + present * vf
        gv_ref[:, lanes] = mm(scores, g_2, TN) + present * gf
        r_near = mm(beside(products), late_2, NN)
        k_near = mm(products, early_2, TN)
        gr_ref[:, lanes] = upward * r_near + bonus * kf * agree
        gk_ref[:, lanes] = downward * k_near + bonus * rf * agree
        row_ref[pl.ds(p, 1), :] = jnp.sum(rf * kf * agree, axis=0, keepdims=True)
        r_part = early.astype(F32) * r_near
        k_part = late.astype(F32) * k_near
        fade_ref[:, lanes] = sum_rows(before, k_part - r_part) - r_part


def start_and_end(p, i, core, mine_ref, other_ref, own_ref, pull_ref, decay_0, decay_1):
    half = p // HALF
    row = pl.multiple_of((p - half * HALF) * LANE_TOTAL, LANE_TOTAL)
    here = slice(i * LANE_TOTAL, i * LANE_TOTAL + LANE_TOTAL)

    def of(rows):
        return jnp.where(half == core, mine_ref[rows, :], other_ref[rows, :])

    start_0 = of(pl.ds(row, LANE_TOTAL))
    end_1 = of(pl.ds(HALF_ROWS + row, LANE_TOTAL))
    start_1 = decay_0 * start_0 + own_ref[here, :]
    end_0 = decay_1 * end_1 + pull_ref[1, here, :]
    return start_0, start_1, end_0, end_1


def slope_kernel(core_ref, x_ref, v_ref, g_ref, up_ref, smooth_ref, log_ref, inc_ref, reached_ref, faded_ref, own_ref, pull_ref,
                 mine_ref, other_ref, fade_ref, row_ref, keep_ref, give_ref, project_ref, stage_ref, total_ref, sems):
    core = core_ref[0]
    step = pl.program_id(0)
    smooth = smooth_ref[...]
    gate = smooth.astype(BF16)
    rows, cols = iotas()
    strict = (rows > cols) & (rows // BLOCK == cols // BLOCK)
    before = strict.astype(F32).astype(BF16)
    low_lanes = cols[:LANE_TOTAL] < LANE_TOTAL

    def put(index, p, tile):
        half = p // HALF
        for q in range(16):
            group = (p - half * HALF) * 16 + q
            slot = group // 5 * 2 + half
            place = group % 5
            stage_ref[index, slot, pl.ds(pl.multiple_of(place * 8, 8), 8), :] = tile[q * 8 : q * 8 + 8]

    def rounded(z):
        return z.astype(BF16).astype(F32)

    gate_grad = jnp.zeros((TOKENS, 128), F32)
    for i in range(CHUNK):
        p = step * CHUNK + i
        half = p // HALF
        lanes = slice(i * 128, i * 128 + 128)
        here = slice(i * LANE_TOTAL, i * LANE_TOTAL + LANE_TOTAL)
        log_decay = log_ref[:, lanes]
        decay_0 = jnp.exp(inc_ref[BLOCK - 1 : BLOCK, lanes])
        decay_1 = jnp.exp(inc_ref[TOKENS - 1 : TOKENS, lanes])
        start_0, start_1, end_0, end_1 = start_and_end(p, i, core, mine_ref, other_ref, own_ref, pull_ref, decay_0, decay_1)
        s_0, s_1, e_0, e_1 = (corners(z, low_lanes) for z in (start_0, start_1, end_0, end_1))
        r_part = reached_ref[:, lanes].astype(F32) * blocks(g_ref[:, lanes], s_0, s_1, NN)
        k_part = faded_ref[:, lanes].astype(F32) * blocks(v_ref[:, lanes], e_0, e_1, NN)
        couple_0 = jnp.sum((decay_0 * rounded(end_0) + pull_ref[0, here, :]) * rounded(start_0), axis=0, keepdims=True)
        couple_1 = jnp.sum((decay_1 * rounded(end_1) + pull_ref[1, here, :]) * rounded(start_1), axis=0, keepdims=True)
        coupling = jnp.concatenate([jnp.broadcast_to(couple_0, (BLOCK, 128)), jnp.broadcast_to(couple_1, (BLOCK, 128))], axis=0)
        fading = coupling + sum_rows(before, k_part - r_part) - r_part + fade_ref[:, lanes]
        slope = fading * log_decay
        slope_half = slope.astype(BF16)
        put(1 - core, p, mm(slope_half, gate, TN))
        row_slot = (p - half * HALF) * 2 + half
        stage_ref[core, row_slot, 40:41, :] = jnp.sum(slope, axis=0, keepdims=True)
        stage_ref[1 - core, row_slot, 40:41, :] = row_ref[pl.ds(p, 1), :]
        gate_grad = gate_grad + mm(slope_half, up_ref[lanes, :], NN)

    @pl.when(step == 0)
    def _():
        total_ref[...] = gate_grad

    @pl.when(step > 0)
    def _():
        total_ref[...] += gate_grad

    @pl.when(step == STEPS - 1)
    def _():
        project_grad = (total_ref[...] * (1.0 - smooth * smooth)).astype(BF16)
        project_ref[...] = project_grad

        def tail(p, carry):
            lanes = pl.ds(pl.multiple_of(p * 128, 128), 128)
            put(core, p, mm(x_ref[:, lanes], project_grad, TN))
            return carry

        lax.fori_loop(0, PAIRS, tail, 0, unroll=TAIL)
        copies = [pltpu.make_async_copy(stage_ref.at[j], ref, sems.at[j]) for j, ref in enumerate((keep_ref, give_ref))]
        for copy in copies:
            copy.start()
        for copy in copies:
            copy.wait()


def last_kernel(core_ref, v_ref, g_ref, down_ref, log_ref, inc_ref, reached_ref, faded_ref, own_ref, pull_ref, mine_ref, other_ref,
                near_mixed_ref, near_gr_ref, near_gk_ref, near_gv_ref, project_ref,
                mixed_ref, gr_ref, gk_ref, gv_ref, gx_ref):
    _, cols = iotas()
    low_lanes = cols[:LANE_TOTAL] < LANE_TOTAL
    project_grad = project_ref[...]
    core = core_ref[0]
    step = pl.program_id(0)
    for i in range(CHUNK):
        p = step * CHUNK + i
        lanes = slice(i * 128, i * 128 + 128)
        inc = inc_ref[:, lanes]
        decay_0 = jnp.exp(inc[BLOCK - 1 : BLOCK])
        decay_1 = jnp.exp(inc[TOKENS - 1 : TOKENS])
        states = start_and_end(p, i, core, mine_ref, other_ref, own_ref, pull_ref, decay_0, decay_1)
        s_0, s_1, e_0, e_1 = (corners(z, low_lanes) for z in states)
        entering = jnp.exp(inc - log_ref[:, lanes])
        leaving = jnp.exp(per_block(inc, BLOCK - 1) - inc)
        mixed_ref[:, lanes] = (near_mixed_ref[:, lanes] + blocks(reached_ref[:, lanes], s_0, s_1, NT)).astype(BF16)
        gv_ref[:, lanes] = (near_gv_ref[:, lanes] + blocks(faded_ref[:, lanes], e_0, e_1, NT)).astype(BF16)
        gr_ref[:, lanes] = (near_gr_ref[:, lanes] + entering * blocks(g_ref[:, lanes], s_0, s_1, NN)).astype(BF16)
        gk_ref[:, lanes] = (near_gk_ref[:, lanes] + leaving * blocks(v_ref[:, lanes], e_0, e_1, NN)).astype(BF16)
        gx_ref[:, lanes] = mm(project_grad, down_ref[lanes, :], NT).astype(BF16)


def call(kernel, outs, count=0):
    more = {}
    if count:
        more["in_specs"] = [pl.BlockSpec(memory_space=pltpu.SMEM)] + [pl.BlockSpec(memory_space=pltpu.VMEM)] * (count - 1)
    return pl.pallas_call(
        kernel,
        out_shape=[jax.ShapeDtypeStruct(s, d) for s, d in outs],
        compiler_params=pltpu.CompilerParams(vmem_limit_bytes=8 * 1024 * 1024),
        **more,
    )


WIDE = ((TOKENS, SPAN), lambda at: pl.BlockSpec((TOKENS, CHUNK * 128), lambda s, core: (0, at(s, core))))
WEIGHT = ((SPAN, 128), lambda at: pl.BlockSpec((CHUNK * 128, 128), lambda s, core: (at(s, core), 0)))
STATE = ((PAIRS * LANE_TOTAL, 128), lambda at: pl.BlockSpec((CHUNK * LANE_TOTAL, 128), lambda s, core: (at(s, core), 0)))
STATES = ((2, PAIRS * LANE_TOTAL, 128), lambda at: pl.BlockSpec((2, CHUNK * LANE_TOTAL, 128), lambda s, core: (0, at(s, core), 0)))


def whole(*shape):
    return (shape, lambda at: pl.BlockSpec(shape, lambda s, core: (0,) * len(shape)))


def kept(*shape):
    return (shape, lambda at: pl.BlockSpec(memory_space=pl.ANY))


def in_steps(kernel, ins, outs, scratch=(), at=lambda s, core: s, flops=10 ** 9):
    return pl.pallas_call(
        kernel,
        grid_spec=pltpu.PrefetchScalarGridSpec(
            num_scalar_prefetch=1,
            grid=(STEPS,),
            in_specs=[spec(at) for _, spec in ins],
            out_specs=[spec(at) for (_, spec), _ in outs],
            scratch_shapes=list(scratch),
        ),
        out_shape=[jax.ShapeDtypeStruct(shape, dtype) for (shape, _), dtype in outs],
        compiler_params=pltpu.CompilerParams(vmem_limit_bytes=VMEM_LIMIT * 1024 * 1024, dimension_semantics=("arbitrary",)),
        cost_estimate=pl.CostEstimate(flops=flops, bytes_accessed=flops // 1000, transcendentals=0),
    )


def exchange(x, axes):
    return lax.all_to_all(x, axes, 0, 0, tiled=True)


def swap(x):
    return lax.ppermute(x, CORE, [(0, 1), (1, 0)])


def inside(r, k, v, x, g, down, up, speed, bonus):
    r, k, v, x, g = (z[0] for z in (r, k, v, x, g))
    speed = speed.reshape(PAIRS, 128)
    bonus = bonus.reshape(PAIRS, 128)
    core = lax.axis_index(CORE).astype(jnp.int32)[None]
    flip = (lax.axis_index(CHIPS) // 16).astype(jnp.int32)[None]
    rows = whole(PAIRS, 128)
    square = whole(TOKENS, 128)
    part_rows = 2 * HALF_ROWS + 16
    dma = pltpu.SemaphoreType.DMA((2,))
    theirs, mine, smooth, log_decay, inc, reached, faded, own, pull = in_steps(
        early_kernel,
        [whole(TOKENS, SPAN), WIDE, WIDE, WIDE, WIDE, whole(SPAN, 128), WEIGHT, rows],
        [(kept(part_rows, 128), F32), (kept(part_rows, 128), F32), (square, F32), (WIDE, F32), (WIDE, F32), (WIDE, BF16), (WIDE, BF16),
         (STATE, F32), (STATES, F32)],
        (pltpu.VMEM((2, part_rows, 128), F32), dma), lambda s, core: ((1 - core[0]) * 2 + s) % STEPS,
    )(core, x, r, k, v, g, down, up, speed)
    other = swap(theirs)
    (joined,) = call(join_kernel, [((32, 48, 128), F32)], 3)(core, mine, other)
    there = exchange(joined, CHIPS)
    fade, near_mixed, near_gr, near_gk, near_gv, bonus_rows = in_steps(
        near_kernel, [WIDE] * 4 + [rows, WIDE, WIDE], [(WIDE, F32)] * 5 + [(rows, F32)],
    )(core, r, k, v, g, bonus, log_decay, inc)
    (scanned,) = call(scan_kernel, [((32, 40, 128), F32)], 2)(flip, there)
    chip = exchange(scanned, CHIPS).reshape(2 * HALF_ROWS, 128)
    keep, give = call(part_kernel, [((2 * HALF_ROWS, 128), F32)] * 2, 4)(core, chip, mine, other)
    got = swap(give)
    state = whole(2 * HALF_ROWS, 128)
    held, given, project_grad = in_steps(
        slope_kernel,
        [whole(TOKENS, SPAN), WIDE, WIDE, WEIGHT, square, WIDE, WIDE, WIDE, WIDE, STATE, STATES, state, state, WIDE, rows],
        [(kept(64, 48, 128), F32), (kept(64, 48, 128), F32), (square, BF16)],
        (pltpu.VMEM((2, 64, 48, 128), F32), pltpu.VMEM((TOKENS, 128), F32), dma),
    )(core, x, v, g, up, smooth, log_decay, inc, reached, faded, own, pull, keep, got, fade, bonus_rows)
    grads = held + swap(given)
    pieces = exchange(grads, CHIPS + ("dp",))
    mixed, gr, gk, gv, gx = in_steps(
        last_kernel,
        [WIDE, WIDE, WEIGHT, WIDE, WIDE, WIDE, WIDE, STATE, STATES, state, state, WIDE, WIDE, WIDE, WIDE, square],
        [(WIDE, BF16)] * 5,
    )(core, v, g, down, log_decay, inc, reached, faded, own, pull, keep, got, near_mixed, near_gr, near_gk, near_gv, project_grad)
    summed = jnp.sum(pieces, axis=0)
    matrix = exchange(jnp.broadcast_to(summed[None], (32, 48, 128)), CHIPS)
    matrix_2 = swap(matrix)
    a = jnp.where(core[0] == 0, matrix, matrix_2)
    b = jnp.where(core[0] == 0, matrix_2, matrix)
    return (mixed[None], gr[None], gk[None], gv[None], gx[None],
            a[:, :40].reshape(SPAN // 2, 128), b[:, :40].reshape(SPAN // 2, 128),
            a[:HALF, 40].reshape(SPAN // 2), b[:HALF, 40].reshape(SPAN // 2))


def solution(mesh):
    split = Mesh(mesh.devices.reshape(4, 2, 4, 2, mesh.shape["dp"]), SEQ + ("dp",))
    tokens = P("dp", SEQ, None)
    return jax.shard_map(
        inside,
        mesh=split,
        in_specs=(tokens,) * 5 + (P(),) * 4,
        out_specs=(tokens,) * 5 + (P("dp", None), P("dp", None), P("dp"), P("dp")),
        check_vma=False,
    )
```

time: 195 us -> 158 us (0.81)
  waiting for transfers between devices: 46.5 us -> 20 us
  blocking collectives: 76.3 us -> 61.5 us
    all_to_all x2 -> x1, waiting for transfers between devices: 46.5 us -> 14.4 us  [exchange(): return lax.all_to_all(x, axes, 0, 0, tiled=True)]
    all_to_all x2 -> x3, blocking collectives: 76.3 us -> 61.5 us  [exchange(): return lax.all_to_all(x, axes, 0, 0, tiled=True)]
    ppermute x0 -> x4, starting transfers between devices: none -> 7.89 us  [swap(): return lax.ppermute(x, CORE, [(0, 1), (1, 0)])]
    all_to_all x2 -> x1, starting transfers between devices: 17.3 us -> 10.6 us  [exchange(): return lax.all_to_all(x, axes, 0, 0, tiled=True)]
    ppermute x0 -> x4, waiting for transfers between devices: none -> 5.56 us  [swap(): return lax.ppermute(x, CORE, [(0, 1), (1, 0)])]
    broadcast_in_dim x3 -> x1, local copies, waits for them, and re-layouts: 2.04 us -> 0.05 us  [inside(): matrix = exchange(jnp.broadcast_to(summed[None], (32, 48, 128)), CHIPS)]
    pallas_call x3 -> x7, Pallas kernels: 47.7 us -> 49.4 us  [the longest x1 16.5 us: inside(): in_steps(slope_kernel, [whole(TOKENS, SPAN), WIDE, WIDE, WEIGHT, square,...]
  transfers between devices with their start and end apart: 2 -> 5, of which waited for: 2 -> 3; matrix products, arithmetic and copies ran while one was open for 0% -> 0% of each run, Pallas kernels for 0% -> 12%
where the time goes in v2:
time: 158 us; the launch traced here: 157 us
  blocking collectives  61.5 us (39%)
  Pallas kernels  49.4 us (31%)
  waiting for transfers between devices  20 us (13%)
  starting transfers between devices  18.5 us (12%)
  local copies, waits for them, and re-layouts  5.24 us (3%)
  other arithmetic  1.84 us (1%)
    all_to_all x3, blocking collectives, exchange(): return lax.all_to_all(x, axes, 0, 0, tiled=True)  61.5 us
    pallas_call x1, Pallas kernels, inside(): in_steps(slope_kernel, [whole(TOKENS, SPAN), WIDE, WIDE, WEIGHT, square,...  16.5 us
    all_to_all x1, waiting for transfers between devices, exchange(): return lax.all_to_all(x, axes, 0, 0, tiled=True)  14.4 us
    pallas_call x1, Pallas kernels, inside(): in_steps(early_kernel, [whole(TOKENS, SPAN), WIDE, WIDE, WIDE, WIDE, whol...  13.2 us
    all_to_all x1, starting transfers between devices, exchange(): return lax.all_to_all(x, axes, 0, 0, tiled=True)  10.6 us
    pallas_call x1, Pallas kernels, inside(): in_steps(near_kernel, [WIDE] * 4 + [rows, WIDE, WIDE], [(WIDE, F32)] * 5...  9.94 us
    pallas_call x1, Pallas kernels, inside(): in_steps(last_kernel, [WIDE, WIDE, WEIGHT, WIDE, WIDE, WIDE, WIDE, STATE,...  8.42 us
    ppermute x4, starting transfers between devices, swap(): return lax.ppermute(x, CORE, [(0, 1), (1, 0)])  7.89 us
  transfers between devices with their start and end apart: 5, of which 3 were waited for; matrix products, arithmetic and copies ran while one was open for 0% of the time, Pallas kernels for 12%

profile of v2, /device:TPU:1, one launch (start us, length us, event | category | flops | bytes accessed | tf_op | source)
XLA Modules:
  0.0 157.2 jit_solution(36820616789661458)
XLA Ops:
  0.6 13.2 %shard_map.160 = (f32[1296,128]{1,0:T(8,128)}, f32[1296,128]{1,0:T(8,128)}, f32[128,128]{1,0:T(8,128)}, f32[128,2560]{1,0:T(8,128)}, f32[128,2560]{1,0:T(8,128)}...) custom-call(s32[1]{0:T(128)} %bitcast.core_ref.place_ref, ...), custom_call_target="tpu_custom_call" | custom-call | flops 1000000000 | bytes 1000000 | tf_op jit(solution)/shard_map/pallas_call | solution.py:422
  13.8 1.5 collective-permute-start
  15.3 1.9 %collective-permute-done.other_ref = f32[1296,128]{1,0:T(8,128)S(1)} collective-permute-done((f32[1296,128]{1,0:T(8,128)}, f32[1296,128]{1,0:T(8,128)S(1)}, u32[]{:S(2)}, u32[]{:S(2)}) %collective-permute-start) | collective-permute-done | bytes 663584 | tf_op jit(solution)/shard_map/ppermute | solution.py:409
  17.2 1.1 copy-done
  18.3 1.0 shard_map.161
  19.3 10.6 %all-to-all-start = ((f32[32,48,128]{2,1,0:T(8,128)}), f32[32,48,128]{2,1,0:T(8,128)S(1)}, u32[]{:S(2)}, u32[]{:S(2)}) async-start(f32[32,48,128]{2,1,0:T(8,128)} %shard_map.161), calls=%async_computation | async-start | bytes 1572864 | tf_op jit(solution)/shard_map/all_to_all | solution.py:405
  30.0 14.4 %all-to-all-done.in_ref = f32[32,48,128]{2,1,0:T(8,128)S(1)} async-done(((f32[32,48,128]{2,1,0:T(8,128)}), f32[32,48,128]{2,1,0:T(8,128)S(1)}, u32[]{:S(2)}, u32[]{:S(2)}) %all-to-all-start) | async-done | bytes 786464 | tf_op jit(solution)/shard_map/all_to_all | solution.py:405
  44.4 0.2 shard_map.162
  44.7 16.3 %all_to_all.20 = f32[32,40,128]{2,1,0:T(8,128)S(1)} all-to-all(f32[32,40,128]{2,1,0:T(8,128)S(1)} %shard_map.162), channel_id=1, replica_groups=mesh['seq_0'=4,'seq_1'=2,'seq_2'=4,'seq_3'=2,'dp'=2] {'seq_0','seq_1','s..., dimensions={0} | all-to-all | bytes 1310720 | tf_op jit(solution)/shard_map/all_to_all | solution.py:405
  60.9 0.1 shard_map.163
  61.1 0.8 copy-done.2
  61.9 3.3 %collective-permute-start.1 = (f32[1280,128]{1,0:T(8,128)S(1)}, f32[1280,128]{1,0:T(8,128)S(1)}, u32[]{:S(2)}, u32[]{:S(2)}) collective-permute-start(f32[1280,128]{1,0:T(8,128)S(1)} %get-tuple-element.43), channel_id=1, source_target_pairs={{0,2},{2,0},{1,3},{3,1},{4,6},{6,4},{5,7},{7,5},{8,10},{10,8},{9,1... | collective-permute-start | bytes 1966088 | tf_op jit(solution)/shard_map/ppermute | solution.py:409
  65.2 9.9 %shard_map.164 = (f32[128,2560]{1,0:T(8,128)}, f32[128,2560]{1,0:T(8,128)}, f32[128,2560]{1,0:T(8,128)}, f32[128,2560]{1,0:T(8,128)}, f32[128,2560]{1,0:T(8,128)}, /*index=5*/f32[20,128]{1,0:T(8,128)}) custom-call(s32[1]{0:T(128)} %bitcast.core_ref.place_ref, bf16[128,2560]{1,0:T(8,128)(2,1)} %bitcast.31, bf16[128,2560]{1,0:T(8,128)(2,1)} %bitcast.33, ...), custom_call_target="tpu_custom_call" | custom-call | flops 1000000000 | bytes 1000000 | tf_op jit(solution)/shard_map/pallas_call | solution.py:432
  75.2 0.9 copy-done.3
  76.1 16.5 %shard_map.165 = (f32[64,48,128]{2,1,0:T(8,128)}, f32[64,48,128]{2,1,0:T(8,128)}, bf16[128,128]{1,0:T(8,128)(2,1)}) custom-call(s32[1]{0:T(128)} %bitcast.core_ref.place_ref, bf16[128,2560]{1,0:T(8,128)(2,1)} %bitcast.29, bf16[128,2560]{1,0:T(8,128)(2,1)} %bitcast.22, bf16[128,2560]{1,0:T(8,128)(2,1)} %bitcast.26, bf16[2560,128]{1,0:T(8,128)(2,1)} %up_ref.3, ...), custom_call_target="tpu_custom_call" | custom-call | flops 1000000000 | bytes 1000000 | tf_op jit(solution)/shard_map/pallas_call | solution.py:440
  92.6 3.6 %collective-permute-done.2 = f32[64,48,128]{2,1,0:T(8,128)S(1)} collective-permute-done((f32[64,48,128]{2,1,0:T(8,128)}, f32[64,48,128]{2,1,0:T(8,128)S(1)}, u32[]{:S(2)}, u32[]{:S(2)}) %collective-permute-start.2) | collective-permute-done | bytes 1572896 | tf_op jit(solution)/shard_map/ppermute | solution.py:409
  96.2 1.6 %add.12 = f32[64,48,128]{2,1,0:T(8,128)S(1)} add(f32[64,48,128]{2,1,0:T(8,128)} %get-tuple-element.57, f32[64,48,128]{2,1,0:T(8,128)S(1)} %collective-permute-done.2) | non-fusion elementwise | flops 393216 | bytes 4718592 | tf_op jit(solution)/shard_map/add | solution.py:446
  97.8 27.0 %all_to_all.21 = f32[64,48,128]{2,1,0:T(8,128)S(1)} all-to-all(f32[64,48,128]{2,1,0:T(8,128)S(1)} %add.12), channel_id=1, replica_groups=mesh['seq_0'=4,'seq_1'=2,'seq_2'=4,'seq_3'=2,'dp'=2] {'seq_0','seq_1','s..., dimensions={0} | all-to-all | bytes 3145728 | tf_op jit(solution)/shard_map/all_to_all | solution.py:405
  125.0 18.2 %all_to_all.22 = f32[32,48,128]{2,1,0:T(8,128)S(1)} all-to-all(f32[32,48,128]{2,1,0:T(8,128)S(1)} %broadcast_in_dim.34), channel_id=1, replica_groups=mesh['seq_0'=4,'seq_1'=2,'seq_2'=4,'seq_3'=2,'dp'=2] {'seq_0','seq_1','s..., dimensions={0} | all-to-all | bytes 1572864 | tf_op jit(solution)/shard_map/all_to_all | solution.py:405
  143.3 3.0 %collective-permute-start.3 = (f32[32,48,128]{2,1,0:T(8,128)S(1)}, f32[32,48,128]{2,1,0:T(8,128)S(1)}, u32[]{:S(2)}, u32[]{:S(2)}) collective-permute-start(f32[32,48,128]{2,1,0:T(8,128)S(1)} %all_to_all.22), channel_id=1, source_target_pairs={{0,2},{2,0},{1,3},{3,1},{4,6},{6,4},{5,7},{7,5},{8,10},{10,8},{9,1... | collective-permute-start | bytes 2359304 | tf_op jit(solution)/shard_map/ppermute | solution.py:409
  146.3 8.4 %shard_map.166 = (bf16[128,2560]{1,0:T(8,128)(2,1)}, bf16[128,2560]{1,0:T(8,128)(2,1)}, bf16[128,2560]{1,0:T(8,128)(2,1)}, bf16[128,2560]{1,0:T(8,128)(2,1)}, bf16[128,2560]{1,0:T(8,128)(2,1)}) custom-call(s32[1]{0:T(128)} %bitcast.core_ref.place_ref, bf16[128,2560]{1,0:T(8,128)(2,1)} %bitcast.23, bf16[128,2560]{1,0:T(8,128)(2,1)} %bitcast.27, ...), custom_call_target="tpu_custom_call" | custom-call | flops 1000000000 | bytes 1000000 | tf_op jit(solution)/shard_map/pallas_call | solution.py:448
  154.9 0.9 slice.16
  155.7 0.6 slice_reduce_fusion
  156.4 0.9 slice.17
  (11 shorter events, 0.4 us)
Async XLA Ops:
  13.8 3.4 %collective-permute-start = (f32[1296,128]{1,0:T(8,128)}, f32[1296,128]{1,0:T(8,128)S(1)}, u32[]{:S(2)}, u32[]{:S(2)}) collective-permute-start(f32[1296,128]{1,0:T(8,128)} %get-tuple-element.41), channel_id=1, source_target_pairs={{0,2},{2,0},{1,3},{3,1},{4,6},{6,4},{5,7},{7,5},{8,10},{10,8},{9,1... | collective-permute-start | bytes 1990664 | tf_op jit(solution)/shard_map/ppermute | solution.py:409
  17.2 1.1 copy-start
  19.3 25.1 %all-to-all-start = ((f32[32,48,128]{2,1,0:T(8,128)}), f32[32,48,128]{2,1,0:T(8,128)S(1)}, u32[]{:S(2)}, u32[]{:S(2)}) async-start(f32[32,48,128]{2,1,0:T(8,128)} %shard_map.161), calls=%async_computation | async-start | bytes 1572864 | tf_op jit(solution)/shard_map/all_to_all | solution.py:405
  44.4 16.5 %copy-start.1 = (f32[1296,128]{1,0:T(8,128)S(1)}, f32[1296,128]{1,0:T(8,128)}, u32[]{:S(2)}) copy-start(f32[1296,128]{1,0:T(8,128)} %get-tuple-element.40.mine_ref) | copy-start | bytes 1990660
  61.1 0.9 copy-start.2
  61.9 13.3 %collective-permute-start.1 = (f32[1280,128]{1,0:T(8,128)S(1)}, f32[1280,128]{1,0:T(8,128)S(1)}, u32[]{:S(2)}, u32[]{:S(2)}) collective-permute-start(f32[1280,128]{1,0:T(8,128)S(1)} %get-tuple-element.43), channel_id=1, source_target_pairs={{0,2},{2,0},{1,3},{3,1},{4,6},{6,4},{5,7},{7,5},{8,10},{10,8},{9,1... | collective-permute-start | bytes 1966088 | tf_op jit(solution)/shard_map/ppermute | solution.py:409
  75.2 0.9 copy-start.3
  92.5 3.7 %collective-permute-start.2 = (f32[64,48,128]{2,1,0:T(8,128)}, f32[64,48,128]{2,1,0:T(8,128)S(1)}, u32[]{:S(2)}, u32[]{:S(2)}) collective-permute-start(f32[64,48,128]{2,1,0:T(8,128)} %get-tuple-element.58), channel_id=1, source_target_pairs={{0,2},{2,0},{1,3},{3,1},{4,6},{6,4},{5,7},{7,5},{8,10},{10,8},{9,1... | collective-permute-start | bytes 4718600 | tf_op jit(solution)/shard_map/ppermute | solution.py:409
  143.3 11.5 %collective-permute-start.3 = (f32[32,48,128]{2,1,0:T(8,128)S(1)}, f32[32,48,128]{2,1,0:T(8,128)S(1)}, u32[]{:S(2)}, u32[]{:S(2)}) collective-permute-start(f32[32,48,128]{2,1,0:T(8,128)S(1)} %all_to_all.22), channel_id=1, source_target_pairs={{0,2},{2,0},{1,3},{3,1},{4,6},{6,4},{5,7},{7,5},{8,10},{10,8},{9,1... | collective-permute-start | bytes 2359304 | tf_op jit(solution)/shard_map/ppermute | solution.py:409

commit v3 on v2

--- a/solution.py
+++ b/solution.py
@@ -19,7 +19,6 @@
 HALF_ROWS = 640
 CHUNK = 5
 STEPS = 4
-TAIL = 5
 VMEM_LIMIT = 56
 F32 = jnp.float32
 BF16 = jnp.bfloat16
@@ -38,17 +37,22 @@
     return rows, cols
 
 
-def parts3(x):
+def sum_rows(matrix_2, x):
     hi = x.astype(BF16)
-    rest = x - hi.astype(F32)
-    mid = rest.astype(BF16)
-    low = (rest - mid.astype(F32)).astype(BF16)
-    return hi, mid, low
-
-
-def sum_rows(matrix, x):
-    hi, mid, low = parts3(x)
-    return mm(matrix, hi, NN) + mm(matrix, mid, NN) + mm(matrix, low, NN)
+    low = (x - hi.astype(F32)).astype(BF16)
+    return mm(matrix_2, jnp.concatenate([hi, low], axis=0), NN)
+
+
+def twice(mask):
+    one = mask.astype(F32).astype(BF16)
+    return jnp.concatenate([one, one], axis=1)
+
+
+def apart(x):
+    zero = jnp.zeros((BLOCK, x.shape[1]), x.dtype)
+    top = jnp.concatenate([x[:BLOCK], zero], axis=1)
+    bottom = jnp.concatenate([zero, x[BLOCK:]], axis=1)
+    return jnp.concatenate([top, bottom], axis=0)
 
 
 def per_block(row_of, first):
@@ -73,17 +77,18 @@
 
     gate = smooth_ref[...].astype(BF16)
     rows, cols = iotas()
-    lower = ((rows >= cols) & (rows // BLOCK == cols // BLOCK)).astype(F32).astype(BF16)
+    lower = twice((rows >= cols) & (rows // BLOCK == cols // BLOCK))
     low_lanes = cols[:LANE_TOTAL] < LANE_TOTAL
     base = (step % 2) * CHUNK
+    speed = jnp.concatenate([speed_ref[pl.ds(half * HALF + base + i, 1), :] for i in range(CHUNK)], axis=1)
+    log_decays = -speed * jnp.exp(mm(gate, up_ref[...], NT))
+    incs = sum_rows(lower, log_decays)
+    log_ref[...] = log_decays
+    inc_ref[...] = incs
     for i in range(CHUNK):
         lanes = slice(i * 128, i * 128 + 128)
-        rank = mm(gate, up_ref[lanes, :], NT)
-        log_decay = -speed_ref[pl.ds(half * HALF + base + i, 1), :] * jnp.exp(rank)
-        inc = sum_rows(lower, log_decay)
-        log_ref[:, lanes] = log_decay
-        inc_ref[:, lanes] = inc
-        exc = inc - log_decay
+        inc = incs[:, lanes]
+        exc = inc - log_decays[:, lanes]
         total = per_block(inc, BLOCK - 1)
         reached = (r_ref[:, lanes].astype(F32) * jnp.exp(exc)).astype(BF16)
         faded = (k_ref[:, lanes].astype(F32) * jnp.exp(total - inc)).astype(BF16)
@@ -91,8 +96,10 @@
         faded_ref[:, lanes] = faded
         v = v_ref[:, lanes]
         g = g_ref[:, lanes]
-        own = [pack(mm(v[b : b + BLOCK], faded[b : b + BLOCK], TN), low_lanes) for b in (0, BLOCK)]
-        pull = [pack(mm(g[b : b + BLOCK], reached[b : b + BLOCK], TN), low_lanes) for b in (0, BLOCK)]
+        owns = mm(v, apart(faded), TN)
+        pulls = mm(g, apart(reached), TN)
+        own = [pack(owns[:, b : b + 128], low_lanes) for b in (0, 128)]
+        pull = [pack(pulls[:, b : b + 128], low_lanes) for b in (0, 128)]
         total_0 = inc[BLOCK - 1 : BLOCK]
         total_1 = inc[TOKENS - 1 : TOKENS]
         here = slice(i * LANE_TOTAL, i * LANE_TOTAL + LANE_TOTAL)
@@ -189,7 +196,7 @@
 
 
 def blocks(left, right_0, right_1, dims):
-    return jnp.concatenate([mm(left[:BLOCK], right_0, dims), mm(left[BLOCK:], right_1, dims)], axis=0)
+    return mm(apart(left), jnp.concatenate([right_0, right_1], axis=1 if dims == NT else 0), dims)
 
 
 def near_kernel(core_ref, r_ref, k_ref, v_ref, g_ref, bonus_ref, log_ref, inc_ref,
@@ -198,7 +205,7 @@
     same = rows // BLOCK == cols // BLOCK
     strict = (rows > cols) & same
     strict_2 = jnp.concatenate([strict, strict], axis=0)
-    before = strict.astype(F32).astype(BF16)
+    before = twice(strict)
     heads = ((rows // LANE_TOTAL) == (cols // LANE_TOTAL)).astype(F32).astype(BF16)
     heads_2 = jnp.concatenate([heads, heads], axis=0)
     low = cols < LANE_TOTAL
@@ -209,6 +216,7 @@
         return mm(jnp.concatenate([hi, rest], axis=1), heads_2, NN)
 
     step = pl.program_id(0)
+    parts = []
     for i in range(CHUNK):
         p = step * CHUNK + i
         lanes = slice(i * 128, i * 128 + 128)
@@ -243,7 +251,9 @@
         row_ref[pl.ds(p, 1), :] = jnp.sum(rf * kf * agree, axis=0, keepdims=True)
         r_part = early.astype(F32) * r_near
         k_part = late.astype(F32) * k_near
-        fade_ref[:, lanes] = sum_rows(before, k_part - r_part) - r_part
+        parts.append((r_part, k_part))
+    r_parts, k_parts = (jnp.concatenate(z, axis=1) for z in zip(*parts))
+    fade_ref[...] = sum_rows(before, k_parts - r_parts) - r_parts
 
 
 def start_and_end(p, i, core, mine_ref, other_ref, own_ref, pull_ref, decay_0, decay_1):
@@ -262,51 +272,48 @@
 
 
 def slope_kernel(core_ref, x_ref, v_ref, g_ref, up_ref, smooth_ref, log_ref, inc_ref, reached_ref, faded_ref, own_ref, pull_ref,
-                 mine_ref, other_ref, fade_ref, row_ref, keep_ref, give_ref, project_ref, stage_ref, total_ref, sems):
+                 mine_ref, other_ref, fade_ref, row_ref, keep_ref, give_ref, project_ref, stage_ref, rest_ref, total_ref, sems):
     core = core_ref[0]
     step = pl.program_id(0)
     smooth = smooth_ref[...]
     gate = smooth.astype(BF16)
     rows, cols = iotas()
     strict = (rows > cols) & (rows // BLOCK == cols // BLOCK)
-    before = strict.astype(F32).astype(BF16)
+    before = twice(strict)
     low_lanes = cols[:LANE_TOTAL] < LANE_TOTAL
-
-    def put(index, p, tile):
-        half = p // HALF
-        for q in range(16):
-            group = (p - half * HALF) * 16 + q
-            slot = group // 5 * 2 + half
-            place = group % 5
-            stage_ref[index, slot, pl.ds(pl.multiple_of(place * 8, 8), 8), :] = tile[q * 8 : q * 8 + 8]
 
     def rounded(z):
         return z.astype(BF16).astype(F32)
 
-    gate_grad = jnp.zeros((TOKENS, 128), F32)
-    for i in range(CHUNK):
-        p = step * CHUNK + i
-        half = p // HALF
-        lanes = slice(i * 128, i * 128 + 128)
-        here = slice(i * LANE_TOTAL, i * LANE_TOTAL + LANE_TOTAL)
-        log_decay = log_ref[:, lanes]
-        decay_0 = jnp.exp(inc_ref[BLOCK - 1 : BLOCK, lanes])
-        decay_1 = jnp.exp(inc_ref[TOKENS - 1 : TOKENS, lanes])
-        start_0, start_1, end_0, end_1 = start_and_end(p, i, core, mine_ref, other_ref, own_ref, pull_ref, decay_0, decay_1)
-        s_0, s_1, e_0, e_1 = (corners(z, low_lanes) for z in (start_0, start_1, end_0, end_1))
-        r_part = reached_ref[:, lanes].astype(F32) * blocks(g_ref[:, lanes], s_0, s_1, NN)
-        k_part = faded_ref[:, lanes].astype(F32) * blocks(v_ref[:, lanes], e_0, e_1, NN)
-        couple_0 = jnp.sum((decay_0 * rounded(end_0) + pull_ref[0, here, :]) * rounded(start_0), axis=0, keepdims=True)
-        couple_1 = jnp.sum((decay_1 * rounded(end_1) + pull_ref[1, here, :]) * rounded(start_1), axis=0, keepdims=True)
-        coupling = jnp.concatenate([jnp.broadcast_to(couple_0, (BLOCK, 128)), jnp.broadcast_to(couple_1, (BLOCK, 128))], axis=0)
-        fading = coupling + sum_rows(before, k_part - r_part) - r_part + fade_ref[:, lanes]
-        slope = fading * log_decay
-        slope_half = slope.astype(BF16)
-        put(1 - core, p, mm(slope_half, gate, TN))
-        row_slot = (p - half * HALF) * 2 + half
-        stage_ref[core, row_slot, 40:41, :] = jnp.sum(slope, axis=0, keepdims=True)
-        stage_ref[1 - core, row_slot, 40:41, :] = row_ref[pl.ds(p, 1), :]
-        gate_grad = gate_grad + mm(slope_half, up_ref[lanes, :], NN)
+    spread = range(CHUNK)
+    lanes = [slice(i * 128, i * 128 + 128) for i in spread]
+    here = [slice(i * LANE_TOTAL, i * LANE_TOTAL + LANE_TOTAL) for i in spread]
+    decays = jnp.exp(jnp.concatenate([inc_ref[BLOCK - 1 : BLOCK, :], inc_ref[TOKENS - 1 : TOKENS, :]], axis=0))
+    decay = [(decays[0:1, z], decays[1:2, z]) for z in lanes]
+    states = [start_and_end(step * CHUNK + i, i, core, mine_ref, other_ref, own_ref, pull_ref, *decay[i]) for i in spread]
+    sides = [[corners(z, low_lanes) for z in four] for four in states]
+    r_starts = jnp.concatenate([blocks(g_ref[:, lanes[i]], sides[i][0], sides[i][1], NN) for i in spread], axis=1)
+    k_ends = jnp.concatenate([blocks(v_ref[:, lanes[i]], sides[i][2], sides[i][3], NN) for i in spread], axis=1)
+    couples = []
+    for i in spread:
+        start_0, start_1, end_0, end_1 = (rounded(z) for z in states[i])
+        couple_0 = jnp.sum((decay[i][0] * end_0 + pull_ref[0, here[i], :]) * start_0, axis=0, keepdims=True)
+        couple_1 = jnp.sum((decay[i][1] * end_1 + pull_ref[1, here[i], :]) * start_1, axis=0, keepdims=True)
+        couples.append(jnp.concatenate([jnp.broadcast_to(couple_0, (BLOCK, 128)), jnp.broadcast_to(couple_1, (BLOCK, 128))], axis=0))
+    r_part = reached_ref[...].astype(F32) * r_starts
+    k_part = faded_ref[...].astype(F32) * k_ends
+    fading = jnp.concatenate(couples, axis=1) + sum_rows(before, k_part - r_part) - r_part + fade_ref[...]
+    slope = fading * log_ref[...]
+    slope_half = slope.astype(BF16)
+    slope_rows = jnp.sum(slope, axis=0, keepdims=True)
+    gate_grad = mm(slope_half, up_ref[...], NN)
+    tiles = mm(slope_half, gate, TN)
+    half = step // 2
+    base = (step % 2) * CHUNK
+    stage_ref[1 - core, half, pl.ds(pl.multiple_of(base * 128, 128), CHUNK * 128), :] = tiles
+    for i in spread:
+        rest_ref[core, half, base + i, 0:1, :] = slope_rows[:, lanes[i]]
+        rest_ref[1 - core, half, base + i, 0:1, :] = row_ref[pl.ds(step * CHUNK + i, 1), :]
 
     @pl.when(step == 0)
     def _():
@@ -321,13 +328,16 @@
         project_grad = (total_ref[...] * (1.0 - smooth * smooth)).astype(BF16)
         project_ref[...] = project_grad
 
-        def tail(p, carry):
-            lanes = pl.ds(pl.multiple_of(p * 128, 128), 128)
-            put(core, p, mm(x_ref[:, lanes], project_grad, TN))
-            return carry
-
-        lax.fori_loop(0, PAIRS, tail, 0, unroll=TAIL)
-        copies = [pltpu.make_async_copy(stage_ref.at[j], ref, sems.at[j]) for j, ref in enumerate((keep_ref, give_ref))]
+        for c in range(STEPS):
+            tiles = mm(x_ref[:, c * CHUNK * 128 : (c + 1) * CHUNK * 128], project_grad, TN)
+            stage_ref[core, c // 2, (c % 2) * CHUNK * 128 : (c % 2 + 1) * CHUNK * 128, :] = tiles
+
+        copies = []
+        for j, ref in enumerate((keep_ref, give_ref)):
+            for half in range(2):
+                tiles = stage_ref.at[j, half].reshape(32, 40, 128)
+                copies.append(pltpu.make_async_copy(tiles, ref.at[:, half, pl.ds(0, 40), :], sems.at[j, half, 0]))
+                copies.append(pltpu.make_async_copy(rest_ref.at[j, half], ref.at[pl.ds(0, HALF), half, pl.ds(40, 8), :], sems.at[j, half, 1]))
         for copy in copies:
             copy.start()
         for copy in copies:
@@ -409,47 +419,63 @@
     return lax.ppermute(x, CORE, [(0, 1), (1, 0)])
 
 
+ROWS = whole(PAIRS, 128)
+SQUARE = whole(TOKENS, 128)
+PART_ROWS = 2 * HALF_ROWS + 16
+STATE_PART = whole(2 * HALF_ROWS, 128)
+
+
+def early_call():
+    return in_steps(
+        early_kernel,
+        [whole(TOKENS, SPAN), WIDE, WIDE, WIDE, WIDE, whole(SPAN, 128), WEIGHT, ROWS],
+        [(kept(PART_ROWS, 128), F32), (kept(PART_ROWS, 128), F32), (SQUARE, F32), (WIDE, F32), (WIDE, F32), (WIDE, BF16), (WIDE, BF16),
+         (STATE, F32), (STATES, F32)],
+        (pltpu.VMEM((2, PART_ROWS, 128), F32), pltpu.SemaphoreType.DMA((2,))), lambda s, core: ((1 - core[0]) * 2 + s) % STEPS,
+    )
+
+
+def near_call():
+    return in_steps(near_kernel, [WIDE] * 4 + [ROWS, WIDE, WIDE], [(WIDE, F32)] * 5 + [(ROWS, F32)])
+
+
+def slope_call():
+    return in_steps(
+        slope_kernel,
+        [whole(TOKENS, SPAN), WIDE, WIDE, WEIGHT, SQUARE, WIDE, WIDE, WIDE, WIDE, STATE, STATES, STATE_PART, STATE_PART, WIDE, ROWS],
+        [(kept(32, 2, 48, 128), F32), (kept(32, 2, 48, 128), F32), (SQUARE, BF16)],
+        (pltpu.VMEM((2, 2, SPAN // 2, 128), F32), pltpu.VMEM((2, 2, HALF, 8, 128), F32), pltpu.VMEM((TOKENS, 128), F32),
+         pltpu.SemaphoreType.DMA((2, 2, 2))),
+    )
+
+
+def last_call():
+    return in_steps(
+        last_kernel,
+        [WIDE, WIDE, WEIGHT, WIDE, WIDE, WIDE, WIDE, STATE, STATES, STATE_PART, STATE_PART, WIDE, WIDE, WIDE, WIDE, SQUARE],
+        [(WIDE, BF16)] * 5,
+    )
+
+
 def inside(r, k, v, x, g, down, up, speed, bonus):
     r, k, v, x, g = (z[0] for z in (r, k, v, x, g))
     speed = speed.reshape(PAIRS, 128)
     bonus = bonus.reshape(PAIRS, 128)
     core = lax.axis_index(CORE).astype(jnp.int32)[None]
     flip = (lax.axis_index(CHIPS) // 16).astype(jnp.int32)[None]
-    rows = whole(PAIRS, 128)
-    square = whole(TOKENS, 128)
-    part_rows = 2 * HALF_ROWS + 16
-    dma = pltpu.SemaphoreType.DMA((2,))
-    theirs, mine, smooth, log_decay, inc, reached, faded, own, pull = in_steps(
-        early_kernel,
-        [whole(TOKENS, SPAN), WIDE, WIDE, WIDE, WIDE, whole(SPAN, 128), WEIGHT, rows],
-        [(kept(part_rows, 128), F32), (kept(part_rows, 128), F32), (square, F32), (WIDE, F32), (WIDE, F32), (WIDE, BF16), (WIDE, BF16),
-         (STATE, F32), (STATES, F32)],
-        (pltpu.VMEM((2, part_rows, 128), F32), dma), lambda s, core: ((1 - core[0]) * 2 + s) % STEPS,
-    )(core, x, r, k, v, g, down, up, speed)
+    theirs, mine, smooth, log_decay, inc, reached, faded, own, pull = early_call()(core, x, r, k, v, g, down, up, speed)
     other = swap(theirs)
     (joined,) = call(join_kernel, [((32, 48, 128), F32)], 3)(core, mine, other)
     there = exchange(joined, CHIPS)
-    fade, near_mixed, near_gr, near_gk, near_gv, bonus_rows = in_steps(
-        near_kernel, [WIDE] * 4 + [rows, WIDE, WIDE], [(WIDE, F32)] * 5 + [(rows, F32)],
-    )(core, r, k, v, g, bonus, log_decay, inc)
+    fade, near_mixed, near_gr, near_gk, near_gv, bonus_rows = near_call()(core, r, k, v, g, bonus, log_decay, inc)
     (scanned,) = call(scan_kernel, [((32, 40, 128), F32)], 2)(flip, there)
     chip = exchange(scanned, CHIPS).reshape(2 * HALF_ROWS, 128)
     keep, give = call(part_kernel, [((2 * HALF_ROWS, 128), F32)] * 2, 4)(core, chip, mine, other)
     got = swap(give)
-    state = whole(2 * HALF_ROWS, 128)
-    held, given, project_grad = in_steps(
-        slope_kernel,
-        [whole(TOKENS, SPAN), WIDE, WIDE, WEIGHT, square, WIDE, WIDE, WIDE, WIDE, STATE, STATES, state, state, WIDE, rows],
-        [(kept(64, 48, 128), F32), (kept(64, 48, 128), F32), (square, BF16)],
-        (pltpu.VMEM((2, 64, 48, 128), F32), pltpu.VMEM((TOKENS, 128), F32), dma),
-    )(core, x, v, g, up, smooth, log_decay, inc, reached, faded, own, pull, keep, got, fade, bonus_rows)
-    grads = held + swap(given)
+    held, given, project_grad = slope_call()(core, x, v, g, up, smooth, log_decay, inc, reached, faded, own, pull, keep, got, fade, bonus_rows)
+    grads = (held + swap(given)).reshape(64, 48, 128)
     pieces = exchange(grads, CHIPS + ("dp",))
-    mixed, gr, gk, gv, gx = in_steps(
-        last_kernel,
-        [WIDE, WIDE, WEIGHT, WIDE, WIDE, WIDE, WIDE, STATE, STATES, state, state, WIDE, WIDE, WIDE, WIDE, square],
-        [(WIDE, BF16)] * 5,
-    )(core, v, g, down, log_decay, inc, reached, faded, own, pull, keep, got, near_mixed, near_gr, near_gk, near_gv, project_grad)
+    mixed, gr, gk, gv, gx = last_call()(core, v, g, down, log_decay, inc, reached, faded, own, pull, keep, got, near_mixed, near_gr, near_gk, near_gv, project_grad)
     summed = jnp.sum(pieces, axis=0)
     matrix = exchange(jnp.broadcast_to(summed[None], (32, 48, 128)), CHIPS)
     matrix_2 = swap(matrix)

time: 158 us -> 145 us (0.918)
  Pallas kernels: 49.4 us -> 36.1 us
    pallas_call x4, Pallas kernels: 48 us -> 34.7 us  [the longest x1 9.14 us: inside(): slope_call()]
where the time goes in v3:
time: 145 us; the launch traced here: 144 us
  blocking collectives  61.5 us (42%)
  Pallas kernels  36.1 us (25%)
  waiting for transfers between devices  20 us (14%)
  starting transfers between devices  18.5 us (13%)
  local copies, waits for them, and re-layouts  5.24 us (4%)
  other arithmetic  1.87 us (1%)
    all_to_all x3, blocking collectives, exchange(): return lax.all_to_all(x, axes, 0, 0, tiled=True)  61.5 us
    all_to_all x1, waiting for transfers between devices, exchange(): return lax.all_to_all(x, axes, 0, 0, tiled=True)  14.4 us
    all_to_all x1, starting transfers between devices, exchange(): return lax.all_to_all(x, axes, 0, 0, tiled=True)  10.6 us
    pallas_call x1, Pallas kernels, inside(): slope_call()  9.14 us
    pallas_call x1, Pallas kernels, inside(): near_call()(core, r, k, v, g, bonus, log_decay, inc)  8.92 us
    pallas_call x1, Pallas kernels, inside(): early_call()(core, x, r, k, v, g, down, up, speed)  8.63 us
    pallas_call x1, Pallas kernels, inside(): last_call()  8.01 us
    ppermute x4, starting transfers between devices, swap(): return lax.ppermute(x, CORE, [(0, 1), (1, 0)])  7.89 us
  transfers between devices with their start and end apart: 5, of which 3 were waited for; matrix products, arithmetic and copies ran while one was open for 0% of the time, Pallas kernels for 12%

profile of v3, /device:TPU:1, one launch (start us, length us, event | category | flops | bytes accessed | tf_op | source)
XLA Modules:
  0.0 144.0 jit_solution(3618900964278475768)
XLA Ops:
  0.6 8.6 %shard_map.160 = (f32[1296,128]{1,0:T(8,128)}, f32[1296,128]{1,0:T(8,128)}, f32[128,128]{1,0:T(8,128)}, f32[128,2560]{1,0:T(8,128)}, f32[128,2560]{1,0:T(8,128)}...) custom-call(s32[1]{0:T(128)} %bitcast.core_ref.place_ref, ...), custom_call_target="tpu_custom_call" | custom-call | flops 1000000000 | bytes 1000000 | tf_op jit(solution)/shard_map/pallas_call | solution.py:466
  9.3 1.5 %collective-permute-start = (f32[1296,128]{1,0:T(8,128)}, f32[1296,128]{1,0:T(8,128)S(1)}, u32[]{:S(2)}, u32[]{:S(2)}) collective-permute-start(f32[1296,128]{1,0:T(8,128)} %get-tuple-element.41), channel_id=1, source_target_pairs={{0,2},{2,0},{1,3},{3,1},{4,6},{6,4},{5,7},{7,5},{8,10},{10,8},{9,1... | collective-permute-start | bytes 1990664 | tf_op jit(solution)/shard_map/ppermute | solution.py:419
  10.8 1.9 %collective-permute-done.other_ref = f32[1296,128]{1,0:T(8,128)S(1)} collective-permute-done((f32[1296,128]{1,0:T(8,128)}, f32[1296,128]{1,0:T(8,128)S(1)}, u32[]{:S(2)}, u32[]{:S(2)}) %collective-permute-start) | collective-permute-done | bytes 663584 | tf_op jit(solution)/shard_map/ppermute | solution.py:419
  12.7 1.1 copy-done
  13.8 1.0 shard_map.161
  14.8 10.6 %all-to-all-start = ((f32[32,48,128]{2,1,0:T(8,128)}), f32[32,48,128]{2,1,0:T(8,128)S(1)}, u32[]{:S(2)}, u32[]{:S(2)}) async-start(f32[32,48,128]{2,1,0:T(8,128)} %shard_map.161), calls=%async_computation | async-start | bytes 1572864 | tf_op jit(solution)/shard_map/all_to_all | solution.py:415
  25.5 14.4 %all-to-all-done.in_ref = f32[32,48,128]{2,1,0:T(8,128)S(1)} async-done(((f32[32,48,128]{2,1,0:T(8,128)}), f32[32,48,128]{2,1,0:T(8,128)S(1)}, u32[]{:S(2)}, u32[]{:S(2)}) %all-to-all-start) | async-done | bytes 786464 | tf_op jit(solution)/shard_map/all_to_all | solution.py:415
  39.9 0.2 shard_map.162
  40.2 16.3 %all_to_all.20 = f32[32,40,128]{2,1,0:T(8,128)S(1)} all-to-all(f32[32,40,128]{2,1,0:T(8,128)S(1)} %shard_map.162), channel_id=1, replica_groups=mesh['seq_0'=4,'seq_1'=2,'seq_2'=4,'seq_3'=2,'dp'=2] {'seq_0','seq_1','s..., dimensions={0} | all-to-all | bytes 1310720 | tf_op jit(solution)/shard_map/all_to_all | solution.py:415
  56.4 0.1 shard_map.163
  56.6 0.8 copy-done.2
  57.4 3.3 %collective-permute-start.1 = (f32[1280,128]{1,0:T(8,128)S(1)}, f32[1280,128]{1,0:T(8,128)S(1)}, u32[]{:S(2)}, u32[]{:S(2)}) collective-permute-start(f32[1280,128]{1,0:T(8,128)S(1)} %get-tuple-element.43), channel_id=1, source_target_pairs={{0,2},{2,0},{1,3},{3,1},{4,6},{6,4},{5,7},{7,5},{8,10},{10,8},{9,1... | collective-permute-start | bytes 1966088 | tf_op jit(solution)/shard_map/ppermute | solution.py:419
  60.7 8.9 %shard_map.164 = (f32[128,2560]{1,0:T(8,128)}, f32[128,2560]{1,0:T(8,128)}, f32[128,2560]{1,0:T(8,128)}, f32[128,2560]{1,0:T(8,128)}, f32[128,2560]{1,0:T(8,128)}, /*index=5*/f32[20,128]{1,0:T(8,128)}) custom-call(s32[1]{0:T(128)} %bitcast.core_ref.place_ref, bf16[128,2560]{1,0:T(8,128)(2,1)} %bitcast.33, bf16[128,2560]{1,0:T(8,128)(2,1)} %bitcast.35, ...), custom_call_target="tpu_custom_call" | custom-call | flops 1000000000 | bytes 1000000 | tf_op jit(solution)/shard_map/pallas_call | solution.py:470
  69.7 0.9 copy-done.3
  70.5 9.1 %shard_map.165 = (f32[32,2,48,128]{3,2,1,0:T(8,128)}, f32[32,2,48,128]{3,2,1,0:T(8,128)}, bf16[128,128]{1,0:T(8,128)(2,1)}) custom-call(s32[1]{0:T(128)} %bitcast.core_ref.place_ref, bf16[128,2560]{1,0:T(8,128)(2,1)} %bitcast.31, bf16[128,2560]{1,0:T(8,128)(2,1)} %bitcast.23, bf16[128,2560]{1,0:T(8,128)(2,1)} %bitcast.27, bf16[2560,128]{1,0:T(8,128)(2,1)} %up_ref.3, ...), custom_call_target="tpu_custom_call" | custom-call | flops 1000000000 | bytes 1000000 | tf_op jit(solution)/shard_map/pallas_call | solution.py:475
  79.8 3.6 %collective-permute-done.2 = f32[32,2,48,128]{3,2,1,0:T(8,128)S(1)} collective-permute-done((f32[32,2,48,128]{3,2,1,0:T(8,128)}, f32[32,2,48,128]{3,2,1,0:T(8,128)S(1)}, u32[]{:S(2)}, u32[]{:S(2)}) %collective-permute-start.2) | collective-permute-done | bytes 1572896 | tf_op jit(solution)/shard_map/ppermute | solution.py:419
  83.4 1.6 %add.12 = f32[32,2,48,128]{3,2,1,0:T(8,128)S(1)} add(f32[32,2,48,128]{3,2,1,0:T(8,128)} %get-tuple-element.57, f32[32,2,48,128]{3,2,1,0:T(8,128)S(1)} %collective-permute-done.2) | non-fusion elementwise | flops 393216 | bytes 4718592 | tf_op jit(solution)/shard_map/add | solution.py:476
  85.0 27.0 %all_to_all.21 = f32[64,48,128]{2,1,0:T(8,128)S(1)} all-to-all(f32[64,48,128]{2,1,0:T(8,128)S(1)} %bitcast.29), channel_id=1, replica_groups=mesh['seq_0'=4,'seq_1'=2,'seq_2'=4,'seq_3'=2,'dp'=2] {'seq_0','seq_1','s..., dimensions={0} | all-to-all | bytes 3145728 | tf_op jit(solution)/shard_map/all_to_all | solution.py:415
  112.2 18.2 %all_to_all.22 = f32[32,48,128]{2,1,0:T(8,128)S(1)} all-to-all(f32[32,48,128]{2,1,0:T(8,128)S(1)} %broadcast_in_dim.34), channel_id=1, replica_groups=mesh['seq_0'=4,'seq_1'=2,'seq_2'=4,'seq_3'=2,'dp'=2] {'seq_0','seq_1','s..., dimensions={0} | all-to-all | bytes 1572864 | tf_op jit(solution)/shard_map/all_to_all | solution.py:415
  130.4 3.0 %collective-permute-start.3 = (f32[32,48,128]{2,1,0:T(8,128)S(1)}, f32[32,48,128]{2,1,0:T(8,128)S(1)}, u32[]{:S(2)}, u32[]{:S(2)}) collective-permute-start(f32[32,48,128]{2,1,0:T(8,128)S(1)} %all_to_all.22), channel_id=1, source_target_pairs={{0,2},{2,0},{1,3},{3,1},{4,6},{6,4},{5,7},{7,5},{8,10},{10,8},{9,1... | collective-permute-start | bytes 2359304 | tf_op jit(solution)/shard_map/ppermute | solution.py:419
  133.5 8.0 %shard_map.166 = (bf16[128,2560]{1,0:T(8,128)(2,1)}, bf16[128,2560]{1,0:T(8,128)(2,1)}, bf16[128,2560]{1,0:T(8,128)(2,1)}, bf16[128,2560]{1,0:T(8,128)(2,1)}, bf16[128,2560]{1,0:T(8,128)(2,1)}) custom-call(s32[1]{0:T(128)} %bitcast.core_ref.place_ref, bf16[128,2560]{1,0:T(8,128)(2,1)} %bitcast.24, bf16[128,2560]{1,0:T(8,128)(2,1)} %bitcast.28, ...), custom_call_target="tpu_custom_call" | custom-call | flops 1000000000 | bytes 1000000 | tf_op jit(solution)/shard_map/pallas_call | solution.py:478
  141.6 0.9 slice.16
  142.5 0.6 slice_reduce_fusion
  143.1 0.9 slice.17
  (11 shorter events, 0.4 us)
Async XLA Ops:
  9.3 3.4 %collective-permute-start = (f32[1296,128]{1,0:T(8,128)}, f32[1296,128]{1,0:T(8,128)S(1)}, u32[]{:S(2)}, u32[]{:S(2)}) collective-permute-start(f32[1296,128]{1,0:T(8,128)} %get-tuple-element.41), channel_id=1, source_target_pairs={{0,2},{2,0},{1,3},{3,1},{4,6},{6,4},{5,7},{7,5},{8,10},{10,8},{9,1... | collective-permute-start | bytes 1990664 | tf_op jit(solution)/shard_map/ppermute | solution.py:419
  12.7 1.1 copy-start
  14.8 25.1 %all-to-all-start = ((f32[32,48,128]{2,1,0:T(8,128)}), f32[32,48,128]{2,1,0:T(8,128)S(1)}, u32[]{:S(2)}, u32[]{:S(2)}) async-start(f32[32,48,128]{2,1,0:T(8,128)} %shard_map.161), calls=%async_computation | async-start | bytes 1572864 | tf_op jit(solution)/shard_map/all_to_all | solution.py:415
  39.9 16.5 %copy-start.1 = (f32[1296,128]{1,0:T(8,128)S(1)}, f32[1296,128]{1,0:T(8,128)}, u32[]{:S(2)}) copy-start(f32[1296,128]{1,0:T(8,128)} %get-tuple-element.40.mine_ref) | copy-start | bytes 1990660
  56.6 0.9 copy-start.2
  57.4 12.2 %collective-permute-start.1 = (f32[1280,128]{1,0:T(8,128)S(1)}, f32[1280,128]{1,0:T(8,128)S(1)}, u32[]{:S(2)}, u32[]{:S(2)}) collective-permute-start(f32[1280,128]{1,0:T(8,128)S(1)} %get-tuple-element.43), channel_id=1, source_target_pairs={{0,2},{2,0},{1,3},{3,1},{4,6},{6,4},{5,7},{7,5},{8,10},{10,8},{9,1... | collective-permute-start | bytes 1966088 | tf_op jit(solution)/shard_map/ppermute | solution.py:419
  69.7 0.9 copy-start.3
  79.7 3.7 %collective-permute-start.2 = (f32[32,2,48,128]{3,2,1,0:T(8,128)}, f32[32,2,48,128]{3,2,1,0:T(8,128)S(1)}, u32[]{:S(2)}, u32[]{:S(2)}) collective-permute-start(f32[32,2,48,128]{3,2,1,0:T(8,128)} %get-tuple-element.58), channel_id=1, source_target_pairs={{0,2},{2,0},{1,3},{3,1},{4,6},{6,4},{5,7},{7,5},{8,10},{10,8},{9,1... | collective-permute-start | bytes 4718600 | tf_op jit(solution)/shard_map/ppermute | solution.py:419
  130.4 11.1 %collective-permute-start.3 = (f32[32,48,128]{2,1,0:T(8,128)S(1)}, f32[32,48,128]{2,1,0:T(8,128)S(1)}, u32[]{:S(2)}, u32[]{:S(2)}) collective-permute-start(f32[32,48,128]{2,1,0:T(8,128)S(1)} %all_to_all.22), channel_id=1, source_target_pairs={{0,2},{2,0},{1,3},{3,1},{4,6},{6,4},{5,7},{7,5},{8,10},{10,8},{9,1... | collective-permute-start | bytes 2359304 | tf_op jit(solution)/shard_map/ppermute | solution.py:419

commit v4 on v3

--- a/solution.py
+++ b/solution.py
@@ -19,7 +19,8 @@
 HALF_ROWS = 640
 CHUNK = 5
 STEPS = 4
-VMEM_LIMIT = 56
+VMEM_LIMIT = 24
+FREE = ((32, 2, 48, 128), (1296, 128))
 F32 = jnp.float32
 BF16 = jnp.bfloat16
 NN = (((1,), (0,)), ((), ()))
@@ -65,26 +66,16 @@
     return jnp.where(low_lanes, full[:LANE_TOTAL], full[LANE_TOTAL:])
 
 
-def early_kernel(core_ref, x_ref, r_ref, k_ref, v_ref, g_ref, down_ref, up_ref, speed_ref,
-                 theirs_ref, mine_ref, smooth_ref, log_ref, inc_ref, reached_ref, faded_ref, own_ref, pull_ref,
-                 stage_ref, sems):
+def early_steps(half, gate, r_ref, k_ref, v_ref, g_ref, up_ref, speed_ref,
+                log_ref, reached_ref, faded_ref, own_ref, pull_ref, total_ref, send_ref):
     step = pl.program_id(0)
-    half = jnp.where(step < 2, 1 - core_ref[0], core_ref[0])
-
-    @pl.when(step == 0)
-    def _():
-        smooth_ref[...] = jnp.tanh(mm(x_ref[...], down_ref[...], NN))
-
-    gate = smooth_ref[...].astype(BF16)
-    rows, cols = iotas()
-    lower = twice((rows >= cols) & (rows // BLOCK == cols // BLOCK))
-    low_lanes = cols[:LANE_TOTAL] < LANE_TOTAL
-    base = (step % 2) * CHUNK
+    lower = lower_twice()
+    low_lanes = iotas()[1][:LANE_TOTAL] < LANE_TOTAL
+    base = step * CHUNK
     speed = jnp.concatenate([speed_ref[pl.ds(half * HALF + base + i, 1), :] for i in range(CHUNK)], axis=1)
     log_decays = -speed * jnp.exp(mm(gate, up_ref[...], NT))
     incs = sum_rows(lower, log_decays)
     log_ref[...] = log_decays
-    inc_ref[...] = incs
     for i in range(CHUNK):
         lanes = slice(i * 128, i * 128 + 128)
         inc = incs[:, lanes]
@@ -94,10 +85,8 @@
         faded = (k_ref[:, lanes].astype(F32) * jnp.exp(total - inc)).astype(BF16)
         reached_ref[:, lanes] = reached
         faded_ref[:, lanes] = faded
-        v = v_ref[:, lanes]
-        g = g_ref[:, lanes]
-        owns = mm(v, apart(faded), TN)
-        pulls = mm(g, apart(reached), TN)
+        owns = mm(v_ref[:, lanes], apart(faded), TN)
+        pulls = mm(g_ref[:, lanes], apart(reached), TN)
         own = [pack(owns[:, b : b + 128], low_lanes) for b in (0, 128)]
         pull = [pack(pulls[:, b : b + 128], low_lanes) for b in (0, 128)]
         total_0 = inc[BLOCK - 1 : BLOCK]
@@ -106,18 +95,29 @@
         own_ref[here, :] = own[0]
         pull_ref[0, here, :] = pull[0]
         pull_ref[1, here, :] = pull[1]
+        total_ref[0, 0:1, lanes] = total_0
+        total_ref[0, 1:2, lanes] = total_1
         row = pl.multiple_of((base + i) * LANE_TOTAL, LANE_TOTAL)
-        stage_ref[step // 2, pl.ds(row, LANE_TOTAL), :] = jnp.exp(total_1) * own[0] + own[1]
-        stage_ref[step // 2, pl.ds(HALF_ROWS + row, LANE_TOTAL), :] = jnp.exp(total_0) * pull[1] + pull[0]
-        stage_ref[step // 2, pl.ds(2 * HALF_ROWS + base + i, 1), :] = jnp.exp(total_0 + total_1)
-
-    @pl.when(step == STEPS - 1)
+        send_ref[pl.ds(row, LANE_TOTAL), :] = jnp.exp(total_1) * own[0] + own[1]
+        send_ref[pl.ds(HALF_ROWS + row, LANE_TOTAL), :] = jnp.exp(total_0) * pull[1] + pull[0]
+        send_ref[pl.ds(2 * HALF_ROWS + base + i, 1), :] = jnp.exp(total_0 + total_1)
+
+
+def lower_twice():
+    rows, cols = iotas()
+    return twice((rows >= cols) & (rows // BLOCK == cols // BLOCK))
+
+
+def theirs_kernel(core_ref, x_ref, down_ref, r_ref, k_ref, v_ref, g_ref, up_ref, speed_ref, smooth_ref, *outs):
+    @pl.when(pl.program_id(0) == 0)
     def _():
-        copies = [pltpu.make_async_copy(stage_ref.at[j], ref, sems.at[j]) for j, ref in enumerate((theirs_ref, mine_ref))]
-        for copy in copies:
-            copy.start()
-        for copy in copies:
-            copy.wait()
+        smooth_ref[...] = jnp.tanh(mm(x_ref[...], down_ref[...], NN))
+
+    early_steps(1 - core_ref[0], smooth_ref[...].astype(BF16), r_ref, k_ref, v_ref, g_ref, up_ref, speed_ref, *outs)
+
+
+def mine_kernel(core_ref, smooth_ref, r_ref, k_ref, v_ref, g_ref, up_ref, speed_ref, *rest):
+    early_steps(core_ref[0], smooth_ref[...].astype(BF16), r_ref, k_ref, v_ref, g_ref, up_ref, speed_ref, *rest[6:])
 
 
 def join_kernel(place_ref, mine_ref, other_ref, send_ref):
@@ -199,7 +199,7 @@
     return mm(apart(left), jnp.concatenate([right_0, right_1], axis=1 if dims == NT else 0), dims)
 
 
-def near_kernel(core_ref, r_ref, k_ref, v_ref, g_ref, bonus_ref, log_ref, inc_ref,
+def near_kernel(core_ref, r_ref, k_ref, v_ref, g_ref, bonus_ref, log_ref,
                 fade_ref, mixed_ref, gr_ref, gk_ref, gv_ref, row_ref):
     rows, cols = iotas()
     same = rows // BLOCK == cols // BLOCK
@@ -217,6 +217,7 @@
 
     step = pl.program_id(0)
     parts = []
+    incs = sum_rows(lower_twice(), log_ref[...])
     for i in range(CHUNK):
         p = step * CHUNK + i
         lanes = slice(i * 128, i * 128 + 128)
@@ -227,7 +228,7 @@
         vf = v.astype(F32)
         gf = g.astype(F32)
         bonus = bonus_ref[pl.ds(p, 1), :]
-        inc = inc_ref[:, lanes]
+        inc = incs[:, lanes]
         exc = inc - log_ref[:, lanes]
         middle = per_block(inc, BLOCK // 2 - 1)
         upward = jnp.exp(exc - middle)
@@ -256,30 +257,17 @@
     fade_ref[...] = sum_rows(before, k_parts - r_parts) - r_parts
 
 
-def start_and_end(p, i, core, mine_ref, other_ref, own_ref, pull_ref, decay_0, decay_1):
-    half = p // HALF
-    row = pl.multiple_of((p - half * HALF) * LANE_TOTAL, LANE_TOTAL)
+def start_and_end(i, start_0, end_1, own_ref, pull_ref, decay_0, decay_1):
     here = slice(i * LANE_TOTAL, i * LANE_TOTAL + LANE_TOTAL)
-
-    def of(rows):
-        return jnp.where(half == core, mine_ref[rows, :], other_ref[rows, :])
-
-    start_0 = of(pl.ds(row, LANE_TOTAL))
-    end_1 = of(pl.ds(HALF_ROWS + row, LANE_TOTAL))
     start_1 = decay_0 * start_0 + own_ref[here, :]
     end_0 = decay_1 * end_1 + pull_ref[1, here, :]
     return start_0, start_1, end_0, end_1
 
 
-def slope_kernel(core_ref, x_ref, v_ref, g_ref, up_ref, smooth_ref, log_ref, inc_ref, reached_ref, faded_ref, own_ref, pull_ref,
-                 mine_ref, other_ref, fade_ref, row_ref, keep_ref, give_ref, project_ref, stage_ref, rest_ref, total_ref, sems):
-    core = core_ref[0]
+def slope_steps(v_ref, g_ref, log_ref, total_ref, reached_ref, faded_ref, own_ref, pull_ref, state_ref, fade_ref):
     step = pl.program_id(0)
-    smooth = smooth_ref[...]
-    gate = smooth.astype(BF16)
     rows, cols = iotas()
-    strict = (rows > cols) & (rows // BLOCK == cols // BLOCK)
-    before = twice(strict)
+    before = twice((rows > cols) & (rows // BLOCK == cols // BLOCK))
     low_lanes = cols[:LANE_TOTAL] < LANE_TOTAL
 
     def rounded(z):
@@ -288,9 +276,13 @@
     spread = range(CHUNK)
     lanes = [slice(i * 128, i * 128 + 128) for i in spread]
     here = [slice(i * LANE_TOTAL, i * LANE_TOTAL + LANE_TOTAL) for i in spread]
-    decays = jnp.exp(jnp.concatenate([inc_ref[BLOCK - 1 : BLOCK, :], inc_ref[TOKENS - 1 : TOKENS, :]], axis=0))
+    decays = jnp.exp(total_ref[0, 0:2, :])
     decay = [(decays[0:1, z], decays[1:2, z]) for z in lanes]
-    states = [start_and_end(step * CHUNK + i, i, core, mine_ref, other_ref, own_ref, pull_ref, *decay[i]) for i in spread]
+    states = []
+    for i in spread:
+        row = pl.multiple_of((step * CHUNK + i) * LANE_TOTAL, LANE_TOTAL)
+        pair = state_ref[pl.ds(row, LANE_TOTAL), :], state_ref[pl.ds(HALF_ROWS + row, LANE_TOTAL), :]
+        states.append(start_and_end(i, *pair, own_ref, pull_ref, *decay[i]))
     sides = [[corners(z, low_lanes) for z in four] for four in states]
     r_starts = jnp.concatenate([blocks(g_ref[:, lanes[i]], sides[i][0], sides[i][1], NN) for i in spread], axis=1)
     k_ends = jnp.concatenate([blocks(v_ref[:, lanes[i]], sides[i][2], sides[i][3], NN) for i in spread], axis=1)
@@ -304,34 +296,51 @@
     k_part = faded_ref[...].astype(F32) * k_ends
     fading = jnp.concatenate(couples, axis=1) + sum_rows(before, k_part - r_part) - r_part + fade_ref[...]
     slope = fading * log_ref[...]
-    slope_half = slope.astype(BF16)
-    slope_rows = jnp.sum(slope, axis=0, keepdims=True)
-    gate_grad = mm(slope_half, up_ref[...], NN)
-    tiles = mm(slope_half, gate, TN)
-    half = step // 2
-    base = (step % 2) * CHUNK
-    stage_ref[1 - core, half, pl.ds(pl.multiple_of(base * 128, 128), CHUNK * 128), :] = tiles
-    for i in spread:
-        rest_ref[core, half, base + i, 0:1, :] = slope_rows[:, lanes[i]]
-        rest_ref[1 - core, half, base + i, 0:1, :] = row_ref[pl.ds(step * CHUNK + i, 1), :]
+    return slope.astype(BF16), jnp.sum(slope, axis=0, keepdims=True)
+
+
+def slope_kernel(core_ref, v_ref, g_ref, log_ref, total_ref, reached_ref, faded_ref, own_ref, pull_ref, state_ref, fade_ref,
+                 slope_ref, sums_ref):
+    slope_half, sums = slope_steps(v_ref, g_ref, log_ref, total_ref, reached_ref, faded_ref, own_ref, pull_ref, state_ref, fade_ref)
+    slope_ref[...] = slope_half
+    for i in range(CHUNK):
+        sums_ref[pl.ds(pl.program_id(0) * CHUNK + i, 1), :] = sums[:, i * 128 : i * 128 + 128]
+
+
+def grads_kernel(core_ref, v_ref, g_ref, log_ref, total_ref, reached_ref, faded_ref, own_ref, pull_ref, state_ref, fade_ref,
+                 x_ref, up_ref, smooth_ref, slope_ref, sums_ref, row_ref,
+                 keep_ref, give_ref, project_ref, stage_ref, rest_ref, gate_ref, sems):
+    core = core_ref[0]
+    step = pl.program_id(0)
+    smooth = smooth_ref[...]
+    gate = smooth.astype(BF16)
+    width = CHUNK * 128
+
+    def rows_of(half, at):
+        return pl.ds(pl.multiple_of(half * (SPAN // 2) + at * width, 128), width)
 
     @pl.when(step == 0)
     def _():
-        total_ref[...] = gate_grad
-
-    @pl.when(step > 0)
+        slopes = slope_ref[...]
+        stage_ref[1 - core, core] = mm(slopes, gate, TN)
+        gate_ref[...] = mm(slopes, up_ref[pl.ds(pl.multiple_of(core * (SPAN // 2), 128), SPAN // 2), :], NN)
+        for i in range(HALF):
+            rest_ref[core, core, i, 0:1, :] = sums_ref[i : i + 1, :]
+            for half in range(2):
+                rest_ref[1 - core, half, i, 0:1, :] = row_ref[half * HALF + i : half * HALF + i + 1, :]
+
+    slope_half, sums = slope_steps(v_ref, g_ref, log_ref, total_ref, reached_ref, faded_ref, own_ref, pull_ref, state_ref, fade_ref)
+    stage_ref[1 - core, 1 - core, pl.ds(pl.multiple_of(step * width, 128), width), :] = mm(slope_half, gate, TN)
+    for i in range(CHUNK):
+        rest_ref[core, 1 - core, step * CHUNK + i, 0:1, :] = sums[:, i * 128 : i * 128 + 128]
+    gate_ref[...] += mm(slope_half, up_ref[rows_of(1 - core, step), :], NN)
+
+    @pl.when(step == 1)
     def _():
-        total_ref[...] += gate_grad
-
-    @pl.when(step == STEPS - 1)
-    def _():
-        project_grad = (total_ref[...] * (1.0 - smooth * smooth)).astype(BF16)
+        project_grad = (gate_ref[...] * (1.0 - smooth * smooth)).astype(BF16)
         project_ref[...] = project_grad
-
-        for c in range(STEPS):
-            tiles = mm(x_ref[:, c * CHUNK * 128 : (c + 1) * CHUNK * 128], project_grad, TN)
-            stage_ref[core, c // 2, (c % 2) * CHUNK * 128 : (c % 2 + 1) * CHUNK * 128, :] = tiles
-
+        for c in range(4):
+            stage_ref[core, c // 2, c % 2 * width : (c % 2 + 1) * width, :] = mm(x_ref[:, c * width : (c + 1) * width], project_grad, TN)
         copies = []
         for j, ref in enumerate((keep_ref, give_ref)):
             for half in range(2):
@@ -344,7 +353,7 @@
             copy.wait()
 
 
-def last_kernel(core_ref, v_ref, g_ref, down_ref, log_ref, inc_ref, reached_ref, faded_ref, own_ref, pull_ref, mine_ref, other_ref,
+def last_kernel(core_ref, v_ref, g_ref, down_ref, log_ref, reached_ref, faded_ref, own_ref, pull_ref, mine_ref, other_ref,
                 near_mixed_ref, near_gr_ref, near_gk_ref, near_gv_ref, project_ref,
                 mixed_ref, gr_ref, gk_ref, gv_ref, gx_ref):
     _, cols = iotas()
@@ -352,13 +361,16 @@
     project_grad = project_ref[...]
     core = core_ref[0]
     step = pl.program_id(0)
+    incs = sum_rows(lower_twice(), log_ref[...])
     for i in range(CHUNK):
-        p = step * CHUNK + i
         lanes = slice(i * 128, i * 128 + 128)
-        inc = inc_ref[:, lanes]
+        inc = incs[:, lanes]
         decay_0 = jnp.exp(inc[BLOCK - 1 : BLOCK])
         decay_1 = jnp.exp(inc[TOKENS - 1 : TOKENS])
-        states = start_and_end(p, i, core, mine_ref, other_ref, own_ref, pull_ref, decay_0, decay_1)
+        row = pl.multiple_of((step % 2 * CHUNK + i) * LANE_TOTAL, LANE_TOTAL)
+        pair = [jnp.where(step // 2 == core, mine_ref[at, :], other_ref[at, :])
+                for at in (pl.ds(row, LANE_TOTAL), pl.ds(HALF_ROWS + row, LANE_TOTAL))]
+        states = start_and_end(i, *pair, own_ref, pull_ref, decay_0, decay_1)
         s_0, s_1, e_0, e_1 = (corners(z, low_lanes) for z in states)
         entering = jnp.exp(inc - log_ref[:, lanes])
         leaving = jnp.exp(per_block(inc, BLOCK - 1) - inc)
@@ -367,6 +379,37 @@
         gr_ref[:, lanes] = (near_gr_ref[:, lanes] + entering * blocks(g_ref[:, lanes], s_0, s_1, NN)).astype(BF16)
         gk_ref[:, lanes] = (near_gk_ref[:, lanes] + leaving * blocks(v_ref[:, lanes], e_0, e_1, NN)).astype(BF16)
         gx_ref[:, lanes] = mm(project_grad, down_ref[lanes, :], NT).astype(BF16)
+
+
+def final_kernel(core_ref, mine_ref, other_ref, a_ref, b_ref, a_row_ref, b_row_ref, sems):
+    first = core_ref[0] == 0
+
+    def send(x_ref, y_ref):
+        copies = [pltpu.make_async_copy(z.at[:, pl.ds(0, 40), :], ref, sems.at[j]) for j, (z, ref) in enumerate(((x_ref, a_ref), (y_ref, b_ref)))]
+        for copy in copies:
+            copy.start()
+        for i in range(HALF):
+            a_row_ref[i : i + 1, :] = x_ref[i, 40:41, :]
+            b_row_ref[i : i + 1, :] = y_ref[i, 40:41, :]
+        for copy in copies:
+            copy.wait()
+
+    pl.when(first)(lambda: send(mine_ref, other_ref))
+    pl.when(jnp.logical_not(first))(lambda: send(other_ref, mine_ref))
+
+
+def final_call():
+    vmem = pl.BlockSpec(memory_space=pltpu.VMEM)
+    hbm = pl.BlockSpec(memory_space=pl.ANY)
+    return pl.pallas_call(
+        final_kernel,
+        in_specs=[pl.BlockSpec(memory_space=pltpu.SMEM), vmem, vmem],
+        out_specs=[hbm, hbm, vmem, vmem],
+        out_shape=[jax.ShapeDtypeStruct(z, F32) for z in ((32, 40, 128), (32, 40, 128), (HALF, 128), (HALF, 128))],
+        scratch_shapes=[pltpu.SemaphoreType.DMA((2,))],
+        compiler_params=pltpu.CompilerParams(vmem_limit_bytes=8 * 1024 * 1024),
+        name="final",
+    )
 
 
 def call(kernel, outs, count=0):
@@ -395,95 +438,128 @@
     return (shape, lambda at: pl.BlockSpec(memory_space=pl.ANY))
 
 
-def in_steps(kernel, ins, outs, scratch=(), at=lambda s, core: s, flops=10 ** 9):
+TOTAL = ((STEPS, 2, CHUNK * 128), lambda at: pl.BlockSpec((1, 2, CHUNK * 128), lambda s, core: (at(s, core), 0, 0)))
+
+
+def in_steps(kernel, ins, outs, scratch=(), at=lambda s, core: s, steps=STEPS, aliases=None, flops=10 ** 9):
     return pl.pallas_call(
         kernel,
         grid_spec=pltpu.PrefetchScalarGridSpec(
             num_scalar_prefetch=1,
-            grid=(STEPS,),
+            grid=(steps,),
             in_specs=[spec(at) for _, spec in ins],
             out_specs=[spec(at) for (_, spec), _ in outs],
             scratch_shapes=list(scratch),
         ),
-        out_shape=[jax.ShapeDtypeStruct(shape, dtype) for (shape, _), dtype in outs],
+        out_shape=[jax.ShapeDtypeStruct(shape, dtype) if shape in FREE else pltpu.HBM(shape, dtype) for (shape, spec), dtype in outs],
         compiler_params=pltpu.CompilerParams(vmem_limit_bytes=VMEM_LIMIT * 1024 * 1024, dimension_semantics=("arbitrary",)),
         cost_estimate=pl.CostEstimate(flops=flops, bytes_accessed=flops // 1000, transcendentals=0),
-    )
-
-
-def exchange(x, axes):
-    return lax.all_to_all(x, axes, 0, 0, tiled=True)
-
-
-def swap(x):
-    return lax.ppermute(x, CORE, [(0, 1), (1, 0)])
+        input_output_aliases=aliases or {},
+    )
 
 
 ROWS = whole(PAIRS, 128)
 SQUARE = whole(TOKENS, 128)
-PART_ROWS = 2 * HALF_ROWS + 16
+PART = whole(2 * HALF_ROWS + 16, 128)
 STATE_PART = whole(2 * HALF_ROWS, 128)
-
-
-def early_call():
+HALF_WIDE = ((TOKENS, SPAN // 2), lambda at: pl.BlockSpec((TOKENS, CHUNK * 128), lambda s, core: (0, s)))
+EARLY = [(WIDE, F32), (WIDE, BF16), (WIDE, BF16), (STATE, F32), (STATES, F32), (TOTAL, F32)]
+SLOPE = [WIDE, WIDE, WIDE, TOTAL, WIDE, WIDE, STATE, STATES, STATE_PART, WIDE]
+
+
+def mine_half(s, core):
+    return core[0] * 2 + s
+
+
+def their_half(s, core):
+    return (1 - core[0]) * 2 + s
+
+
+def theirs_call():
     return in_steps(
-        early_kernel,
-        [whole(TOKENS, SPAN), WIDE, WIDE, WIDE, WIDE, whole(SPAN, 128), WEIGHT, ROWS],
-        [(kept(PART_ROWS, 128), F32), (kept(PART_ROWS, 128), F32), (SQUARE, F32), (WIDE, F32), (WIDE, F32), (WIDE, BF16), (WIDE, BF16),
-         (STATE, F32), (STATES, F32)],
-        (pltpu.VMEM((2, PART_ROWS, 128), F32), pltpu.SemaphoreType.DMA((2,))), lambda s, core: ((1 - core[0]) * 2 + s) % STEPS,
+        theirs_kernel, [whole(TOKENS, SPAN), whole(SPAN, 128), WIDE, WIDE, WIDE, WIDE, WEIGHT, ROWS],
+        [(SQUARE, F32)] + EARLY + [(PART, F32)], at=their_half, steps=2,
+    )
+
+
+def mine_call():
+    return in_steps(
+        mine_kernel, [SQUARE, WIDE, WIDE, WIDE, WIDE, WEIGHT, ROWS] + [kept(*z[0][0]) for z in EARLY],
+        EARLY + [(PART, F32)], at=mine_half, steps=2, aliases={8 + j: j for j in range(len(EARLY))},
     )
 
 
 def near_call():
-    return in_steps(near_kernel, [WIDE] * 4 + [ROWS, WIDE, WIDE], [(WIDE, F32)] * 5 + [(ROWS, F32)])
+    return in_steps(near_kernel, [WIDE] * 4 + [ROWS, WIDE], [(WIDE, F32)] * 5 + [(ROWS, F32)])
 
 
 def slope_call():
+    return in_steps(slope_kernel, SLOPE, [(HALF_WIDE, BF16), (whole(HALF, 128), F32)], at=mine_half, steps=2)
+
+
+def grads_call():
     return in_steps(
-        slope_kernel,
-        [whole(TOKENS, SPAN), WIDE, WIDE, WEIGHT, SQUARE, WIDE, WIDE, WIDE, WIDE, STATE, STATES, STATE_PART, STATE_PART, WIDE, ROWS],
+        grads_kernel, SLOPE + [whole(TOKENS, SPAN), whole(SPAN, 128), SQUARE, whole(TOKENS, SPAN // 2), whole(HALF, 128), ROWS],
         [(kept(32, 2, 48, 128), F32), (kept(32, 2, 48, 128), F32), (SQUARE, BF16)],
         (pltpu.VMEM((2, 2, SPAN // 2, 128), F32), pltpu.VMEM((2, 2, HALF, 8, 128), F32), pltpu.VMEM((TOKENS, 128), F32),
          pltpu.SemaphoreType.DMA((2, 2, 2))),
+        at=their_half, steps=2,
     )
 
 
 def last_call():
     return in_steps(
         last_kernel,
-        [WIDE, WIDE, WEIGHT, WIDE, WIDE, WIDE, WIDE, STATE, STATES, STATE_PART, STATE_PART, WIDE, WIDE, WIDE, WIDE, SQUARE],
+        [WIDE, WIDE, WEIGHT, WIDE, WIDE, WIDE, STATE, STATES, STATE_PART, STATE_PART, WIDE, WIDE, WIDE, WIDE, SQUARE],
         [(WIDE, BF16)] * 5,
     )
+
+
+def exchange(x, axes):
+    return lax.all_to_all(x, axes, 0, 0, tiled=True)
+
+
+def swap(x):
+    return lax.ppermute(x, CORE, [(0, 1), (1, 0)])
+
+
+def far(*arrays):
+    return [pltpu.with_memory_space_constraint(z, pltpu.HBM) for z in arrays]
 
 
 def inside(r, k, v, x, g, down, up, speed, bonus):
     r, k, v, x, g = (z[0] for z in (r, k, v, x, g))
     speed = speed.reshape(PAIRS, 128)
     bonus = bonus.reshape(PAIRS, 128)
+    r, k, v, x, g, down, up, speed, bonus = far(r, k, v, x, g, down, up, speed, bonus)
     core = lax.axis_index(CORE).astype(jnp.int32)[None]
     flip = (lax.axis_index(CHIPS) // 16).astype(jnp.int32)[None]
-    theirs, mine, smooth, log_decay, inc, reached, faded, own, pull = early_call()(core, x, r, k, v, g, down, up, speed)
+    smooth, *early, theirs = theirs_call()(core, x, down, r, k, v, g, up, speed)
+    (smooth,) = far(smooth)
     other = swap(theirs)
+    *early, mine = mine_call()(core, smooth, r, k, v, g, up, speed, *far(*early))
+    log_decay, reached, faded, own, pull, total = far(*early)
     (joined,) = call(join_kernel, [((32, 48, 128), F32)], 3)(core, mine, other)
     there = exchange(joined, CHIPS)
-    fade, near_mixed, near_gr, near_gk, near_gv, bonus_rows = near_call()(core, r, k, v, g, bonus, log_decay, inc)
+    near = near_call()(core, r, k, v, g, bonus, log_decay)
+    fade, near_mixed, near_gr, near_gk, near_gv, bonus_rows = far(*near)
     (scanned,) = call(scan_kernel, [((32, 40, 128), F32)], 2)(flip, there)
     chip = exchange(scanned, CHIPS).reshape(2 * HALF_ROWS, 128)
     keep, give = call(part_kernel, [((2 * HALF_ROWS, 128), F32)] * 2, 4)(core, chip, mine, other)
     got = swap(give)
-    held, given, project_grad = slope_call()(core, x, v, g, up, smooth, log_decay, inc, reached, faded, own, pull, keep, got, fade, bonus_rows)
+    slope_mine, sums_mine = far(*slope_call()(core, v, g, log_decay, total, reached, faded, own, pull, keep, fade))
+    held, given, project_grad = grads_call()(core, v, g, log_decay, total, reached, faded, own, pull, got, fade,
+                                             x, up, smooth, slope_mine, sums_mine, bonus_rows)
+    (project_grad,) = far(project_grad)
     grads = (held + swap(given)).reshape(64, 48, 128)
     pieces = exchange(grads, CHIPS + ("dp",))
-    mixed, gr, gk, gv, gx = last_call()(core, v, g, down, log_decay, inc, reached, faded, own, pull, keep, got, near_mixed, near_gr, near_gk, near_gv, project_grad)
+    mixed, gr, gk, gv, gx = last_call()(core, v, g, down, log_decay, reached, faded, own, pull, keep, got,
+                                        near_mixed, near_gr, near_gk, near_gv, project_grad)
     summed = jnp.sum(pieces, axis=0)
     matrix = exchange(jnp.broadcast_to(summed[None], (32, 48, 128)), CHIPS)
-    matrix_2 = swap(matrix)
-    a = jnp.where(core[0] == 0, matrix, matrix_2)
-    b = jnp.where(core[0] == 0, matrix_2, matrix)
+    a, b, a_row, b_row = final_call()(core, matrix, swap(matrix))
     return (mixed[None], gr[None], gk[None], gv[None], gx[None],
-            a[:, :40].reshape(SPAN // 2, 128), b[:, :40].reshape(SPAN // 2, 128),
-            a[:HALF, 40].reshape(SPAN // 2), b[:HALF, 40].reshape(SPAN // 2))
+            a.reshape(SPAN // 2, 128), b.reshape(SPAN // 2, 128), a_row.reshape(SPAN // 2), b_row.reshape(SPAN // 2))
 
 
 def solution(mesh):

time: 145 us -> 137 us (0.945)
  local copies, waits for them, and re-layouts: 5.24 us -> 0.05 us
  waiting for transfers between devices: 20 us -> 18.2 us
  Pallas kernels: 36.1 us -> 37.6 us
  other arithmetic: 1.87 us -> 0.37 us
    pallas_call x2 -> x5, Pallas kernels: 17.6 us -> 25 us  [the longest x1 9.42 us: inside(): near = near_call()(core, r, k, v, g, bonus, log_decay)]
    pallas_call x1, Pallas kernels: 9.14 us -> 3.46 us  [inside(): slope_call()]
    unnamed x8 -> x0, local copies, waits for them, and re-layouts: 2.8 us -> none
    slice x3 -> x0, local copies, waits for them, and re-layouts: 2.38 us -> none  [the longest x1 0.88 us: inside(): a[:, :40].reshape(SPAN // 2, 128)]
    ppermute x4, waiting for transfers between devices: 5.56 us -> 3.38 us  [swap(): return lax.ppermute(x, CORE, [(0, 1), (1, 0)])]
  transfers between devices with their start and end apart: 5 -> 5, of which waited for: 3 -> 2; matrix products, arithmetic and copies ran while one was open for 0% -> 0% of each run, Pallas kernels for 12% -> 18%
where the time goes in v4:
time: 137 us
  blocking collectives  61.4 us (45%)
  Pallas kernels  37.6 us (27%)
  starting transfers between devices  18.5 us (14%)
  waiting for transfers between devices  18.2 us (13%)
    all_to_all x3, blocking collectives, exchange(): return lax.all_to_all(x, axes, 0, 0, tiled=True)  61.4 us
    all_to_all x1, waiting for transfers between devices, exchange(): return lax.all_to_all(x, axes, 0, 0, tiled=True)  14.8 us
    all_to_all x1, starting transfers between devices, exchange(): return lax.all_to_all(x, axes, 0, 0, tiled=True)  10.6 us
    pallas_call x1, Pallas kernels, inside(): near = near_call()(core, r, k, v, g, bonus, log_decay)  9.42 us
    ppermute x4, starting transfers between devices, swap(): return lax.ppermute(x, CORE, [(0, 1), (1, 0)])  7.87 us
    pallas_call x1, Pallas kernels, inside(): last_call()  7.65 us
    pallas_call x1, Pallas kernels, inside(): grads_call()  5.45 us
    pallas_call x1, Pallas kernels, inside(): smooth, *early, theirs = theirs_call()(core, x, down, r, k, v, g, up, speed)  4.67 us
  transfers between devices with their start and end apart: 5, of which 2 were waited for; matrix products, arithmetic and copies ran while one was open for 0% of the time, Pallas kernels for 18%

profile of v4, /device:TPU:1, one launch (start us, length us, event | category | flops | bytes accessed | tf_op | source)
XLA Modules:
  0.0 136.8 jit_solution(8781979606873211684)
XLA Ops:
  0.6 4.7 %shard_map.160 = (f32[128,128]{1,0:T(8,128)}, f32[128,2560]{1,0:T(8,128)}, bf16[128,2560]{1,0:T(8,128)(2,1)}, bf16[128,2560]{1,0:T(8,128)(2,1)}, f32[1280,128]{1...) custom-call(s32[1]{0:T(128)} %bitcast.core_ref.place_ref, ...), custom_call_target="tpu_custom_call" | custom-call | flops 1000000000 | bytes 1000000 | tf_op jit(solution)/shard_map/pallas_call | solution.py:537
  5.3 1.5 %collective-permute-start = (f32[1296,128]{1,0:T(8,128)S(1)}, f32[1296,128]{1,0:T(8,128)S(1)}, u32[]{:S(2)}, u32[]{:S(2)}) collective-permute-start(f32[1296,128]{1,0:T(8,128)S(1)} %get-tuple-element.59), channel_id=1, source_target_pairs={{0,2},{2,0},{1,3},{3,1},{4,6},{6,4},{5,7},{7,5},{8,10},{10,8},{9,1... | collective-permute-start | bytes 1990664 | tf_op jit(solution)/shard_map/ppermute | solution.py:523
  6.8 3.8 %shard_map.161 = (f32[128,2560]{1,0:T(8,128)}, bf16[128,2560]{1,0:T(8,128)(2,1)}, bf16[128,2560]{1,0:T(8,128)(2,1)}, f32[1280,128]{1,0:T(8,128)}, f32[2,1280,128...) custom-call(s32[1]{0:T(128)} %bitcast.core_ref.place_ref, ...), custom_call_target="tpu_custom_call", output_to_operand_aliasing={{0}: (8, {}), {1}: (9, {}), {2}: (10, {}), {3}: (11, {}), {... | custom-call | flops 1000000000 | bytes 1000000 | tf_op jit(solution)/shard_map/pallas_call | solution.py:540
  10.6 0.0 collective-permute-done.other_ref
  10.6 1.0 shard_map.162
  11.7 10.6 %all-to-all-start = ((f32[32,48,128]{2,1,0:T(8,128)}), f32[32,48,128]{2,1,0:T(8,128)S(1)}, u32[]{:S(2)}, u32[]{:S(2)}) async-start(f32[32,48,128]{2,1,0:T(8,128)} %shard_map.162), calls=%async_computation | async-start | bytes 1572864 | tf_op jit(solution)/shard_map/all_to_all | solution.py:519
  22.3 14.8 %all-to-all-done.in_ref = f32[32,48,128]{2,1,0:T(8,128)S(1)} async-done(((f32[32,48,128]{2,1,0:T(8,128)}), f32[32,48,128]{2,1,0:T(8,128)S(1)}, u32[]{:S(2)}, u32[]{:S(2)}) %all-to-all-start) | async-done | bytes 786464 | tf_op jit(solution)/shard_map/all_to_all | solution.py:519
  37.1 0.2 shard_map.163
  37.4 16.2 %all_to_all.20 = f32[32,40,128]{2,1,0:T(8,128)S(1)} all-to-all(f32[32,40,128]{2,1,0:T(8,128)S(1)} %shard_map.163), channel_id=1, replica_groups=mesh['seq_0'=4,'seq_1'=2,'seq_2'=4,'seq_3'=2,'dp'=2] {'seq_0','seq_1','s..., dimensions={0} | all-to-all | bytes 1310720 | tf_op jit(solution)/shard_map/all_to_all | solution.py:519
  53.5 0.2 shard_map.164
  53.7 3.2 %collective-permute-start.1 = (f32[1280,128]{1,0:T(8,128)S(1)}, f32[1280,128]{1,0:T(8,128)S(1)}, u32[]{:S(2)}, u32[]{:S(2)}) collective-permute-start(f32[1280,128]{1,0:T(8,128)S(1)} %get-tuple-element.61), channel_id=1, source_target_pairs={{0,2},{2,0},{1,3},{3,1},{4,6},{6,4},{5,7},{7,5},{8,10},{10,8},{9,1... | collective-permute-start | bytes 1966088 | tf_op jit(solution)/shard_map/ppermute | solution.py:523
  56.9 9.4 %shard_map.165 = (f32[128,2560]{1,0:T(8,128)}, f32[128,2560]{1,0:T(8,128)}, f32[128,2560]{1,0:T(8,128)}, f32[128,2560]{1,0:T(8,128)}, f32[128,2560]{1,0:T(8,128)}, /*index=5*/f32[20,128]{1,0:T(8,128)}) custom-call(s32[1]{0:T(128)} %bitcast.core_ref.place_ref, bf16[128,2560]{1,0:T(8,128)(2,1)} %bitcast.36, bf16[128,2560]{1,0:T(8,128)(2,1)} %bitcast.39, ...), custom_call_target="tpu_custom_call" | custom-call | flops 1000000000 | bytes 1000000 | tf_op jit(solution)/shard_map/pallas_call | solution.py:544
  66.4 3.5 %shard_map.166 = (bf16[128,1280]{1,0:T(8,128)(2,1)}, f32[10,128]{1,0:T(8,128)}) custom-call(s32[1]{0:T(128)} %bitcast.core_ref.place_ref, bf16[128,2560]{1,0:T(8,128)(2,1)} %bitcast.24, bf16[128,2560]{1,0:T(8,128)(2,1)} %bitcast.30, f32[128,2560]{1,0:T(8,128)} %get-tuple-element.53.log_ref, f32[4,2,640]{2,1,0:T(2,128)} %get-tuple-element.66.total_ref, ...), custom_call_target="tpu_custom_call" | custom-call | flops 1000000000 | bytes 1000000 | tf_op jit(solution)/shard_map/pallas_call | solution.py:550
  69.8 5.4 %shard_map.167 = (f32[32,2,48,128]{3,2,1,0:T(8,128)S(1)}, f32[32,2,48,128]{3,2,1,0:T(8,128)S(1)}, bf16[128,128]{1,0:T(8,128)(2,1)}) custom-call(s32[1]{0:T(128)} %bitcast.core_ref.place_ref, bf16[128,2560]{1,0:T(8,128)(2,1)} %bitcast.25, bf16[128,2560]{1,0:T(8,128)(2,1)} %bitcast.31, f32[128,2560]{1,0:T(8,128)} %get-tuple-element.53.log_ref, ...), custom_call_target="tpu_custom_call" | custom-call | flops 1000000000 | bytes 1000000 | tf_op jit(solution)/shard_map/pallas_call | solution.py:551
  75.3 0.1 collective-permute-start.2
  75.4 3.4 %collective-permute-done.2 = f32[32,2,48,128]{3,2,1,0:T(8,128)S(1)} collective-permute-done((f32[32,2,48,128]{3,2,1,0:T(8,128)S(1)}, f32[32,2,48,128]{3,2,1,0:T(8,128)S(1)}, u32[]{:S(2)}, u32[]{:S(2)}) %collective-permute-start.2) | collective-permute-done | bytes 1572896 | tf_op jit(solution)/shard_map/ppermute | solution.py:523
  78.8 0.2 add.12
  79.0 27.0 %all_to_all.21 = f32[64,48,128]{2,1,0:T(8,128)S(1)} all-to-all(f32[64,48,128]{2,1,0:T(8,128)S(1)} %bitcast.33), channel_id=1, replica_groups=mesh['seq_0'=4,'seq_1'=2,'seq_2'=4,'seq_3'=2,'dp'=2] {'seq_0','seq_1','s..., dimensions={0} | all-to-all | bytes 3145728 | tf_op jit(solution)/shard_map/all_to_all | solution.py:519
  106.0 0.1 reduce_sum.9
  106.1 0.1 broadcast_in_dim.34
  106.2 18.2 %all_to_all.22.mine_ref = f32[32,48,128]{2,1,0:T(8,128)S(1)} all-to-all(f32[32,48,128]{2,1,0:T(8,128)S(1)} %broadcast_in_dim.34), channel_id=1, replica_groups=mesh['seq_0'=4,'seq_1'=2,'seq_2'=4,'seq_3'=2,'dp'=2] {'seq_0','seq_1','s..., dimensions={0} | all-to-all | bytes 1572864 | tf_op jit(solution)/shard_map/all_to_all | solution.py:519
  124.5 3.0 %collective-permute-start.3 = (f32[32,48,128]{2,1,0:T(8,128)S(1)}, f32[32,48,128]{2,1,0:T(8,128)S(1)}, u32[]{:S(2)}, u32[]{:S(2)}) collective-permute-start(f32[32,48,128]{2,1,0:T(8,128)S(1)} %all_to_all.22.mine_ref), channel_id=1, source_target_pairs={{0,2},{2,0},{1,3},{3,1},{4,6},{6,4},{5,7},{7,5},{8,10},{10,8},{9,1... | collective-permute-start | bytes 2359304 | tf_op jit(solution)/shard_map/ppermute | solution.py:523
  127.5 7.6 %shard_map.168 = (bf16[128,2560]{1,0:T(8,128)(2,1)}, bf16[128,2560]{1,0:T(8,128)(2,1)}, bf16[128,2560]{1,0:T(8,128)(2,1)}, bf16[128,2560]{1,0:T(8,128)(2,1)}, bf16[128,2560]{1,0:T(8,128)(2,1)}) custom-call(s32[1]{0:T(128)} %bitcast.core_ref.place_ref, bf16[128,2560]{1,0:T(8,128)(2,1)} %bitcast.26, bf16[128,2560]{1,0:T(8,128)(2,1)} %bitcast.32, ...), custom_call_target="tpu_custom_call" | custom-call | flops 1000000000 | bytes 1000000 | tf_op jit(solution)/shard_map/pallas_call | solution.py:556
  135.1 1.7 %final.1 = (f32[32,40,128]{2,1,0:T(8,128)}, f32[32,40,128]{2,1,0:T(8,128)}, f32[10,128]{1,0:T(8,128)}, f32[10,128]{1,0:T(8,128)}) custom-call(s32[1]{0:T(128)} %bitcast.core_ref.place_ref, f32[32,48,128]{2,1,0:T(8,128)S(1)} %all_to_all.22.mine_ref, f32[32,48,128]{2,1,0:T(8,128)S(1)} %collective-permute-done.3.other_ref), custom_call_target="tpu_custom_call" | custom-call | tf_op jit(solution)/shard_map/final/pallas_call | solution.py:560
  (2 shorter events, 0.0 us)
Async XLA Ops:
  5.3 5.3 %collective-permute-start = (f32[1296,128]{1,0:T(8,128)S(1)}, f32[1296,128]{1,0:T(8,128)S(1)}, u32[]{:S(2)}, u32[]{:S(2)}) collective-permute-start(f32[1296,128]{1,0:T(8,128)S(1)} %get-tuple-element.59), channel_id=1, source_target_pairs={{0,2},{2,0},{1,3},{3,1},{4,6},{6,4},{5,7},{7,5},{8,10},{10,8},{9,1... | collective-permute-start | bytes 1990664 | tf_op jit(solution)/shard_map/ppermute | solution.py:523
  11.7 25.5 %all-to-all-start = ((f32[32,48,128]{2,1,0:T(8,128)}), f32[32,48,128]{2,1,0:T(8,128)S(1)}, u32[]{:S(2)}, u32[]{:S(2)}) async-start(f32[32,48,128]{2,1,0:T(8,128)} %shard_map.162), calls=%async_computation | async-start | bytes 1572864 | tf_op jit(solution)/shard_map/all_to_all | solution.py:519
  53.7 16.1 %collective-permute-start.1 = (f32[1280,128]{1,0:T(8,128)S(1)}, f32[1280,128]{1,0:T(8,128)S(1)}, u32[]{:S(2)}, u32[]{:S(2)}) collective-permute-start(f32[1280,128]{1,0:T(8,128)S(1)} %get-tuple-element.61), channel_id=1, source_target_pairs={{0,2},{2,0},{1,3},{3,1},{4,6},{6,4},{5,7},{7,5},{8,10},{10,8},{9,1... | collective-permute-start | bytes 1966088 | tf_op jit(solution)/shard_map/ppermute | solution.py:523
  75.3 3.5 %collective-permute-start.2 = (f32[32,2,48,128]{3,2,1,0:T(8,128)S(1)}, f32[32,2,48,128]{3,2,1,0:T(8,128)S(1)}, u32[]{:S(2)}, u32[]{:S(2)}) collective-permute-start(f32[32,2,48,128]{3,2,1,0:T(8,128)S(1)} %get-tuple-element.78), channel_id=1, source_target_pairs={{0,2},{2,0},{1,3},{3,1},{4,6},{6,4},{5,7},{7,5},{8,10},{10,8},{9,1... | collective-permute-start | bytes 4718600 | tf_op jit(solution)/shard_map/ppermute | solution.py:523
  124.5 10.7 %collective-permute-start.3 = (f32[32,48,128]{2,1,0:T(8,128)S(1)}, f32[32,48,128]{2,1,0:T(8,128)S(1)}, u32[]{:S(2)}, u32[]{:S(2)}) collective-permute-start(f32[32,48,128]{2,1,0:T(8,128)S(1)} %all_to_all.22.mine_ref), channel_id=1, source_target_pairs={{0,2},{2,0},{1,3},{3,1},{4,6},{6,4},{5,7},{7,5},{8,10},{10,8},{9,1... | collective-permute-start | bytes 2359304 | tf_op jit(solution)/shard_map/ppermute | solution.py:523

commit v5 on v4

--- a/solution.py
+++ b/solution.py
@@ -17,8 +17,9 @@
 CORE = SEQ[3]
 HALF = 10
 HALF_ROWS = 640
-CHUNK = 5
-STEPS = 4
+CHUNK = 10
+HALF_STEPS = HALF // CHUNK
+STEPS = 2 * HALF_STEPS
 VMEM_LIMIT = 24
 FREE = ((32, 2, 48, 128), (1296, 128))
 F32 = jnp.float32
@@ -335,12 +336,12 @@
         rest_ref[core, 1 - core, step * CHUNK + i, 0:1, :] = sums[:, i * 128 : i * 128 + 128]
     gate_ref[...] += mm(slope_half, up_ref[rows_of(1 - core, step), :], NN)
 
-    @pl.when(step == 1)
+    @pl.when(step == HALF_STEPS - 1)
     def _():
         project_grad = (gate_ref[...] * (1.0 - smooth * smooth)).astype(BF16)
         project_ref[...] = project_grad
-        for c in range(4):
-            stage_ref[core, c // 2, c % 2 * width : (c % 2 + 1) * width, :] = mm(x_ref[:, c * width : (c + 1) * width], project_grad, TN)
+        for c in range(2):
+            stage_ref[core, c] = mm(x_ref[:, c * SPAN // 2 : (c + 1) * SPAN // 2], project_grad, TN)
         copies = []
         for j, ref in enumerate((keep_ref, give_ref)):
             for half in range(2):
@@ -367,8 +368,8 @@
         inc = incs[:, lanes]
         decay_0 = jnp.exp(inc[BLOCK - 1 : BLOCK])
         decay_1 = jnp.exp(inc[TOKENS - 1 : TOKENS])
-        row = pl.multiple_of((step % 2 * CHUNK + i) * LANE_TOTAL, LANE_TOTAL)
-        pair = [jnp.where(step // 2 == core, mine_ref[at, :], other_ref[at, :])
+        row = pl.multiple_of((step % HALF_STEPS * CHUNK + i) * LANE_TOTAL, LANE_TOTAL)
+        pair = [jnp.where(step // HALF_STEPS == core, mine_ref[at, :], other_ref[at, :])
                 for at in (pl.ds(row, LANE_TOTAL), pl.ds(HALF_ROWS + row, LANE_TOTAL))]
         states = start_and_end(i, *pair, own_ref, pull_ref, decay_0, decay_1)
         s_0, s_1, e_0, e_1 = (corners(z, low_lanes) for z in states)
@@ -468,24 +469,24 @@
 
 
 def mine_half(s, core):
-    return core[0] * 2 + s
+    return core[0] * HALF_STEPS + s
 
 
 def their_half(s, core):
-    return (1 - core[0]) * 2 + s
+    return (1 - core[0]) * HALF_STEPS + s
 
 
 def theirs_call():
     return in_steps(
         theirs_kernel, [whole(TOKENS, SPAN), whole(SPAN, 128), WIDE, WIDE, WIDE, WIDE, WEIGHT, ROWS],
-        [(SQUARE, F32)] + EARLY + [(PART, F32)], at=their_half, steps=2,
+        [(SQUARE, F32)] + EARLY + [(PART, F32)], at=their_half, steps=HALF_STEPS,
     )
 
 
 def mine_call():
     return in_steps(
         mine_kernel, [SQUARE, WIDE, WIDE, WIDE, WIDE, WEIGHT, ROWS] + [kept(*z[0][0]) for z in EARLY],
-        EARLY + [(PART, F32)], at=mine_half, steps=2, aliases={8 + j: j for j in range(len(EARLY))},
+        EARLY + [(PART, F32)], at=mine_half, steps=HALF_STEPS, aliases={8 + j: j for j in range(len(EARLY))},
     )
 
 
@@ -494,7 +495,7 @@
 
 
 def slope_call():
-    return in_steps(slope_kernel, SLOPE, [(HALF_WIDE, BF16), (whole(HALF, 128), F32)], at=mine_half, steps=2)
+    return in_steps(slope_kernel, SLOPE, [(HALF_WIDE, BF16), (whole(HALF, 128), F32)], at=mine_half, steps=HALF_STEPS)
 
 
 def grads_call():
@@ -503,7 +504,7 @@
         [(kept(32, 2, 48, 128), F32), (kept(32, 2, 48, 128), F32), (SQUARE, BF16)],
         (pltpu.VMEM((2, 2, SPAN // 2, 128), F32), pltpu.VMEM((2, 2, HALF, 8, 128), F32), pltpu.VMEM((TOKENS, 128), F32),
          pltpu.SemaphoreType.DMA((2, 2, 2))),
-        at=their_half, steps=2,
+        at=their_half, steps=HALF_STEPS,
     )
 
 

time: 137 us -> 135 us (0.985)
  Pallas kernels: 37.6 us -> 34.9 us
  transfers between devices with their start and end apart: 5 -> 5, of which waited for: 2 -> 2; matrix products, arithmetic and copies ran while one was open for 0% -> 0% of each run, Pallas kernels for 18% -> 17%
where the time goes in v5:
time: 135 us; the launch traced here: 134 us
  blocking collectives  61.5 us (46%)
  Pallas kernels  34.9 us (26%)
  starting transfers between devices  18.4 us (14%)
  waiting for transfers between devices  18.2 us (13%)
    all_to_all x3, blocking collectives, exchange(): return lax.all_to_all(x, axes, 0, 0, tiled=True)  61.5 us
    all_to_all x1, waiting for transfers between devices, exchange(): return lax.all_to_all(x, axes, 0, 0, tiled=True)  14.8 us
    all_to_all x1, starting transfers between devices, exchange(): return lax.all_to_all(x, axes, 0, 0, tiled=True)  10.6 us
    pallas_call x1, Pallas kernels, inside(): near = near_call()(core, r, k, v, g, bonus, log_decay)  9.44 us
    ppermute x4, starting transfers between devices, swap(): return lax.ppermute(x, CORE, [(0, 1), (1, 0)])  7.77 us
    pallas_call x1, Pallas kernels, inside(): last_call()  6.73 us
    pallas_call x1, Pallas kernels, inside(): grads_call()  4.87 us
    pallas_call x1, Pallas kernels, inside(): smooth, *early, theirs = theirs_call()(core, x, down, r, k, v, g, up, speed)  3.96 us
  transfers between devices with their start and end apart: 5, of which 2 were waited for; matrix products, arithmetic and copies ran while one was open for 0% of the time, Pallas kernels for 17%

profile of v5, /device:TPU:1, one launch (start us, length us, event | category | flops | bytes accessed | tf_op | source)
XLA Modules:
  0.0 134.1 jit_solution(3332308883380974175)
XLA Ops:
  0.6 4.0 %shard_map.160 = (f32[128,128]{1,0:T(8,128)}, f32[128,2560]{1,0:T(8,128)}, bf16[128,2560]{1,0:T(8,128)(2,1)}, bf16[128,2560]{1,0:T(8,128)(2,1)}, f32[1280,128]{1...) custom-call(s32[1]{0:T(128)} %bitcast.core_ref.place_ref, ...), custom_call_target="tpu_custom_call" | custom-call | flops 1000000000 | bytes 1000000 | tf_op jit(solution)/shard_map/pallas_call | solution.py:538
  4.6 1.4 %collective-permute-start = (f32[1296,128]{1,0:T(8,128)S(1)}, f32[1296,128]{1,0:T(8,128)S(1)}, u32[]{:S(2)}, u32[]{:S(2)}) collective-permute-start(f32[1296,128]{1,0:T(8,128)S(1)} %get-tuple-element.59), channel_id=1, source_target_pairs={{0,2},{2,0},{1,3},{3,1},{4,6},{6,4},{5,7},{7,5},{8,10},{10,8},{9,1... | collective-permute-start | bytes 1990664 | tf_op jit(solution)/shard_map/ppermute | solution.py:524
  6.0 3.4 %shard_map.161 = (f32[128,2560]{1,0:T(8,128)}, bf16[128,2560]{1,0:T(8,128)(2,1)}, bf16[128,2560]{1,0:T(8,128)(2,1)}, f32[1280,128]{1,0:T(8,128)}, f32[2,1280,128...) custom-call(s32[1]{0:T(128)} %bitcast.core_ref.place_ref, ...), custom_call_target="tpu_custom_call", output_to_operand_aliasing={{0}: (8, {}), {1}: (9, {}), {2}: (10, {}), {3}: (11, {}), {... | custom-call | flops 1000000000 | bytes 1000000 | tf_op jit(solution)/shard_map/pallas_call | solution.py:541
  9.4 0.0 collective-permute-done.other_ref
  9.4 1.0 shard_map.162
  10.4 10.6 %all-to-all-start = ((f32[32,48,128]{2,1,0:T(8,128)}), f32[32,48,128]{2,1,0:T(8,128)S(1)}, u32[]{:S(2)}, u32[]{:S(2)}) async-start(f32[32,48,128]{2,1,0:T(8,128)} %shard_map.162), calls=%async_computation | async-start | bytes 1572864 | tf_op jit(solution)/shard_map/all_to_all | solution.py:520
  21.0 14.8 %all-to-all-done.in_ref = f32[32,48,128]{2,1,0:T(8,128)S(1)} async-done(((f32[32,48,128]{2,1,0:T(8,128)}), f32[32,48,128]{2,1,0:T(8,128)S(1)}, u32[]{:S(2)}, u32[]{:S(2)}) %all-to-all-start) | async-done | bytes 786464 | tf_op jit(solution)/shard_map/all_to_all | solution.py:520
  35.9 0.2 shard_map.163
  36.1 16.2 %all_to_all.20 = f32[32,40,128]{2,1,0:T(8,128)S(1)} all-to-all(f32[32,40,128]{2,1,0:T(8,128)S(1)} %shard_map.163), channel_id=1, replica_groups=mesh['seq_0'=4,'seq_1'=2,'seq_2'=4,'seq_3'=2,'dp'=2] {'seq_0','seq_1','s..., dimensions={0} | all-to-all | bytes 1310720 | tf_op jit(solution)/shard_map/all_to_all | solution.py:520
  52.3 0.2 shard_map.164
  52.5 3.2 %collective-permute-start.1 = (f32[1280,128]{1,0:T(8,128)S(1)}, f32[1280,128]{1,0:T(8,128)S(1)}, u32[]{:S(2)}, u32[]{:S(2)}) collective-permute-start(f32[1280,128]{1,0:T(8,128)S(1)} %get-tuple-element.61), channel_id=1, source_target_pairs={{0,2},{2,0},{1,3},{3,1},{4,6},{6,4},{5,7},{7,5},{8,10},{10,8},{9,1... | collective-permute-start | bytes 1966088 | tf_op jit(solution)/shard_map/ppermute | solution.py:524
  55.7 9.4 %shard_map.165 = (f32[128,2560]{1,0:T(8,128)}, f32[128,2560]{1,0:T(8,128)}, f32[128,2560]{1,0:T(8,128)}, f32[128,2560]{1,0:T(8,128)}, f32[128,2560]{1,0:T(8,128)}, /*index=5*/f32[20,128]{1,0:T(8,128)}) custom-call(s32[1]{0:T(128)} %bitcast.core_ref.place_ref, bf16[128,2560]{1,0:T(8,128)(2,1)} %bitcast.36, bf16[128,2560]{1,0:T(8,128)(2,1)} %bitcast.39, ...), custom_call_target="tpu_custom_call" | custom-call | flops 1000000000 | bytes 1000000 | tf_op jit(solution)/shard_map/pallas_call | solution.py:545
  65.2 3.5 %shard_map.166 = (bf16[128,1280]{1,0:T(8,128)(2,1)}, f32[10,128]{1,0:T(8,128)}) custom-call(s32[1]{0:T(128)} %bitcast.core_ref.place_ref, bf16[128,2560]{1,0:T(8,128)(2,1)} %bitcast.24, bf16[128,2560]{1,0:T(8,128)(2,1)} %bitcast.30, f32[128,2560]{1,0:T(8,128)} %get-tuple-element.53.log_ref, f32[2,2,1280]{2,1,0:T(2,128)} %get-tuple-element.66.total_ref, ...), custom_call_target="tpu_custom_call" | custom-call | flops 1000000000 | bytes 1000000 | tf_op jit(solution)/shard_map/pallas_call | solution.py:551
  68.6 4.9 %shard_map.167 = (f32[32,2,48,128]{3,2,1,0:T(8,128)S(1)}, f32[32,2,48,128]{3,2,1,0:T(8,128)S(1)}, bf16[128,128]{1,0:T(8,128)(2,1)}) custom-call(s32[1]{0:T(128)} %bitcast.core_ref.place_ref, bf16[128,2560]{1,0:T(8,128)(2,1)} %bitcast.25, bf16[128,2560]{1,0:T(8,128)(2,1)} %bitcast.31, f32[128,2560]{1,0:T(8,128)} %get-tuple-element.53.log_ref, ...), custom_call_target="tpu_custom_call" | custom-call | flops 1000000000 | bytes 1000000 | tf_op jit(solution)/shard_map/pallas_call | solution.py:552
  73.5 0.1 collective-permute-start.2
  73.6 3.4 %collective-permute-done.2 = f32[32,2,48,128]{3,2,1,0:T(8,128)S(1)} collective-permute-done((f32[32,2,48,128]{3,2,1,0:T(8,128)S(1)}, f32[32,2,48,128]{3,2,1,0:T(8,128)S(1)}, u32[]{:S(2)}, u32[]{:S(2)}) %collective-permute-start.2) | collective-permute-done | bytes 1572896 | tf_op jit(solution)/shard_map/ppermute | solution.py:524
  77.0 0.2 add.12
  77.2 27.0 %all_to_all.21 = f32[64,48,128]{2,1,0:T(8,128)S(1)} all-to-all(f32[64,48,128]{2,1,0:T(8,128)S(1)} %bitcast.33), channel_id=1, replica_groups=mesh['seq_0'=4,'seq_1'=2,'seq_2'=4,'seq_3'=2,'dp'=2] {'seq_0','seq_1','s..., dimensions={0} | all-to-all | bytes 3145728 | tf_op jit(solution)/shard_map/all_to_all | solution.py:520
  104.2 0.1 reduce_sum.9
  104.4 0.1 broadcast_in_dim.34
  104.4 18.2 %all_to_all.22.mine_ref = f32[32,48,128]{2,1,0:T(8,128)S(1)} all-to-all(f32[32,48,128]{2,1,0:T(8,128)S(1)} %broadcast_in_dim.34), channel_id=1, replica_groups=mesh['seq_0'=4,'seq_1'=2,'seq_2'=4,'seq_3'=2,'dp'=2] {'seq_0','seq_1','s..., dimensions={0} | all-to-all | bytes 1572864 | tf_op jit(solution)/shard_map/all_to_all | solution.py:520
  122.7 3.0 %collective-permute-start.3 = (f32[32,48,128]{2,1,0:T(8,128)S(1)}, f32[32,48,128]{2,1,0:T(8,128)S(1)}, u32[]{:S(2)}, u32[]{:S(2)}) collective-permute-start(f32[32,48,128]{2,1,0:T(8,128)S(1)} %all_to_all.22.mine_ref), channel_id=1, source_target_pairs={{0,2},{2,0},{1,3},{3,1},{4,6},{6,4},{5,7},{7,5},{8,10},{10,8},{9,1... | collective-permute-start | bytes 2359304 | tf_op jit(solution)/shard_map/ppermute | solution.py:524
  125.7 6.7 %shard_map.168 = (bf16[128,2560]{1,0:T(8,128)(2,1)}, bf16[128,2560]{1,0:T(8,128)(2,1)}, bf16[128,2560]{1,0:T(8,128)(2,1)}, bf16[128,2560]{1,0:T(8,128)(2,1)}, bf16[128,2560]{1,0:T(8,128)(2,1)}) custom-call(s32[1]{0:T(128)} %bitcast.core_ref.place_ref, bf16[128,2560]{1,0:T(8,128)(2,1)} %bitcast.26, bf16[128,2560]{1,0:T(8,128)(2,1)} %bitcast.32, ...), custom_call_target="tpu_custom_call" | custom-call | flops 1000000000 | bytes 1000000 | tf_op jit(solution)/shard_map/pallas_call | solution.py:557
  132.5 1.7 %final.1 = (f32[32,40,128]{2,1,0:T(8,128)}, f32[32,40,128]{2,1,0:T(8,128)}, f32[10,128]{1,0:T(8,128)}, f32[10,128]{1,0:T(8,128)}) custom-call(s32[1]{0:T(128)} %bitcast.core_ref.place_ref, f32[32,48,128]{2,1,0:T(8,128)S(1)} %all_to_all.22.mine_ref, f32[32,48,128]{2,1,0:T(8,128)S(1)} %collective-permute-done.3.other_ref), custom_call_target="tpu_custom_call" | custom-call | tf_op jit(solution)/shard_map/final/pallas_call | solution.py:561
  (2 shorter events, 0.0 us)
Async XLA Ops:
  4.6 4.8 %collective-permute-start = (f32[1296,128]{1,0:T(8,128)S(1)}, f32[1296,128]{1,0:T(8,128)S(1)}, u32[]{:S(2)}, u32[]{:S(2)}) collective-permute-start(f32[1296,128]{1,0:T(8,128)S(1)} %get-tuple-element.59), channel_id=1, source_target_pairs={{0,2},{2,0},{1,3},{3,1},{4,6},{6,4},{5,7},{7,5},{8,10},{10,8},{9,1... | collective-permute-start | bytes 1990664 | tf_op jit(solution)/shard_map/ppermute | solution.py:524
  10.4 25.5 %all-to-all-start = ((f32[32,48,128]{2,1,0:T(8,128)}), f32[32,48,128]{2,1,0:T(8,128)S(1)}, u32[]{:S(2)}, u32[]{:S(2)}) async-start(f32[32,48,128]{2,1,0:T(8,128)} %shard_map.162), calls=%async_computation | async-start | bytes 1572864 | tf_op jit(solution)/shard_map/all_to_all | solution.py:520
  52.5 16.1 %collective-permute-start.1 = (f32[1280,128]{1,0:T(8,128)S(1)}, f32[1280,128]{1,0:T(8,128)S(1)}, u32[]{:S(2)}, u32[]{:S(2)}) collective-permute-start(f32[1280,128]{1,0:T(8,128)S(1)} %get-tuple-element.61), channel_id=1, source_target_pairs={{0,2},{2,0},{1,3},{3,1},{4,6},{6,4},{5,7},{7,5},{8,10},{10,8},{9,1... | collective-permute-start | bytes 1966088 | tf_op jit(solution)/shard_map/ppermute | solution.py:524
  73.5 3.5 %collective-permute-start.2 = (f32[32,2,48,128]{3,2,1,0:T(8,128)S(1)}, f32[32,2,48,128]{3,2,1,0:T(8,128)S(1)}, u32[]{:S(2)}, u32[]{:S(2)}) collective-permute-start(f32[32,2,48,128]{3,2,1,0:T(8,128)S(1)} %get-tuple-element.78), channel_id=1, source_target_pairs={{0,2},{2,0},{1,3},{3,1},{4,6},{6,4},{5,7},{7,5},{8,10},{10,8},{9,1... | collective-permute-start | bytes 4718600 | tf_op jit(solution)/shard_map/ppermute | solution.py:524
  122.7 9.8 %collective-permute-start.3 = (f32[32,48,128]{2,1,0:T(8,128)S(1)}, f32[32,48,128]{2,1,0:T(8,128)S(1)}, u32[]{:S(2)}, u32[]{:S(2)}) collective-permute-start(f32[32,48,128]{2,1,0:T(8,128)S(1)} %all_to_all.22.mine_ref), channel_id=1, source_target_pairs={{0,2},{2,0},{1,3},{3,1},{4,6},{6,4},{5,7},{7,5},{8,10},{10,8},{9,1... | collective-permute-start | bytes 2359304 | tf_op jit(solution)/shard_map/ppermute | solution.py:524

commit v6 on v5

--- a/solution.py
+++ b/solution.py
@@ -413,6 +413,14 @@
     )
 
 
+def fold_kernel(in_ref, out_ref):
+    total = in_ref[0]
+    for e in range(1, in_ref.shape[0]):
+        total = total + in_ref[e]
+    for e in range(out_ref.shape[0]):
+        out_ref[e] = total
+
+
 def call(kernel, outs, count=0):
     more = {}
     if count:
@@ -556,8 +564,8 @@
     pieces = exchange(grads, CHIPS + ("dp",))
     mixed, gr, gk, gv, gx = last_call()(core, v, g, down, log_decay, reached, faded, own, pull, keep, got,
                                         near_mixed, near_gr, near_gk, near_gv, project_grad)
-    summed = jnp.sum(pieces, axis=0)
-    matrix = exchange(jnp.broadcast_to(summed[None], (32, 48, 128)), CHIPS)
+    (summed,) = call(fold_kernel, [((32, 48, 128), F32)])(pieces)
+    matrix = exchange(summed, CHIPS)
     a, b, a_row, b_row = final_call()(core, matrix, swap(matrix))
     return (mixed[None], gr[None], gk[None], gv[None], gx[None],
             a.reshape(SPAN // 2, 128), b.reshape(SPAN // 2, 128), a_row.reshape(SPAN // 2), b_row.reshape(SPAN // 2))

time: 135 us -> 134 us (level)
  no operation moved by 1% of the time
where the time goes in v6:
time: 134 us
  blocking collectives  61.4 us (46%)
  Pallas kernels  35 us (26%)
  starting transfers between devices  18.4 us (14%)
  waiting for transfers between devices  18.2 us (14%)
    all_to_all x3, blocking collectives, exchange(): return lax.all_to_all(x, axes, 0, 0, tiled=True)  61.4 us
    all_to_all x1, waiting for transfers between devices, exchange(): return lax.all_to_all(x, axes, 0, 0, tiled=True)  14.8 us
    all_to_all x1, starting transfers between devices, exchange(): return lax.all_to_all(x, axes, 0, 0, tiled=True)  10.6 us
    pallas_call x1, Pallas kernels, inside(): near = near_call()(core, r, k, v, g, bonus, log_decay)  9.32 us
    ppermute x4, starting transfers between devices, swap(): return lax.ppermute(x, CORE, [(0, 1), (1, 0)])  7.78 us
    pallas_call x1, Pallas kernels, inside(): last_call()  6.76 us
    pallas_call x1, Pallas kernels, inside(): grads_call()  4.88 us
    pallas_call x1, Pallas kernels, inside(): smooth, *early, theirs = theirs_call()(core, x, down, r, k, v, g, up, speed)  3.95 us
  transfers between devices with their start and end apart: 5, of which 2 were waited for; matrix products, arithmetic and copies ran while one was open for 0% of the time, Pallas kernels for 17%

profile of v6, /device:TPU:1, one launch (start us, length us, event | category | flops | bytes accessed | tf_op | source)
XLA Modules:
  0.0 134.0 jit_solution(5369593729390499780)
XLA Ops:
  0.6 3.9 %shard_map.160 = (f32[128,128]{1,0:T(8,128)}, f32[128,2560]{1,0:T(8,128)}, bf16[128,2560]{1,0:T(8,128)(2,1)}, bf16[128,2560]{1,0:T(8,128)(2,1)}, f32[1280,128]{1...) custom-call(s32[1]{0:T(128)} %bitcast.core_ref.place_ref, ...), custom_call_target="tpu_custom_call" | custom-call | flops 1000000000 | bytes 1000000 | tf_op jit(solution)/shard_map/pallas_call | solution.py:546
  4.6 1.4 %collective-permute-start = (f32[1296,128]{1,0:T(8,128)S(1)}, f32[1296,128]{1,0:T(8,128)S(1)}, u32[]{:S(2)}, u32[]{:S(2)}) collective-permute-start(f32[1296,128]{1,0:T(8,128)S(1)} %get-tuple-element.59), channel_id=1, source_target_pairs={{0,2},{2,0},{1,3},{3,1},{4,6},{6,4},{5,7},{7,5},{8,10},{10,8},{9,1... | collective-permute-start | bytes 1990664 | tf_op jit(solution)/shard_map/ppermute | solution.py:532
  6.0 3.3 %shard_map.161 = (f32[128,2560]{1,0:T(8,128)}, bf16[128,2560]{1,0:T(8,128)(2,1)}, bf16[128,2560]{1,0:T(8,128)(2,1)}, f32[1280,128]{1,0:T(8,128)}, f32[2,1280,128...) custom-call(s32[1]{0:T(128)} %bitcast.core_ref.place_ref, ...), custom_call_target="tpu_custom_call", output_to_operand_aliasing={{0}: (8, {}), {1}: (9, {}), {2}: (10, {}), {3}: (11, {}), {... | custom-call | flops 1000000000 | bytes 1000000 | tf_op jit(solution)/shard_map/pallas_call | solution.py:549
  9.4 0.0 collective-permute-done.other_ref
  9.4 1.0 shard_map.162
  10.4 10.6 %all-to-all-start = ((f32[32,48,128]{2,1,0:T(8,128)}), f32[32,48,128]{2,1,0:T(8,128)S(1)}, u32[]{:S(2)}, u32[]{:S(2)}) async-start(f32[32,48,128]{2,1,0:T(8,128)} %shard_map.162), calls=%async_computation | async-start | bytes 1572864 | tf_op jit(solution)/shard_map/all_to_all | solution.py:528
  21.0 14.8 %all-to-all-done.in_ref = f32[32,48,128]{2,1,0:T(8,128)S(1)} async-done(((f32[32,48,128]{2,1,0:T(8,128)}), f32[32,48,128]{2,1,0:T(8,128)S(1)}, u32[]{:S(2)}, u32[]{:S(2)}) %all-to-all-start) | async-done | bytes 786464 | tf_op jit(solution)/shard_map/all_to_all | solution.py:528
  35.9 0.2 shard_map.163
  36.1 16.2 %all_to_all.20 = f32[32,40,128]{2,1,0:T(8,128)S(1)} all-to-all(f32[32,40,128]{2,1,0:T(8,128)S(1)} %shard_map.163), channel_id=1, replica_groups=mesh['seq_0'=4,'seq_1'=2,'seq_2'=4,'seq_3'=2,'dp'=2] {'seq_0','seq_1','s..., dimensions={0} | all-to-all | bytes 1310720 | tf_op jit(solution)/shard_map/all_to_all | solution.py:528
  52.3 0.2 shard_map.164
  52.5 3.2 %collective-permute-start.1 = (f32[1280,128]{1,0:T(8,128)S(1)}, f32[1280,128]{1,0:T(8,128)S(1)}, u32[]{:S(2)}, u32[]{:S(2)}) collective-permute-start(f32[1280,128]{1,0:T(8,128)S(1)} %get-tuple-element.61), channel_id=1, source_target_pairs={{0,2},{2,0},{1,3},{3,1},{4,6},{6,4},{5,7},{7,5},{8,10},{10,8},{9,1... | collective-permute-start | bytes 1966088 | tf_op jit(solution)/shard_map/ppermute | solution.py:532
  55.7 9.3 %shard_map.165 = (f32[128,2560]{1,0:T(8,128)}, f32[128,2560]{1,0:T(8,128)}, f32[128,2560]{1,0:T(8,128)}, f32[128,2560]{1,0:T(8,128)}, f32[128,2560]{1,0:T(8,128)}, /*index=5*/f32[20,128]{1,0:T(8,128)}) custom-call(s32[1]{0:T(128)} %bitcast.core_ref.place_ref, bf16[128,2560]{1,0:T(8,128)(2,1)} %bitcast.36, bf16[128,2560]{1,0:T(8,128)(2,1)} %bitcast.39, ...), custom_call_target="tpu_custom_call" | custom-call | flops 1000000000 | bytes 1000000 | tf_op jit(solution)/shard_map/pallas_call | solution.py:553
  65.0 3.5 %shard_map.166 = (bf16[128,1280]{1,0:T(8,128)(2,1)}, f32[10,128]{1,0:T(8,128)}) custom-call(s32[1]{0:T(128)} %bitcast.core_ref.place_ref, bf16[128,2560]{1,0:T(8,128)(2,1)} %bitcast.24, bf16[128,2560]{1,0:T(8,128)(2,1)} %bitcast.30, f32[128,2560]{1,0:T(8,128)} %get-tuple-element.53.log_ref, f32[2,2,1280]{2,1,0:T(2,128)} %get-tuple-element.66.total_ref, ...), custom_call_target="tpu_custom_call" | custom-call | flops 1000000000 | bytes 1000000 | tf_op jit(solution)/shard_map/pallas_call | solution.py:559
  68.5 4.9 %shard_map.167 = (f32[32,2,48,128]{3,2,1,0:T(8,128)S(1)}, f32[32,2,48,128]{3,2,1,0:T(8,128)S(1)}, bf16[128,128]{1,0:T(8,128)(2,1)}) custom-call(s32[1]{0:T(128)} %bitcast.core_ref.place_ref, bf16[128,2560]{1,0:T(8,128)(2,1)} %bitcast.25, bf16[128,2560]{1,0:T(8,128)(2,1)} %bitcast.31, f32[128,2560]{1,0:T(8,128)} %get-tuple-element.53.log_ref, ...), custom_call_target="tpu_custom_call" | custom-call | flops 1000000000 | bytes 1000000 | tf_op jit(solution)/shard_map/pallas_call | solution.py:560
  73.4 0.1 collective-permute-start.2
  73.5 3.4 %collective-permute-done.2 = f32[32,2,48,128]{3,2,1,0:T(8,128)S(1)} collective-permute-done((f32[32,2,48,128]{3,2,1,0:T(8,128)S(1)}, f32[32,2,48,128]{3,2,1,0:T(8,128)S(1)}, u32[]{:S(2)}, u32[]{:S(2)}) %collective-permute-start.2) | collective-permute-done | bytes 1572896 | tf_op jit(solution)/shard_map/ppermute | solution.py:532
  76.9 0.2 add.12
  77.1 27.0 %all_to_all.21.in_ref = f32[64,48,128]{2,1,0:T(8,128)S(1)} all-to-all(f32[64,48,128]{2,1,0:T(8,128)S(1)} %bitcast.33), channel_id=1, replica_groups=mesh['seq_0'=4,'seq_1'=2,'seq_2'=4,'seq_3'=2,'dp'=2] {'seq_0','seq_1','s..., dimensions={0} | all-to-all | bytes 3145728 | tf_op jit(solution)/shard_map/all_to_all | solution.py:528
  104.1 0.1 shard_map.169
  104.3 18.2 %all_to_all.22.mine_ref = f32[32,48,128]{2,1,0:T(8,128)S(1)} all-to-all(f32[32,48,128]{2,1,0:T(8,128)S(1)} %shard_map.169), channel_id=1, replica_groups=mesh['seq_0'=4,'seq_1'=2,'seq_2'=4,'seq_3'=2,'dp'=2] {'seq_0','seq_1','s..., dimensions={0} | all-to-all | bytes 1572864 | tf_op jit(solution)/shard_map/all_to_all | solution.py:528
  122.5 3.0 %collective-permute-start.3 = (f32[32,48,128]{2,1,0:T(8,128)S(1)}, f32[32,48,128]{2,1,0:T(8,128)S(1)}, u32[]{:S(2)}, u32[]{:S(2)}) collective-permute-start(f32[32,48,128]{2,1,0:T(8,128)S(1)} %all_to_all.22.mine_ref), channel_id=1, source_target_pairs={{0,2},{2,0},{1,3},{3,1},{4,6},{6,4},{5,7},{7,5},{8,10},{10,8},{9,1... | collective-permute-start | bytes 2359304 | tf_op jit(solution)/shard_map/ppermute | solution.py:532
  125.6 6.8 %shard_map.168 = (bf16[128,2560]{1,0:T(8,128)(2,1)}, bf16[128,2560]{1,0:T(8,128)(2,1)}, bf16[128,2560]{1,0:T(8,128)(2,1)}, bf16[128,2560]{1,0:T(8,128)(2,1)}, bf16[128,2560]{1,0:T(8,128)(2,1)}) custom-call(s32[1]{0:T(128)} %bitcast.core_ref.place_ref, bf16[128,2560]{1,0:T(8,128)(2,1)} %bitcast.26, bf16[128,2560]{1,0:T(8,128)(2,1)} %bitcast.32, ...), custom_call_target="tpu_custom_call" | custom-call | flops 1000000000 | bytes 1000000 | tf_op jit(solution)/shard_map/pallas_call | solution.py:565
  132.3 0.0 collective-permute-done.3.other_ref
  132.3 1.7 %final.1 = (f32[32,40,128]{2,1,0:T(8,128)}, f32[32,40,128]{2,1,0:T(8,128)}, f32[10,128]{1,0:T(8,128)}, f32[10,128]{1,0:T(8,128)}) custom-call(s32[1]{0:T(128)} %bitcast.core_ref.place_ref, f32[32,48,128]{2,1,0:T(8,128)S(1)} %all_to_all.22.mine_ref, f32[32,48,128]{2,1,0:T(8,128)S(1)} %collective-permute-done.3.other_ref), custom_call_target="tpu_custom_call" | custom-call | tf_op jit(solution)/shard_map/final/pallas_call | solution.py:569
  (1 shorter events, 0.0 us)
Async XLA Ops:
  4.6 4.8 %collective-permute-start = (f32[1296,128]{1,0:T(8,128)S(1)}, f32[1296,128]{1,0:T(8,128)S(1)}, u32[]{:S(2)}, u32[]{:S(2)}) collective-permute-start(f32[1296,128]{1,0:T(8,128)S(1)} %get-tuple-element.59), channel_id=1, source_target_pairs={{0,2},{2,0},{1,3},{3,1},{4,6},{6,4},{5,7},{7,5},{8,10},{10,8},{9,1... | collective-permute-start | bytes 1990664 | tf_op jit(solution)/shard_map/ppermute | solution.py:532
  10.4 25.5 %all-to-all-start = ((f32[32,48,128]{2,1,0:T(8,128)}), f32[32,48,128]{2,1,0:T(8,128)S(1)}, u32[]{:S(2)}, u32[]{:S(2)}) async-start(f32[32,48,128]{2,1,0:T(8,128)} %shard_map.162), calls=%async_computation | async-start | bytes 1572864 | tf_op jit(solution)/shard_map/all_to_all | solution.py:528
  52.5 16.0 %collective-permute-start.1 = (f32[1280,128]{1,0:T(8,128)S(1)}, f32[1280,128]{1,0:T(8,128)S(1)}, u32[]{:S(2)}, u32[]{:S(2)}) collective-permute-start(f32[1280,128]{1,0:T(8,128)S(1)} %get-tuple-element.61), channel_id=1, source_target_pairs={{0,2},{2,0},{1,3},{3,1},{4,6},{6,4},{5,7},{7,5},{8,10},{10,8},{9,1... | collective-permute-start | bytes 1966088 | tf_op jit(solution)/shard_map/ppermute | solution.py:532
  73.4 3.5 %collective-permute-start.2 = (f32[32,2,48,128]{3,2,1,0:T(8,128)S(1)}, f32[32,2,48,128]{3,2,1,0:T(8,128)S(1)}, u32[]{:S(2)}, u32[]{:S(2)}) collective-permute-start(f32[32,2,48,128]{3,2,1,0:T(8,128)S(1)} %get-tuple-element.78), channel_id=1, source_target_pairs={{0,2},{2,0},{1,3},{3,1},{4,6},{6,4},{5,7},{7,5},{8,10},{10,8},{9,1... | collective-permute-start | bytes 4718600 | tf_op jit(solution)/shard_map/ppermute | solution.py:532
  122.5 9.8 %collective-permute-start.3 = (f32[32,48,128]{2,1,0:T(8,128)S(1)}, f32[32,48,128]{2,1,0:T(8,128)S(1)}, u32[]{:S(2)}, u32[]{:S(2)}) collective-permute-start(f32[32,48,128]{2,1,0:T(8,128)S(1)} %all_to_all.22.mine_ref), channel_id=1, source_target_pairs={{0,2},{2,0},{1,3},{3,1},{4,6},{6,4},{5,7},{7,5},{8,10},{10,8},{9,1... | collective-permute-start | bytes 2359304 | tf_op jit(solution)/shard_map/ppermute | solution.py:532
